TPU v7x, 512 devices: a whole 4x8x8 slice. The times are simulated.
512 devices in a mesh: bx: 16 (over y_hi, z), by: 32 (over x, y_lo, core).
Axes of the slice: x: 4, y: 8 (y_hi: 2, y_lo: 4; y = y_hi * 4 + y_lo), z: 8, core: 2. Of those that a mesh axis runs over, the one named last changes fastest.
Arguments:
- incident: float32 [2, 96, 16, 32, 128], P(None, None, 'bx', 'by'), may hold values from -6 to 6
- mie: float32 [2, 12, 16, 32, 128], P(None, None, 'bx', 'by'), may hold values from -1 to 1
- offsets: float32 [3, 16, 32, 128], P(None, 'bx', 'by'), may hold values from -1 to 1
- sphere_box: int32 [16, 32, 128], P('bx', 'by'), may hold values from 0 to 15
- near_table: bfloat16 [16, 2, 96, 96], replicated, may hold values from -0.078125 to 0.078125
- near_src: int32 [16, 32, 16, 256], P('bx', 'by'), may hold values from 0 to 1151
- near_dst: int32 [16, 32, 16, 256], P('bx', 'by'), may hold values from 0 to 127
- pattern: bfloat16 [2, 128, 96], replicated, may hold values from -0.84 to 0.84
- receive: bfloat16 [2, 96, 128], replicated, may hold values from -0.375 to 0.375
- leaf_transfer: float32 [32, 2, 128], replicated, may hold values from -0.15 to 0.15
- far_src: int32 [16, 32, 16, 24], P('bx', 'by'), may hold values from 0 to 143
- far_cls: int32 [16, 32, 16, 24], P('bx', 'by'), may hold values from 0 to 31
- coarse_transfer: float32 [2, 31, 63, 128], replicated, may hold values from -0.012 to 0.012
Outputs:
- solution: float32 [2, 96, 16, 32, 128], P(None, None, 'bx', 'by')
- residual: float32 [2, 96, 16, 32, 128], P(None, None, 'bx', 'by')
All inputs are finite; a program needn't handle non-finite values.
Results may differ from a plain program's by a relative error of at most 0.0095.
Values may be sent and summed in bfloat16 or wider, within the bound.
No kernel may reach another device: no remote copies, remote signals or barrier semaphores. Data moves between devices by JAX's collectives and lax.ppermute only.
A program may use at most 64 MiB of HBM per device.

v0:
```python
import functools
import math

import jax
import jax.numpy as jnp
import numpy as np
from jax import lax
from jax.sharding import Mesh
from jax.sharding import PartitionSpec as P

ITERS = 2
BX = ("bx_0", "bx_1")
BY = ("by_0", "by_1", "by_2")
BX_BY = ("bx_0", "bx_1", "by_0", "by_1", "by_2")


HIGHEST = lax.Precision.HIGHEST
KAPPA = 1.5
GOLDEN = 2.399963229728653


def extended(x, sides, width):
    for axis, dim in sides:
        devices, length = (lax.axis_size(axis), x.shape[dim])
        up = [(i, (i + 1) % devices) for i in range(devices - 1)]
        down = [(j, i) for i, j in up]
        last = lax.slice_in_dim(x, length - width, length, axis=dim)
        first = lax.slice_in_dim(x, 0, width, axis=dim)
        before = lax.ppermute(last, axis, up)
        after = lax.ppermute(first, axis, down)
        x = jnp.concatenate([before, x, after], axis=dim)
    return x


def laid_out(tiles, dim):
    shape = list(tiles.shape[1:])
    shape[dim] *= tiles.shape[0]
    return jnp.moveaxis(tiles, 0, dim).reshape(shape)


def from_everyone(x, axis):
    copies = jnp.broadcast_to(x, (lax.axis_size(axis), *x.shape))
    return lax.all_to_all(copies, axis, split_axis=0, concat_axis=0, tiled=True)


def collect(x, axis, dim):
    return laid_out(from_everyone(x, axis), dim)


def one_axis_at_a_time(x, axes):
    return functools.reduce(lax.psum, axes, x)


def int_starts(values):
    return tuple((jnp.asarray(value).astype(jnp.int32) for value in values))


def directions(number):
    ordinal = jnp.arange(number).astype(jnp.float32)
    height = 1.0 - (2.0 * ordinal + 1.0) / number
    radius = jnp.sqrt(1.0 - height * height)
    return jnp.stack(
        [radius * jnp.cos(GOLDEN * ordinal), radius * jnp.sin(GOLDEN * ordinal), height]
    )


def leaf_centers(number):
    ordinal = jnp.arange(number, dtype=jnp.int32)
    first_c = 2.0 * (ordinal % 2).astype(jnp.float32) - 1.0
    second_c = 2.0 * (ordinal // 2 % 2).astype(jnp.float32) - 1.0
    third_c = 2.0 * (ordinal // 4).astype(jnp.float32) - (number // 4 - 1)
    return jnp.stack([first_c, second_c, third_c])


def mie_spread(coef_count, mie_count):
    half_count = coef_count // 2
    table = np.zeros((coef_count, mie_count), np.float32)
    for number in range(coef_count):
        within = number % half_count
        degree = math.isqrt(within + 1)
        table[number, number // half_count * (mie_count // 2) + degree - 1] = 1.0
    return table


def complex_block(matrix):
    real_part = matrix[..., 0, :, :]
    imag_part = matrix[..., 1, :, :]
    upper = jnp.concatenate([real_part, -imag_part], axis=-1)
    bottom = jnp.concatenate([imag_part, real_part], axis=-1)
    return jnp.concatenate([upper, bottom], axis=-2)


def rotate(real_part, imag_part, cosines, sine_vals):
    return (
        real_part * cosines - imag_part * sine_vals,
        real_part * sine_vals + imag_part * cosines,
    )


def far_mask(first_pos, second_pos, across_x, across_y):
    ordinal = jnp.arange(across_x * across_y, dtype=jnp.int32)
    apart_x = jnp.abs(ordinal // across_y - first_pos)
    apart_y = jnp.abs(ordinal % across_y - second_pos)
    return ((apart_x >= 2) | (apart_y >= 2)).astype(jnp.float32)


def small_solve(normal, rhs_vec, size_count):
    lower_tri = jnp.linalg.cholesky(normal)
    middle = []
    for row_num in range(size_count):
        accum = rhs_vec[row_num]
        for col_num in range(row_num):
            accum = accum - lower_tri[row_num, col_num] * middle[col_num]
        middle.append(accum / lower_tri[row_num, row_num])
    weights = [None] * size_count
    for row_num in reversed(range(size_count)):
        accum = middle[row_num]
        for col_num in range(row_num + 1, size_count):
            accum = accum - lower_tri[col_num, row_num] * weights[col_num]
        weights[row_num] = accum / lower_tri[row_num, row_num]
    return weights


def local(
    incident,
    mie,
    offsets,
    sphere_box,
    near_table,
    near_src,
    near_dst,
    pattern,
    receive,
    leaf_transfer,
    far_src,
    far_cls,
    coarse_transfer,
):
    coef_rows = incident.shape[1]
    spheres = incident.shape[4]
    block_rows = 2 * coef_rows
    plane_dirs = pattern.shape[1]
    leaf_boxes = far_src.shape[2]
    list_length = far_src.shape[3]
    leaf_classes = leaf_transfer.shape[0]
    class_count = near_src.shape[2]
    pair_count = near_src.shape[3]
    across_x = lax.axis_size(BX)
    across_y = lax.axis_size(BY)
    first_pos = lax.axis_index(BX)
    second_pos = lax.axis_index(BY)
    blocks = complex_block(near_table)
    send_block = complex_block(pattern)
    take_block = complex_block(receive)
    planes = directions(plane_dirs)
    phases = KAPPA * jnp.dot(planes.T, offsets.reshape(3, spheres), precision=HIGHEST)
    cos_sphere, sin_sphere = (jnp.cos(phases), jnp.sin(phases))
    centre = KAPPA * jnp.dot(planes.T, leaf_centers(leaf_boxes), precision=HIGHEST)
    cos_leaf, sin_leaf = (jnp.cos(centre), jnp.sin(centre))
    member = (
        jnp.arange(leaf_boxes, dtype=jnp.int32)[:, None] == sphere_box.reshape(1, spheres)
    ).astype(jnp.float32)
    class_hot = (
        jnp.arange(leaf_classes, dtype=jnp.int32)[:, None] == far_cls.reshape(1, -1)
    ).astype(jnp.float32)
    chosen = jnp.dot(
        leaf_transfer.reshape(leaf_classes, 2 * plane_dirs).T, class_hot, precision=HIGHEST
    ).reshape(2, plane_dirs, leaf_boxes * list_length)
    mie_full = jnp.einsum(
        "nk,rks->rns",
        jnp.asarray(mie_spread(coef_rows, mie.shape[1])),
        mie.reshape(2, mie.shape[1], spheres),
        precision=HIGHEST,
    )
    coarse_window = lax.dynamic_slice(
        coarse_transfer,
        int_starts((0, across_x - 1 - first_pos, across_y - 1 - second_pos, 0)),
        (2, across_x, across_y, plane_dirs),
    ).reshape(2, across_x * across_y, plane_dirs)
    coarse_window = coarse_window.transpose(0, 2, 1) * far_mask(
        first_pos, second_pos, across_x, across_y
    )
    sources_flat = near_src.reshape(-1)
    targets_flat = near_dst.reshape(-1)
    leaf_sources = far_src.reshape(-1)
    beta_norm = jnp.sqrt(one_axis_at_a_time(jnp.sum(incident * incident), BX_BY))
    basis_list = [incident / beta_norm]
    hess_mat = jnp.zeros((ITERS + 1, ITERS), jnp.float32)
    for col_num in range(ITERS):
        vector = basis_list[col_num]
        rounded = vector.astype(jnp.bfloat16)
        along_rows = extended(rounded, ((BY, 3),), 1)
        beside_all = extended(along_rows, ((BX, 2),), 1)
        signature = jnp.dot(
            send_block, rounded.reshape(block_rows, spheres), preferred_element_type=jnp.float32
        )
        out_real, out_imag = rotate(
            signature[:plane_dirs], signature[plane_dirs:], cos_sphere, -sin_sphere
        )
        leaf_out = jnp.dot(jnp.concatenate([out_real, out_imag]), member.T, precision=HIGHEST)
        leaf_around = extended(
            leaf_out.reshape(2, plane_dirs, 1, 1, leaf_boxes), ((BX, 2), (BY, 3)), 1
        )
        leaf_around = leaf_around.reshape(2, plane_dirs, 9 * leaf_boxes)
        up_real, up_imag = rotate(leaf_out[:plane_dirs], leaf_out[plane_dirs:], cos_leaf, -sin_leaf)
        column_out = jnp.stack([up_real.sum(axis=1), up_imag.sum(axis=1)])[:, :, None]
        empty = jnp.zeros((2, plane_dirs), jnp.float32)
        row_outs = collect(column_out, BY, 2)
        piece = collect(row_outs.astype(jnp.bfloat16), BX, 2).astype(row_outs.dtype)
        prod_real, prod_imag = rotate(piece[0], piece[1], coarse_window[0], coarse_window[1])
        column_in = empty + jnp.stack([prod_real.sum(axis=1), prod_imag.sum(axis=1)])
        columns = beside_all.reshape(block_rows, 9 * spheres)
        picked = jnp.take(columns, sources_flat, axis=1).reshape(
            block_rows, class_count, pair_count
        )
        contrib = jnp.einsum("kab,bkm->akm", blocks, picked, preferred_element_type=jnp.float32)
        near = (
            jnp.zeros((block_rows, spheres), jnp.float32)
            .at[:, targets_flat]
            .add(contrib.reshape(block_rows, class_count * pair_count))
        )
        leaf_picked = jnp.take(leaf_around, leaf_sources, axis=2)
        apply_prod_real, apply_prod_imag = rotate(
            leaf_picked[0], leaf_picked[1], chosen[0], chosen[1]
        )
        leaf_in = (
            jnp.stack([apply_prod_real, apply_prod_imag])
            .reshape(2, plane_dirs, leaf_boxes, list_length)
            .sum(axis=3)
        )
        down_real, down_imag = rotate(
            column_in[0][:, None], column_in[1][:, None], cos_leaf, sin_leaf
        )
        incoming = leaf_in + jnp.stack([down_real, down_imag])
        spread = jnp.dot(incoming.reshape(2 * plane_dirs, leaf_boxes), member, precision=HIGHEST)
        in_real, in_imag = rotate(spread[:plane_dirs], spread[plane_dirs:], cos_sphere, sin_sphere)
        arriving = jnp.concatenate([in_real, in_imag]).astype(jnp.bfloat16)
        far = jnp.dot(take_block, arriving, preferred_element_type=jnp.float32)
        field_sum = near + far
        source = vector.reshape(2, coef_rows, spheres)
        mixed_real, mixed_imag = rotate(
            field_sum[:coef_rows], field_sum[coef_rows:], mie_full[0], mie_full[1]
        )
        krylov_vec = jnp.stack([source[0] - mixed_real, source[1] - mixed_imag]).reshape(
            vector.shape
        )
        local_sums = jnp.stack(
            [jnp.sum(krylov_vec * basis_item) for basis_item in basis_list]
            + [jnp.sum(krylov_vec * krylov_vec)]
        )
        totals = one_axis_at_a_time(local_sums, BX_BY)
        squares = totals[col_num + 1]
        for row_num in range(col_num + 1):
            krylov_vec = krylov_vec - totals[row_num] * basis_list[row_num]
            hess_mat = hess_mat.at[row_num, col_num].set(totals[row_num])
            squares = squares - totals[row_num] * totals[row_num]
        length = jnp.sqrt(squares)
        hess_mat = hess_mat.at[col_num + 1, col_num].set(length)
        basis_list.append(krylov_vec / length)
    normal = jnp.dot(hess_mat.T, hess_mat, precision=HIGHEST)
    weights = small_solve(normal, beta_norm * hess_mat[0], ITERS)
    solution = jnp.zeros_like(incident)
    for col_num in range(ITERS):
        solution = solution + weights[col_num] * basis_list[col_num]
    fitted = jnp.dot(hess_mat, jnp.stack(weights), precision=HIGHEST)
    residual = beta_norm * basis_list[0]
    for row_num in range(ITERS + 1):
        residual = residual - fitted[row_num] * basis_list[row_num]
    return (solution, residual)


def solution(mesh):
    torus = Mesh(mesh.devices.reshape(2, 8, 4, 4, 2), ("bx_0", "bx_1", "by_0", "by_1", "by_2"))
    placed = (
        P(None, None, BX, BY, None),
        P(None, None, BX, BY, None),
        P(None, BX, BY, None),
        P(BX, BY, None),
        P(),
        P(BX, BY, None, None),
        P(BX, BY, None, None),
        P(),
        P(),
        P(),
        P(BX, BY, None, None),
        P(BX, BY, None, None),
        P(),
    )
    return jax.shard_map(
        local,
        mesh=torus,
        in_specs=placed,
        out_specs=(P(None, None, BX, BY, None), P(None, None, BX, BY, None)),
        check_vma=False,
    )
```

profile of v0, /device:TPU:1, one launch (start us, length us, event | category | flops | bytes accessed | tf_op | source)
XLA Modules:
  0.0 449.7 jit_solution(15805214438632430831)
XLA Ops:
  2.5 9.3 %psum.105 = f32[]{:T(128)} all-reduce(f32[]{:T(128)} %multiply_reduce_fusion.3), channel_id=1, replica_groups=mesh['bx_0'=2,'bx_1'=8,'by_0'=4,'by_1'=4,'by_2'=2] {'bx_0'}, use_global_device_ids=true, to_apply=%region_1.2 | all-reduce | flops 1 | bytes 8 | tf_op jit(solution)/shard_map/psum | solution.py:51
  11.8 20.0 %psum.106 = f32[]{:T(128)} all-reduce(f32[]{:T(128)} %psum.105), channel_id=1, replica_groups=mesh['bx_0'=2,'bx_1'=8,'by_0'=4,'by_1'=4,'by_2'=2] {'bx_1'}, use_global_device_ids=true, to_apply=%region_2.3 | all-reduce | flops 1 | bytes 8 | tf_op jit(solution)/shard_map/psum | solution.py:51
  33.4 9.1 %psum.107 = f32[]{:T(128)} all-reduce(f32[]{:T(128)} %psum.106), channel_id=1, replica_groups=mesh['bx_0'=2,'bx_1'=8,'by_0'=4,'by_1'=4,'by_2'=2] {'by_0'}, use_global_device_ids=true, to_apply=%region_3.4 | all-reduce | flops 1 | bytes 8 | tf_op jit(solution)/shard_map/psum | solution.py:51
  42.5 10.5 %psum.108 = f32[]{:T(128)} all-reduce(f32[]{:T(128)} %psum.107), channel_id=1, replica_groups=mesh['bx_0'=2,'bx_1'=8,'by_0'=4,'by_1'=4,'by_2'=2] {'by_1'}, use_global_device_ids=true, to_apply=%region_4.5 | all-reduce | flops 1 | bytes 8 | tf_op jit(solution)/shard_map/psum | solution.py:51
  53.0 12.3 %psum.109 = f32[]{:T(128)} all-reduce(f32[]{:T(128)} %psum.108), channel_id=1, replica_groups=mesh['bx_0'=2,'bx_1'=8,'by_0'=4,'by_1'=4,'by_2'=2] {'by_2'}, use_global_device_ids=true, to_apply=%region_5.6 | all-reduce | flops 1 | bytes 8 | tf_op jit(solution)/shard_map/psum | solution.py:51
  77.0 3.0 collective-permute-start.5
  81.0 6.0 %all-to-all-start = ((bf16[32,2,128,1]{2,1,3,0:T(2,128)(2,1)}), bf16[32,2,128,1]{2,1,3,0:T(2,128)(2,1)}, u32[]{:S(2)}, u32[]{:S(2)}) async-start(bf16[32,2,128,1]{2,1,3,0:T(2,128)(2,1)} %broadcast_in_dim.37), calls=%async_computation | async-start | bytes 32768 | tf_op jit(solution)/shard_map/all_to_all | solution.py:43
  99.3 3.5 collective-permute-start.2
  106.2 13.0 %all-to-all-start.1 = ((bf16[16,2,128,32]{2,3,1,0:T(8,128)(2,1)}), bf16[16,2,128,32]{2,3,1,0:T(8,128)(2,1)}, u32[]{:S(2)}, u32[]{:S(2)}) async-start(bf16[16,2,128,32]{2,3,1,0:T(8,128)(2,1)} %broadcast_in_dim.38), calls=%async_computation.1 | async-start | bytes 524288 | tf_op jit(solution)/shard_map/all_to_all | solution.py:43
  120.8 3.9 collective-permute-start.6
  137.3 17.0 %gather_fusion.1 = bf16[4096,192]{1,0:T(8,128)(2,1)} fusion(bf16[192,1152]{0,1:T(8,128)(2,1)S(1)} %reshape.699, s32[4096]{0:T(1024)S(1)} %fusion.38), kind=kCustom, calls=%fused_computation.1.clone | custom fusion | bytes 3162112 | tf_op jit(solution)/shard_map/jit(_take)/gather | solution.py:213
  159.2 5.1 %copy.107 = f32[4096,192]{1,0:T(8,128)} copy(f32[4096,192]{0,1:T(8,128)} %bitcast.269) | data formatting | bytes 6291456 | tf_op jit(solution)/shard_map/reshape | solution.py:220
  166.3 23.0 %scatter_fusion = f32[192,128]{0,1:T(8,128)S(1)} fusion(f32[192,128]{0,1:T(8,128)S(1)} %fusion.12, s32[4096]{0:T(1024)S(1)} %bitcast.303, f32[4096,192]{1,0:T(8,128)} %copy.107), kind=kCustom, calls=%fused_computation.4 | custom fusion | flops 786432 | bytes 9453568 | tf_op jit(solution)/shard_map/scatter-add | solution.py:220
  196.6 10.7 %psum.110 = f32[2]{0:T(128)S(1)} all-reduce(f32[2]{0:T(128)S(1)} %pad_maximum_fusion.11), channel_id=1, replica_groups=mesh['bx_0'=2,'bx_1'=8,'by_0'=4,'by_1'=4,'by_2'=2] {'bx_0'}, use_global_device_ids=true, to_apply=%region_14.17 | all-reduce | flops 2 | bytes 16 | tf_op jit(solution)/shard_map/psum | solution.py:51
  207.3 18.9 %psum.111 = f32[2]{0:T(128)S(1)} all-reduce(f32[2]{0:T(128)S(1)} %psum.110), channel_id=1, replica_groups=mesh['bx_0'=2,'bx_1'=8,'by_0'=4,'by_1'=4,'by_2'=2] {'bx_1'}, use_global_device_ids=true, to_apply=%region_15.18 | all-reduce | flops 2 | bytes 16 | tf_op jit(solution)/shard_map/psum | solution.py:51
  226.2 7.6 %psum.112 = f32[2]{0:T(128)S(1)} all-reduce(f32[2]{0:T(128)S(1)} %psum.111), channel_id=1, replica_groups=mesh['bx_0'=2,'bx_1'=8,'by_0'=4,'by_1'=4,'by_2'=2] {'by_0'}, use_global_device_ids=true, to_apply=%region_16.19 | all-reduce | flops 2 | bytes 16 | tf_op jit(solution)/shard_map/psum | solution.py:51
  233.8 10.1 %psum.113 = f32[2]{0:T(128)S(1)} all-reduce(f32[2]{0:T(128)S(1)} %psum.112), channel_id=1, replica_groups=mesh['bx_0'=2,'bx_1'=8,'by_0'=4,'by_1'=4,'by_2'=2] {'by_1'}, use_global_device_ids=true, to_apply=%region_17.20 | all-reduce | flops 2 | bytes 16 | tf_op jit(solution)/shard_map/psum | solution.py:51
  243.9 14.0 %psum.114 = f32[2]{0:T(128)S(1)} all-reduce(f32[2]{0:T(128)S(1)} %psum.113), channel_id=1, replica_groups=mesh['bx_0'=2,'bx_1'=8,'by_0'=4,'by_1'=4,'by_2'=2] {'by_2'}, use_global_device_ids=true, to_apply=%region_18.21 | all-reduce | flops 2 | bytes 16 | tf_op jit(solution)/shard_map/psum | solution.py:51
  272.0 6.6 %all-to-all-start.2 = ((bf16[32,2,128,1]{2,1,3,0:T(2,128)(2,1)}), bf16[32,2,128,1]{2,1,3,0:T(2,128)(2,1)S(1)}, u32[]{:S(2)}, u32[]{:S(2)}) async-start(bf16[32,2,128,1]{2,1,3,0:T(2,128)(2,1)} %broadcast_in_dim.39), calls=%async_computation.2 | async-start | bytes 32768 | tf_op jit(solution)/shard_map/all_to_all | solution.py:43
  278.6 3.5 collective-permute-start.10
  286.6 10.4 %all-to-all-start.3 = ((bf16[16,2,128,32]{2,3,1,0:T(8,128)(2,1)}), bf16[16,2,128,32]{2,3,1,0:T(8,128)(2,1)}, u32[]{:S(2)}, u32[]{:S(2)}) async-start(bf16[16,2,128,32]{2,3,1,0:T(8,128)(2,1)} %broadcast_in_dim.40), calls=%async_computation.3 | async-start | bytes 524288 | tf_op jit(solution)/shard_map/all_to_all | solution.py:43
  297.7 3.9 collective-permute-start.14
  306.3 4.8 %collective-permute-done.15 = bf16[2,96,1,3,128]{4,1,0,3,2:T(8,128)(2,1)} collective-permute-done((bf16[2,96,1,3,128]{4,1,0,3,2:T(8,128)(2,1)}, bf16[2,96,1,3,128]{4,1,0,3,2:T(8,128)(2,1)}, u32[]{:S(2)}, u32[]{:S(2)}) %collective-permute-start.15) | collective-permute-done | bytes 147488 | tf_op jit(solution)/shard_map/ppermute | solution.py:30
  315.8 17.0 %gather_fusion.3 = bf16[4096,192]{1,0:T(8,128)(2,1)} fusion(bf16[192,1152]{0,1:T(8,128)(2,1)S(1)} %reshape.700, s32[4096]{0:T(1024)S(1)} %fusion.38), kind=kCustom, calls=%fused_computation.3.clone | custom fusion | bytes 3162112 | tf_op jit(solution)/shard_map/jit(_take)/gather | solution.py:213
  337.7 5.1 %copy.121 = f32[4096,192]{1,0:T(8,128)} copy(f32[4096,192]{0,1:T(8,128)} %bitcast.270) | data formatting | bytes 6291456 | tf_op jit(solution)/shard_map/reshape | solution.py:220
  344.8 23.0 %scatter_fusion.1 = f32[192,128]{0,1:T(8,128)S(1)} fusion(f32[192,128]{0,1:T(8,128)S(1)} %fusion.16, s32[4096]{0:T(1024)S(1)} %bitcast.304, f32[4096,192]{1,0:T(8,128)} %copy.121), kind=kCustom, calls=%fused_computation.5 | custom fusion | flops 786432 | bytes 9453568 | tf_op jit(solution)/shard_map/scatter-add | solution.py:220
  371.5 8.7 %psum.115 = f32[3]{0:T(128)S(1)} all-reduce(f32[3]{0:T(128)S(1)} %pad_maximum_fusion.12), channel_id=1, replica_groups=mesh['bx_0'=2,'bx_1'=8,'by_0'=4,'by_1'=4,'by_2'=2] {'bx_0'}, use_global_device_ids=true, to_apply=%region_28.31 | all-reduce | flops 3 | bytes 24 | tf_op jit(solution)/shard_map/psum | solution.py:51
  380.2 18.1 %psum.116 = f32[3]{0:T(128)S(1)} all-reduce(f32[3]{0:T(128)S(1)} %psum.115), channel_id=1, replica_groups=mesh['bx_0'=2,'bx_1'=8,'by_0'=4,'by_1'=4,'by_2'=2] {'bx_1'}, use_global_device_ids=true, to_apply=%region_29.32 | all-reduce | flops 3 | bytes 24 | tf_op jit(solution)/shard_map/psum | solution.py:51
  398.8 7.1 %psum.117 = f32[3]{0:T(128)S(1)} all-reduce(f32[3]{0:T(128)S(1)} %psum.116), channel_id=1, replica_groups=mesh['bx_0'=2,'bx_1'=8,'by_0'=4,'by_1'=4,'by_2'=2] {'by_0'}, use_global_device_ids=true, to_apply=%region_30.33 | all-reduce | flops 3 | bytes 24 | tf_op jit(solution)/shard_map/psum | solution.py:51
  406.6 10.1 %psum.118 = f32[3]{0:T(128)S(1)} all-reduce(f32[3]{0:T(128)S(1)} %psum.117), channel_id=1, replica_groups=mesh['bx_0'=2,'bx_1'=8,'by_0'=4,'by_1'=4,'by_2'=2] {'by_1'}, use_global_device_ids=true, to_apply=%region_31.34 | all-reduce | flops 3 | bytes 24 | tf_op jit(solution)/shard_map/psum | solution.py:51
  416.7 13.8 %psum.119 = f32[3]{0:T(128)S(1)} all-reduce(f32[3]{0:T(128)S(1)} %psum.118), channel_id=1, replica_groups=mesh['bx_0'=2,'bx_1'=8,'by_0'=4,'by_1'=4,'by_2'=2] {'by_2'}, use_global_device_ids=true, to_apply=%region_32.35 | all-reduce | flops 3 | bytes 24 | tf_op jit(solution)/shard_map/psum | solution.py:51
  446.0 3.7 multiply_subtract_fusion.2
  (251 shorter events, 104.4 us)
Async XLA Ops:
  0.6 93.7 %copy-start = (f32[2,31,63,128]{3,0,2,1:T(2,128)S(1)}, f32[2,31,63,128]{3,0,2,1:T(2,128)}, u32[]{:S(2)}) copy-start(f32[2,31,63,128]{3,0,2,1:T(2,128)} %param.40) | copy-start | bytes 5999620
  0.6 91.8 %copy-start.3 = (bf16[16,2,96,96]{3,2,1,0:T(8,128)(2,1)S(1)}, bf16[16,2,96,96]{3,2,1,0:T(8,128)(2,1)}, u32[]{:S(2)}) copy-start(bf16[16,2,96,96]{3,2,1,0:T(8,128)(2,1)} %param.32) | copy-start | bytes 1769476
  32.6 61.7 %copy-start.36 = (bf16[128,96]{0,1:T(8,128)(2,1)}, bf16[128,96]{0,1:T(8,128)(2,1)S(1)}, u32[]{:S(2)}) copy-start(bf16[128,96]{0,1:T(8,128)(2,1)S(1)} %get-tuple-element.118) | copy-start | bytes 73732
  32.6 61.7 %copy-start.37 = (bf16[128,96]{0,1:T(8,128)(2,1)}, bf16[128,96]{0,1:T(8,128)(2,1)S(1)}, u32[]{:S(2)}) copy-start(bf16[128,96]{0,1:T(8,128)(2,1)S(1)} %get-tuple-element.119) | copy-start | bytes 73732
  33.4 37.1 %copy-start.31 = (bf16[128,96]{0,1:T(8,128)(2,1)}, bf16[128,96]{0,1:T(8,128)(2,1)S(1)}, u32[]{:S(2)}) copy-start(bf16[128,96]{0,1:T(8,128)(2,1)S(1)} %fusion.91) | copy-start | bytes 73732
  71.9 25.2 %collective-permute-start = (f32[2,128,1,1,16]{1,0,4,3,2:T(2,128)}, f32[2,128,1,1,16]{1,0,4,3,2:T(2,128)}, u32[]{:S(2)}, u32[]{:S(2)}) collective-permute-start(f32[2,128,1,1,16]{1,0,4,3,2:T(2,128)} %reshape.609), channel_id=1, source_target_pairs={{0,32},{32,64},{64,96},{96,128},{128,160},{160,192},{192,224},{224... | collective-permute-start | bytes 49160 | tf_op jit(solution)/shard_map/ppermute | solution.py:29
  73.8 24.7 %collective-permute-start.1 = (f32[2,128,1,1,16]{1,0,4,3,2:T(2,128)}, f32[2,128,1,1,16]{1,0,4,3,2:T(2,128)}, u32[]{:S(2)}, u32[]{:S(2)}) collective-permute-start(f32[2,128,1,1,16]{1,0,4,3,2:T(2,128)} %reshape.609), channel_id=1, source_target_pairs={{32,0},{64,32},{96,64},{128,96},{160,128},{192,160},{224,192},{256... | collective-permute-start | bytes 49160 | tf_op jit(solution)/shard_map/ppermute | solution.py:30
  75.1 44.1 %collective-permute-start.4 = (bf16[2,96,1,1,128]{4,1,0,3,2:T(8,128)(2,1)}, bf16[2,96,1,1,128]{4,1,0,3,2:T(8,128)(2,1)}, u32[]{:S(2)}, u32[]{:S(2)}) collective-permute-start(bf16[2,96,1,1,128]{4,1,0,3,2:T(8,128)(2,1)} %get-tuple-element.112), channel_id=1, source_target_pairs={{0,1},{1,2},{2,3},{3,4},{4,5},{5,6},{6,7},{7,8},{8,9},{9,10},{10,1... | collective-permute-start | bytes 147464 | tf_op jit(solution)/shard_map/ppermute | solution.py:29
  77.0 42.2 %collective-permute-start.5 = (bf16[2,96,1,1,128]{4,1,0,3,2:T(8,128)(2,1)}, bf16[2,96,1,1,128]{4,1,0,3,2:T(8,128)(2,1)}, u32[]{:S(2)}, u32[]{:S(2)}) collective-permute-start(bf16[2,96,1,1,128]{4,1,0,3,2:T(8,128)(2,1)} %get-tuple-element.112), channel_id=1, source_target_pairs={{1,0},{2,1},{3,2},{4,3},{5,4},{6,5},{7,6},{8,7},{9,8},{10,9},{11,1... | collective-permute-start | bytes 147464 | tf_op jit(solution)/shard_map/ppermute | solution.py:30
  81.0 23.8 %all-to-all-start = ((bf16[32,2,128,1]{2,1,3,0:T(2,128)(2,1)}), bf16[32,2,128,1]{2,1,3,0:T(2,128)(2,1)}, u32[]{:S(2)}, u32[]{:S(2)}) async-start(bf16[32,2,128,1]{2,1,3,0:T(2,128)(2,1)} %broadcast_in_dim.37), calls=%async_computation | async-start | bytes 32768 | tf_op jit(solution)/shard_map/all_to_all | solution.py:43
  94.5 33.6 %copy-start.45 = (pred[384]{0:T(512)(128)(4,1)S(1)}, pred[384]{0:T(512)(128)(4,1)}, u32[]{:S(2)}) copy-start(pred[384]{0:T(512)(128)(4,1)} %compare_and_fusion.1) | copy-start | bytes 1156
  97.1 31.2 %copy-start.38 = (s32[1024]{0:T(1024)}, s32[1024]{0:T(1024)S(1)}, u32[]{:S(2)}) copy-start(s32[1024]{0:T(1024)S(1)} %pad_clamp_fusion) | copy-start | bytes 12292
  99.3 26.7 %collective-permute-start.2 = (f32[2,128,3,1,16]{1,0,4,3,2:T(2,128)S(1)}, f32[2,128,3,1,16]{1,0,4,3,2:T(2,128)S(1)}, u32[]{:S(2)}, u32[]{:S(2)}) collective-permute-start(f32[2,128,3,1,16]{1,0,4,3,2:T(2,128)S(1)} %constant_dynamic-update-slice_fusion), channel_id=1, source_target_pairs={{0,1},{1,2},{2,3},{3,4},{4,5},{5,6},{6,7},{7,8},{8,9},{9,10},{10,1... | collective-permute-start | bytes 147464 | tf_op jit(solution)/shard_map/ppermute | solution.py:29
  102.8 23.1 %collective-permute-start.3 = (f32[2,128,3,1,16]{1,0,4,3,2:T(2,128)S(1)}, f32[2,128,3,1,16]{1,0,4,3,2:T(2,128)S(1)}, u32[]{:S(2)}, u32[]{:S(2)}) collective-permute-start(f32[2,128,3,1,16]{1,0,4,3,2:T(2,128)S(1)} %constant_dynamic-update-slice_fusion), channel_id=1, source_target_pairs={{1,0},{2,1},{3,2},{4,3},{5,4},{6,5},{7,6},{8,7},{9,8},{10,9},{11,1... | collective-permute-start | bytes 147464 | tf_op jit(solution)/shard_map/ppermute | solution.py:30
  106.2 58.1 %all-to-all-start.1 = ((bf16[16,2,128,32]{2,3,1,0:T(8,128)(2,1)}), bf16[16,2,128,32]{2,3,1,0:T(8,128)(2,1)}, u32[]{:S(2)}, u32[]{:S(2)}) async-start(bf16[16,2,128,32]{2,3,1,0:T(8,128)(2,1)} %broadcast_in_dim.38), calls=%async_computation.1 | async-start | bytes 524288 | tf_op jit(solution)/shard_map/all_to_all | solution.py:43
  120.8 9.4 %collective-permute-start.6 = (bf16[2,96,1,3,128]{4,1,0,3,2:T(8,128)(2,1)}, bf16[2,96,1,3,128]{4,1,0,3,2:T(8,128)(2,1)}, u32[]{:S(2)}, u32[]{:S(2)}) collective-permute-start(bf16[2,96,1,3,128]{4,1,0,3,2:T(8,128)(2,1)} %pad_maximum_fusion.3), channel_id=1, source_target_pairs={{0,32},{32,64},{64,96},{96,128},{128,160},{160,192},{192,224},{224... | collective-permute-start | bytes 442376 | tf_op jit(solution)/shard_map/ppermute | solution.py:29
  124.6 7.9 %collective-permute-start.7 = (bf16[2,96,1,3,128]{4,1,0,3,2:T(8,128)(2,1)}, bf16[2,96,1,3,128]{4,1,0,3,2:T(8,128)(2,1)}, u32[]{:S(2)}, u32[]{:S(2)}) collective-permute-start(bf16[2,96,1,3,128]{4,1,0,3,2:T(8,128)(2,1)} %pad_maximum_fusion.3), channel_id=1, source_target_pairs={{32,0},{64,32},{96,64},{128,96},{160,128},{192,160},{224,192},{256... | collective-permute-start | bytes 442376 | tf_op jit(solution)/shard_map/ppermute | solution.py:30
  166.3 26.8 %copy-start.11 = (f32[2,96,128]{2,1,0:T(8,128)S(1)}, f32[2,96,128]{2,1,0:T(8,128)}, u32[]{:S(2)}) copy-start(f32[2,96,128]{2,1,0:T(8,128)} %convolution_bitcast_fusion.3) | copy-start | bytes 294916
  166.3 26.8 %copy-start.19 = (f32[2,96,1,1,128]{4,1,3,2,0:T(8,128)S(1)}, f32[2,96,1,1,128]{4,1,3,2,0:T(8,128)}, u32[]{:S(2)}) copy-start(f32[2,96,1,1,128]{4,1,3,2,0:T(8,128)} %get-tuple-element.113) | copy-start | bytes 294916
  166.3 27.6 %copy-start.1 = (f32[2,96,1,1,128]{4,3,2,1,0:T(1,128)S(1)}, f32[2,96,1,1,128]{4,3,2,1,0:T(1,128)}, u32[]{:S(2)}) copy-start(f32[2,96,1,1,128]{4,3,2,1,0:T(1,128)} %param.28) | copy-start | bytes 294916
  261.8 35.2 %collective-permute-start.12 = (bf16[2,96,1,1,128]{4,1,0,3,2:T(8,128)(2,1)S(1)}, bf16[2,96,1,1,128]{4,1,0,3,2:T(8,128)(2,1)S(1)}, u32[]{:S(2)}, u32[]{:S(2)}) collective-permute-start(bf16[2,96,1,1,128]{4,1,0,3,2:T(8,128)(2,1)S(1)} %get-tuple-element.82), channel_id=1, source_target_pairs={{0,1},{1,2},{2,3},{3,4},{4,5},{5,6},{6,7},{7,8},{8,9},{9,10},{10,1... | collective-permute-start | bytes 147464 | tf_op jit(solution)/shard_map/ppermute | solution.py:29
  264.2 32.9 %collective-permute-start.13 = (bf16[2,96,1,1,128]{4,1,0,3,2:T(8,128)(2,1)S(1)}, bf16[2,96,1,1,128]{4,1,0,3,2:T(8,128)(2,1)S(1)}, u32[]{:S(2)}, u32[]{:S(2)}) collective-permute-start(bf16[2,96,1,1,128]{4,1,0,3,2:T(8,128)(2,1)S(1)} %get-tuple-element.82), channel_id=1, source_target_pairs={{1,0},{2,1},{3,2},{4,3},{5,4},{6,5},{7,6},{8,7},{9,8},{10,9},{11,1... | collective-permute-start | bytes 147464 | tf_op jit(solution)/shard_map/ppermute | solution.py:30
  268.8 9.8 %collective-permute-start.8 = (f32[2,128,1,1,16]{1,0,4,3,2:T(2,128)S(1)}, f32[2,128,1,1,16]{1,0,4,3,2:T(2,128)S(1)}, u32[]{:S(2)}, u32[]{:S(2)}) collective-permute-start(f32[2,128,1,1,16]{1,0,4,3,2:T(2,128)S(1)} %reshape.624), channel_id=1, source_target_pairs={{0,32},{32,64},{64,96},{96,128},{128,160},{160,192},{192,224},{224... | collective-permute-start | bytes 49160 | tf_op jit(solution)/shard_map/ppermute | solution.py:29
  270.1 8.5 %collective-permute-start.9 = (f32[2,128,1,1,16]{1,0,4,3,2:T(2,128)S(1)}, f32[2,128,1,1,16]{1,0,4,3,2:T(2,128)S(1)}, u32[]{:S(2)}, u32[]{:S(2)}) collective-permute-start(f32[2,128,1,1,16]{1,0,4,3,2:T(2,128)S(1)} %reshape.624), channel_id=1, source_target_pairs={{32,0},{64,32},{96,64},{128,96},{160,128},{192,160},{224,192},{256... | collective-permute-start | bytes 49160 | tf_op jit(solution)/shard_map/ppermute | solution.py:30
  272.0 13.8 %all-to-all-start.2 = ((bf16[32,2,128,1]{2,1,3,0:T(2,128)(2,1)}), bf16[32,2,128,1]{2,1,3,0:T(2,128)(2,1)S(1)}, u32[]{:S(2)}, u32[]{:S(2)}) async-start(bf16[32,2,128,1]{2,1,3,0:T(2,128)(2,1)} %broadcast_in_dim.39), calls=%async_computation.2 | async-start | bytes 32768 | tf_op jit(solution)/shard_map/all_to_all | solution.py:43
  278.6 24.2 %collective-permute-start.10 = (f32[2,128,3,1,16]{1,0,4,3,2:T(2,128)S(1)}, f32[2,128,3,1,16]{1,0,4,3,2:T(2,128)S(1)}, u32[]{:S(2)}, u32[]{:S(2)}) collective-permute-start(f32[2,128,3,1,16]{1,0,4,3,2:T(2,128)S(1)} %constant_dynamic-update-slice_fusion.3), channel_id=1, source_target_pairs={{0,1},{1,2},{2,3},{3,4},{4,5},{5,6},{6,7},{7,8},{8,9},{9,10},{10,1... | collective-permute-start | bytes 147464 | tf_op jit(solution)/shard_map/ppermute | solution.py:29
  282.2 20.7 %collective-permute-start.11 = (f32[2,128,3,1,16]{1,0,4,3,2:T(2,128)S(1)}, f32[2,128,3,1,16]{1,0,4,3,2:T(2,128)S(1)}, u32[]{:S(2)}, u32[]{:S(2)}) collective-permute-start(f32[2,128,3,1,16]{1,0,4,3,2:T(2,128)S(1)} %constant_dynamic-update-slice_fusion.3), channel_id=1, source_target_pairs={{1,0},{2,1},{3,2},{4,3},{5,4},{6,5},{7,6},{8,7},{9,8},{10,9},{11,1... | collective-permute-start | bytes 147464 | tf_op jit(solution)/shard_map/ppermute | solution.py:30
  286.6 56.3 %all-to-all-start.3 = ((bf16[16,2,128,32]{2,3,1,0:T(8,128)(2,1)}), bf16[16,2,128,32]{2,3,1,0:T(8,128)(2,1)}, u32[]{:S(2)}, u32[]{:S(2)}) async-start(bf16[16,2,128,32]{2,3,1,0:T(8,128)(2,1)} %broadcast_in_dim.40), calls=%async_computation.3 | async-start | bytes 524288 | tf_op jit(solution)/shard_map/all_to_all | solution.py:43
  297.7 8.6 %collective-permute-start.14 = (bf16[2,96,1,3,128]{4,1,0,3,2:T(8,128)(2,1)}, bf16[2,96,1,3,128]{4,1,0,3,2:T(8,128)(2,1)}, u32[]{:S(2)}, u32[]{:S(2)}) collective-permute-start(bf16[2,96,1,3,128]{4,1,0,3,2:T(8,128)(2,1)} %pad_maximum_fusion.5), channel_id=1, source_target_pairs={{0,32},{32,64},{64,96},{96,128},{128,160},{160,192},{192,224},{224... | collective-permute-start | bytes 442376 | tf_op jit(solution)/shard_map/ppermute | solution.py:29
  301.6 9.6 %collective-permute-start.15 = (bf16[2,96,1,3,128]{4,1,0,3,2:T(8,128)(2,1)}, bf16[2,96,1,3,128]{4,1,0,3,2:T(8,128)(2,1)}, u32[]{:S(2)}, u32[]{:S(2)}) collective-permute-start(bf16[2,96,1,3,128]{4,1,0,3,2:T(8,128)(2,1)} %pad_maximum_fusion.5), channel_id=1, source_target_pairs={{32,0},{64,32},{96,64},{128,96},{160,128},{192,160},{224,192},{256... | collective-permute-start | bytes 442376 | tf_op jit(solution)/shard_map/ppermute | solution.py:30
  344.8 23.3 %copy-start.10 = (f32[2,96,1,1,128]{4,1,0,3,2:T(8,128)S(1)}, f32[2,96,1,1,128]{4,1,0,3,2:T(8,128)}, u32[]{:S(2)}) copy-start(f32[2,96,1,1,128]{4,1,0,3,2:T(8,128)} %get-tuple-element.83) | copy-start | bytes 294916
  344.8 23.3 %copy-start.2 = (f32[2,96,1,1,128]{4,3,2,1,0:T(1,128)S(1)}, f32[2,96,1,1,128]{4,3,2,1,0:T(1,128)}, u32[]{:S(2)}) copy-start(f32[2,96,1,1,128]{4,3,2,1,0:T(1,128)} %param.28) | copy-start | bytes 294916
  (34 other events, 107.9 us)
where the time goes:
time: 453 us; the launch traced here: 450 us
  blocking collectives  180 us (40%)
  local copies, waits for them, and re-layouts  83.4 us (18%)
  other arithmetic  80.9 us (18%)
  starting transfers between devices  72.1 us (16%)
  between operations  12.7 us (3%)
  waiting for transfers between devices  10.4 us (2%)
  matrix products  10.1 us (2%)
    psum x15, blocking collectives, one_axis_at_a_time(): return functools.reduce(lax.psum, axes, x)  180 us
    scatter-add x2, other arithmetic, local(): near = jnp.zeros((block_rows, spheres), jnp.float32).at[:, targets_flat]....  45.9 us
    all_to_all x4, starting transfers between devices, from_everyone(): return lax.all_to_all(copies, axis, split_axis=0, concat_axis=0, tiled=True)  36 us
    gather x2, local copies, waits for them, and re-layouts, local(): jnp.take(columns, sources_flat, axis=1)  34 us
    ppermute x8, starting transfers between devices, extended(): before = lax.ppermute(last, axis, up)  22.2 us
    reshape x4, local copies, waits for them, and re-layouts, local(): contrib.reshape(block_rows, class_count * pair_count)  14.4 us
    ppermute x8, starting transfers between devices, extended(): after = lax.ppermute(first, axis, down)  13.9 us
  transfers between devices with their start and end apart: 20, of which 5 were waited for; matrix products, arithmetic and copies ran while one was open for 20% of the time, Pallas kernels for 0%

commit v1 on v0

v1 whole, which is shorter than its diff:
```python
import functools
import math

import jax
import jax.numpy as jnp
import numpy as np
from jax import lax
from jax.experimental import pallas as pl
from jax.experimental.pallas import tpu as pltpu
from jax.sharding import Mesh
from jax.sharding import PartitionSpec as P

BX = ("bx_0", "bx_1")
BY = ("by_0", "by_1", "by_2")
FIRST = ("bx_0", "by_1", "by_2")
SECOND = ("bx_1", "by_0")

HIGHEST = lax.Precision.HIGHEST
KAPPA = 1.5
GOLDEN = 2.399963229728653
F32 = jnp.float32
BF16 = jnp.bfloat16
NT = (((1,), (1,)), ((), ()))
TN = (((0,), (0,)), ((), ()))
INTERPRET = False


def call(kernel, out_shape, operands, name, flops=0, **kw):
    if not kw.get("grid") and not kw.get("grid_spec"):
        kw["in_specs"] = [
            pl.BlockSpec(memory_space=pltpu.SMEM if op.ndim == 1 else pltpu.VMEM)
            for op in operands
        ]
    return pl.pallas_call(
        kernel,
        out_shape=out_shape,
        name=name,
        interpret=INTERPRET,
        cost_estimate=pl.CostEstimate(flops=flops, transcendentals=0, bytes_accessed=1 << 20),
        **kw,
    )(*operands)


def shape(dims, dtype=F32):
    return jax.ShapeDtypeStruct(dims, dtype)


def directions(number):
    ordinal = np.arange(number, dtype=np.float64)
    height = 1.0 - (2.0 * ordinal + 1.0) / number
    radius = np.sqrt(1.0 - height * height)
    return np.stack([radius * np.cos(GOLDEN * ordinal), radius * np.sin(GOLDEN * ordinal), height])


def leaf_centers(number):
    ordinal = np.arange(number)
    return np.stack(
        [
            2.0 * (ordinal % 2) - 1.0,
            2.0 * (ordinal // 2 % 2) - 1.0,
            2.0 * (ordinal // 4) - (number // 4 - 1),
        ]
    )


def mie_spread(coef_count, mie_count):
    half_count = coef_count // 2
    table = np.zeros((coef_count, mie_count), np.float32)
    for number in range(coef_count):
        degree = math.isqrt(number % half_count + 1)
        table[number, number // half_count * (mie_count // 2) + degree - 1] = 1.0
    return table


def dot(a, b, dims=(((1,), (0,)), ((), ())), precision=None):
    return lax.dot_general(a, b, dims, precision=precision, preferred_element_type=F32)


def split(x):
    high = x.astype(BF16)
    return high, (x - high.astype(F32)).astype(BF16)


def one_hot(rows, row):
    ordinal = lax.broadcasted_iota(jnp.int32, (rows, row.shape[1]), 0)
    return jnp.where(ordinal == row, 1.0, 0.0)


def emit(vector, pattern, cosines, sines, member, leaf_cos, leaf_sin, halo_ref, column_ref):
    coefs = vector.shape[0] // 2
    boxes, dirs = leaf_cos.shape
    rounded = vector.astype(BF16)
    halo_ref[0, : 2 * coefs, :] = rounded
    by_real = dot(pattern, rounded[:coefs])
    by_imag = dot(pattern, rounded[coefs:])
    real = by_real[:dirs] - by_imag[dirs:]
    imag = by_real[dirs:] + by_imag[:dirs]
    out = jnp.concatenate([real * cosines + imag * sines, imag * cosines - real * sines], axis=0)
    high, low = split(out)
    leaf = dot(member, high, NT) + dot(member, low, NT)
    leaf_real, leaf_imag = leaf[:, :dirs], leaf[:, dirs:]
    halo_ref[0, 2 * coefs : 2 * coefs + boxes, :] = leaf_real.astype(BF16)
    halo_ref[0, 2 * coefs + boxes :, :] = leaf_imag.astype(BF16)
    column_real = jnp.sum(leaf_real * leaf_cos + leaf_imag * leaf_sin, axis=0, keepdims=True)
    column_imag = jnp.sum(leaf_imag * leaf_cos - leaf_real * leaf_sin, axis=0, keepdims=True)
    pair = jnp.concatenate([column_real, column_imag], axis=0)
    column_ref[...] = jnp.broadcast_to(pair[None], column_ref.shape)


def lanes(values):
    lane = lax.broadcasted_iota(jnp.int32, (1, 128), 1)
    row = jnp.zeros((1, 128), F32)
    for place, value in values:
        row = row + jnp.where(lane == place, value, 0.0)
    return row


def inner(a, b):
    return jnp.sum(jnp.sum(a * b, axis=0, keepdims=True), axis=1, keepdims=True)


def first_kernel(
    vector, pattern, offsets, planes, box, leaf_cos, leaf_sin, halo, column, cos_ref, sin_ref
):
    phases = KAPPA * (
        planes[0] * offsets[0:1, :] + planes[1] * offsets[1:2, :] + planes[2] * offsets[2:3, :]
    )
    cosines, sines = jnp.cos(phases), jnp.sin(phases)
    cos_ref[...] = cosines
    sin_ref[...] = sines
    member = one_hot(leaf_cos.shape[0], box[...]).astype(BF16)
    emit(
        vector[...], pattern[...], cosines, sines, member, leaf_cos[...], leaf_sin[...], halo, column
    )


def count_kernel(sources, targets, counts):
    source_hot = one_hot(counts.shape[0], sources[0]).astype(BF16)
    target_hot = one_hot(counts.shape[1], targets[0]).astype(BF16)
    counts[...] = dot(source_hot, target_hot, NT).astype(BF16)


def table_kernel(sources, classes, transfer, mie, spread, select, chosen, mie_full):
    number = select.shape[1]
    source_hot = one_hot(number, sources[...]).astype(BF16)
    row = lax.broadcasted_iota(jnp.int32, (number, number), 0)
    col = lax.broadcasted_iota(jnp.int32, (number, number), 1)
    unit = jnp.where(row == col, 1.0, 0.0).astype(BF16)
    select[...] = dot(source_hot, unit, TN).astype(BF16)
    class_hot = one_hot(transfer.shape[0], classes[...])
    chosen[...] = dot(class_hot, transfer[...], TN, HIGHEST)
    mie_full[0] = dot(spread[...], mie[0], precision=HIGHEST)
    mie_full[1] = dot(spread[...], mie[1], precision=HIGHEST)


def window_kernel(place, transfer, window, *, near_z, near_x, groups, run, top_x, top_y):
    high, depth, across, lane = (place[i] for i in range(4))
    ordinal = lax.broadcasted_iota(jnp.int32, (run, 128), 0)
    for z in range(near_z):
        for x in range(near_x):
            start = (across - x) * run - lane + top_y
            apart_y = jnp.abs(ordinal + (start - top_y))
            for group in range(groups):
                shift = (group - high) * near_z + depth - z
                keep = (apart_y >= 2) | (jnp.abs(shift) >= 2)
                for part in range(2):
                    rows = transfer[part, shift + top_x, pl.ds(start, run), :]
                    window[part, z * near_x + x, group * run : (group + 1) * run, :] = jnp.where(
                        keep, rows, 0.0
                    )


def coarse_kernel(columns, window, partial):
    real, imag = columns[:, 0, :][None], columns[:, 1, :][None]
    partial[:, 0, :] = jnp.sum(real * window[0] - imag * window[1], axis=1)
    partial[:, 1, :] = jnp.sum(imag * window[0] + real * window[1], axis=1)


def near_kernel(before, own, after, counts, table, select, chosen, near, leaf_in, columns):
    coefs = near.shape[0] // 2
    classes = table.shape[0]
    spheres = near.shape[1] // 2
    boxes, dirs = leaf_in.shape[0], leaf_in.shape[1] // 2

    @pl.when(pl.program_id(0) == 0)
    def _():
        leaves = []
        for row, part in enumerate((before, own, after)):
            for col in range(3):
                place = (row * 3 + col) * spheres
                columns[:, place : place + spheres] = part[col, : 2 * coefs, :]
                leaves.append(part[col, 2 * coefs :, :])
        around = jnp.concatenate(
            [
                jnp.concatenate([leaf[:boxes] for leaf in leaves], axis=0),
                jnp.concatenate([leaf[boxes:] for leaf in leaves], axis=0),
            ],
            axis=1,
        )
        picked = dot(select[...], around)
        pick_real, pick_imag = picked[:, :dirs], picked[:, dirs:]
        move_real, move_imag = chosen[:, :dirs], chosen[:, dirs:]
        got_real = pick_real * move_real - pick_imag * move_imag
        got_imag = pick_imag * move_real + pick_real * move_imag
        leaf_in[:, :dirs] = jnp.sum(got_real.reshape(boxes, -1, dirs), axis=1)
        leaf_in[:, dirs:] = jnp.sum(got_imag.reshape(boxes, -1, dirs), axis=1)
        near[...] = jnp.zeros(near.shape, F32)

    gathered = dot(columns[...], counts[...]).astype(BF16)
    total = near[...]
    for item in range(classes):
        at = slice(item * spheres, (item + 1) * spheres)
        pair = jnp.concatenate([gathered[:coefs, at], gathered[coefs:, at]], axis=1)
        total = total + dot(table[item], pair)
    near[...] = total


def arrive(partial, near, leaf_in, receive, cosines, sines, member, leaf_cos, leaf_sin, mie_full):
    boxes, dirs = leaf_cos.shape
    coefs = near.shape[0] // 2
    column_real = jnp.sum(partial[:, 0, :], axis=0, keepdims=True)
    column_imag = jnp.sum(partial[:, 1, :], axis=0, keepdims=True)
    incoming = leaf_in + jnp.concatenate(
        [
            column_real * leaf_cos - column_imag * leaf_sin,
            column_real * leaf_sin + column_imag * leaf_cos,
        ],
        axis=1,
    )
    high, low = split(incoming)
    spread = dot(high, member, TN) + dot(low, member, TN)
    real, imag = spread[:dirs], spread[dirs:]
    arriving = jnp.concatenate(
        [real * cosines - imag * sines, real * sines + imag * cosines], axis=1
    ).astype(BF16)
    total = near + dot(receive, arriving)
    half = total.shape[1] // 2
    field_real = total[:coefs, :half] - total[coefs:, half:]
    field_imag = total[coefs:, :half] + total[:coefs, half:]
    mie_real, mie_imag = mie_full[0], mie_full[1]
    return jnp.concatenate(
        [
            field_real * mie_real - field_imag * mie_imag,
            field_real * mie_imag + field_imag * mie_real,
        ],
        axis=0,
    )


def middle_kernel(
    vector,
    partial,
    near,
    leaf_in,
    receive,
    pattern,
    cosines,
    sines,
    box,
    leaf_cos,
    leaf_sin,
    mie_full,
    applied,
    halo,
    column,
    sums,
):
    member = one_hot(leaf_cos.shape[0], box[...]).astype(BF16)
    scattered = arrive(
        partial[...],
        near[...],
        leaf_in[...],
        receive[...],
        cosines[...],
        sines[...],
        member,
        leaf_cos[...],
        leaf_sin[...],
        mie_full[...],
    )
    applied[...] = scattered
    emit(
        scattered,
        pattern[...],
        cosines[...],
        sines[...],
        member,
        leaf_cos[...],
        leaf_sin[...],
        halo,
        column,
    )
    start = vector[...]
    sums[...] = lanes(
        [(0, inner(start, start)), (1, inner(start, scattered)), (2, inner(scattered, scattered))]
    )


def last_kernel(
    vector,
    scattered,
    partial,
    near,
    leaf_in,
    receive,
    cosines,
    sines,
    box,
    leaf_cos,
    leaf_sin,
    mie_full,
    sums,
    applied,
    everyone,
):
    member = one_hot(leaf_cos.shape[0], box[...]).astype(BF16)
    twice = arrive(
        partial[...],
        near[...],
        leaf_in[...],
        receive[...],
        cosines[...],
        sines[...],
        member,
        leaf_cos[...],
        leaf_sin[...],
        mie_full[...],
    )
    applied[...] = twice
    row = sums[...] + lanes(
        [(3, inner(vector[...], twice)), (4, inner(scattered[...], twice)), (5, inner(twice, twice))]
    )
    everyone[...] = jnp.broadcast_to(row[None], everyone.shape)


def relay_kernel(parts, everyone):
    everyone[...] = jnp.broadcast_to(jnp.sum(parts[...], axis=0, keepdims=True), everyone.shape)


def solve_kernel(parts, vector, scattered, twice, solution, residual):
    row = jnp.sum(parts[...], axis=0)
    lane = lax.broadcasted_iota(jnp.int32, row.shape, 1)

    def total(place):
        value = jnp.sum(jnp.where(lane == place, row, 0.0), axis=1, keepdims=True)
        return jnp.broadcast_to(value, (8, 128))

    uu, ud, dd, ue, de, ee = (total(place) for place in range(6))
    beta = jnp.sqrt(uu)
    along = ud / uu
    across = dd - along * ud
    size = jnp.sqrt(across)
    h00 = 1.0 - along
    h10 = size / beta
    turned = de - along * ue
    h01 = (ue - along * ud) / (size * beta)
    h11 = 1.0 + along - turned / across
    rest_u = ue / uu
    rest_d = turned / across
    left = ee - rest_u * ue - rest_d * turned
    h21 = jnp.sqrt(left) / size
    n00 = h00 * h00 + h10 * h10
    n01 = h00 * h01 + h10 * h11
    n11 = h01 * h01 + h11 * h11 + h21 * h21
    l00 = jnp.sqrt(n00)
    l10 = n01 / l00
    l11 = jnp.sqrt(n11 - l10 * l10)
    m0 = beta * h00 / l00
    m1 = (beta * h01 - l10 * m0) / l11
    y1 = m1 / l11
    y0 = (m0 - l10 * y1) / l00
    z0 = h00 * y0 + h01 * y1
    z1 = h10 * y0 + h11 * y1
    step = y1 / size
    sol_u = y0 / beta + step * along
    sol_d = -step
    res_u = (beta - z0) / beta - z1 / size * along + step * (rest_u - rest_d * along)
    res_d = z1 / size + step * rest_d
    res_e = -step
    u, d, e = vector[...], scattered[...], twice[...]
    solution[...] = sol_u[0:1] * u + sol_d[0:1] * d
    residual[...] = res_u[0:1] * u + res_d[0:1] * d + res_e[0:1] * e


def beside(x, axes):
    devices = lax.axis_size(axes)
    up = [(i, i + 1) for i in range(devices - 1)]
    down = [(j, i) for i, j in up]
    return lax.ppermute(x, axes, up), lax.ppermute(x, axes, down)


def exchange(x, axes):
    return lax.all_to_all(x, axes, split_axis=0, concat_axis=0, tiled=True)


def local(
    incident,
    mie,
    offsets,
    sphere_box,
    near_table,
    near_src,
    near_dst,
    pattern,
    receive,
    leaf_transfer,
    far_src,
    far_cls,
    coarse_transfer,
):
    coefs = incident.shape[1]
    spheres = incident.shape[4]
    rows = 2 * coefs
    dirs = pattern.shape[1]
    boxes, entries = far_src.shape[2:]
    classes, pairs = near_src.shape[2:]
    leaf_classes = leaf_transfer.shape[0]
    high_count, near_z = lax.axis_size("bx_0"), lax.axis_size("bx_1")
    near_x = lax.axis_size("by_0")
    run = lax.axis_size(("by_1", "by_2"))
    first_count, second_count = lax.axis_size(FIRST), lax.axis_size(SECOND)
    place = jnp.stack(
        [
            lax.axis_index("bx_0"),
            lax.axis_index("bx_1"),
            lax.axis_index("by_0"),
            lax.axis_index(("by_1", "by_2")),
        ]
    ).astype(jnp.int32)

    planes = jnp.asarray(directions(dirs)[:, :, None].astype(np.float32))
    centre = KAPPA * (leaf_centers(boxes).T @ directions(dirs))
    leaf_cos = jnp.asarray(np.cos(centre).astype(np.float32))
    leaf_sin = jnp.asarray(np.sin(centre).astype(np.float32))

    vector = incident.reshape(rows, spheres)
    box = sphere_box.reshape(1, spheres)
    pattern = pattern.reshape(2 * dirs, coefs)
    receive = receive.reshape(rows, dirs)
    table = near_table.reshape(classes, rows, coefs)

    halo_shape = shape((1, rows + 2 * boxes, spheres), BF16)
    column_shape = shape((first_count, 2, dirs))
    halo, column, cosines, sines = call(
        first_kernel,
        (halo_shape, column_shape, shape((dirs, spheres)), shape((dirs, spheres))),
        (vector, pattern, offsets.reshape(3, spheres), planes, box, leaf_cos, leaf_sin),
        "first",
        flops=1 << 26,
    )
    counts = call(
        count_kernel,
        shape((9 * spheres, classes * spheres), BF16),
        (near_src.reshape(classes, 1, pairs), near_dst.reshape(classes, 1, pairs)),
        "counts",
        flops=1 << 31,
        grid=(classes,),
        in_specs=[pl.BlockSpec((1, 1, pairs), lambda k: (k, 0, 0))] * 2,
        out_specs=pl.BlockSpec((9 * spheres, spheres), lambda k: (0, k)),
    )
    select, chosen, mie_full = call(
        table_kernel,
        (
            shape((boxes * entries, 9 * boxes), BF16),
            shape((boxes * entries, 2 * dirs)),
            shape((2, coefs, spheres)),
        ),
        (
            far_src.reshape(1, boxes * entries),
            far_cls.reshape(1, boxes * entries),
            leaf_transfer.reshape(leaf_classes, 2 * dirs),
            mie.reshape(2, mie.shape[1], spheres),
            jnp.asarray(mie_spread(coefs, mie.shape[1])),
        ),
        "tables",
        flops=1 << 28,
    )
    window = call(
        functools.partial(
            window_kernel,
            near_z=near_z,
            near_x=near_x,
            groups=high_count,
            run=run,
            top_x=high_count * near_z - 1,
            top_y=near_x * run - 1,
        ),
        shape((2, second_count, first_count, dirs)),
        (place, coarse_transfer),
        "window",
        flops=1 << 28,
    )

    chunk = 4 if classes % 4 == 0 else 1
    whole3 = pl.BlockSpec((3, rows + 2 * boxes, spheres), lambda k: (0, 0, 0))

    def apply(halo, column):
        before, after = beside(halo, BY)
        line = jnp.concatenate([before, halo, after], axis=0)
        columns = exchange(column, FIRST)
        up, down = beside(line, BX)
        partial = call(
            coarse_kernel, shape((second_count, 2, dirs)), (columns, window), "coarse", 1 << 24
        )
        partial = exchange(partial, SECOND)
        near, leaf_in = call(
            near_kernel,
            (shape((rows, 2 * spheres)), shape((boxes, 2 * dirs))),
            (up, line, down, counts, table, select, chosen),
            "near",
            flops=1 << 31,
            grid=(classes // chunk,),
            in_specs=[
                whole3,
                whole3,
                whole3,
                pl.BlockSpec((9 * spheres, chunk * spheres), lambda k: (0, k)),
                pl.BlockSpec((chunk, rows, coefs), lambda k: (k, 0, 0)),
                pl.BlockSpec((boxes * entries, 9 * boxes), lambda k: (0, 0)),
                pl.BlockSpec((boxes * entries, 2 * dirs), lambda k: (0, 0)),
            ],
            out_specs=(
                pl.BlockSpec((rows, 2 * spheres), lambda k: (0, 0)),
                pl.BlockSpec((boxes, 2 * dirs), lambda k: (0, 0)),
            ),
            scratch_shapes=[pltpu.VMEM((rows, 9 * spheres), BF16)],
        )
        return partial, near, leaf_in

    partial, near, leaf_in = apply(halo, column)
    once, halo, column, sums = call(
        middle_kernel,
        (shape((rows, spheres)), halo_shape, column_shape, shape((1, 128))),
        (
            vector,
            partial,
            near,
            leaf_in,
            receive,
            pattern,
            cosines,
            sines,
            box,
            leaf_cos,
            leaf_sin,
            mie_full,
        ),
        "middle",
        flops=1 << 26,
    )
    partial, near, leaf_in = apply(halo, column)
    twice, everyone = call(
        last_kernel,
        (shape((rows, spheres)), shape((first_count, 1, 128))),
        (
            vector,
            once,
            partial,
            near,
            leaf_in,
            receive,
            cosines,
            sines,
            box,
            leaf_cos,
            leaf_sin,
            mie_full,
            sums,
        ),
        "last",
        flops=1 << 26,
    )
    everyone = call(
        relay_kernel, shape((second_count, 1, 128)), (exchange(everyone, FIRST),), "relay", 1 << 20
    )
    solved, residual = call(
        solve_kernel,
        (shape((rows, spheres)), shape((rows, spheres))),
        (exchange(everyone, SECOND), vector, once, twice),
        "solve",
        flops=1 << 24,
    )
    return solved.reshape(incident.shape), residual.reshape(incident.shape)


def build(devices, sizes):
    torus = Mesh(devices.reshape(sizes), BX + BY)
    placed = (
        P(None, None, BX, BY, None),
        P(None, None, BX, BY, None),
        P(None, BX, BY, None),
        P(BX, BY, None),
        P(),
        P(BX, BY, None, None),
        P(BX, BY, None, None),
        P(),
        P(),
        P(),
        P(BX, BY, None, None),
        P(BX, BY, None, None),
        P(),
    )
    return jax.shard_map(
        local,
        mesh=torus,
        in_specs=placed,
        out_specs=(P(None, None, BX, BY, None), P(None, None, BX, BY, None)),
        check_vma=False,
    )


def solution(mesh):
    return build(mesh.devices, (2, 8, 4, 4, 2))
```

time: 453 us -> 172 us (0.38)
  blocking collectives: 180 us -> 43.5 us
  other arithmetic: 80.9 us -> 0.59 us
  local copies, waits for them, and re-layouts: 83.4 us -> 15.1 us
  Pallas kernels: 0 us -> 41.8 us
  between operations: 12.7 us -> 0.87 us
  matrix products: 10.1 us -> 0 us
  starting transfers between devices: 72.1 us -> 63.1 us
  waiting for transfers between devices: 10.4 us -> 5.59 us
    psum x15 -> x0, blocking collectives: 180 us -> none  [one_axis_at_a_time(): return functools.reduce(lax.psum, axes, x)]
    scatter-add x2 -> x0, other arithmetic: 45.9 us -> none  [local(): near = jnp.zeros((block_rows, spheres), jnp.float32).at[:, targets_flat]....]
    all_to_all x0 -> x3, blocking collectives: none -> 43.5 us  [exchange(): return lax.all_to_all(x, axes, split_axis=0, concat_axis=0, tiled=True)]
    pallas_call x0 -> x12, Pallas kernels: none -> 41.8 us  [call(): pl.pallas_call(kernel, out_shape=out_shape, name=name, interpret=INTERPRE...]
    gather x4 -> x0, local copies, waits for them, and re-layouts: 38.2 us -> none  [the longest x2 34 us: local(): jnp.take(columns, sources_flat, axis=1)]
    reshape x11 -> x5, local copies, waits for them, and re-layouts: 23.1 us -> 4.54 us  [the longest x1 1.33 us: local(): near_src.reshape(classes, 1, pairs)]
    dot_general x16 -> x0, matrix products: 10.1 us -> none  [the longest x2 2.05 us: local(): jnp.dot(send_block, rounded.reshape(block_rows, spheres), preferred_eleme...]
    ppermute x16 -> x8, starting transfers between devices: 36.2 us -> 28.8 us  [beside(): return (lax.ppermute(x, axes, up), lax.ppermute(x, axes, down))]
  transfers between devices with their start and end apart: 20 -> 11, of which waited for: 5 -> 3; matrix products, arithmetic and copies ran while one was open for 20% -> 5% of each run, Pallas kernels for 0% -> 18%
where the time goes in v1:
time: 172 us; the launch traced here: 171 us
  starting transfers between devices  63.1 us (37%)
  blocking collectives  43.5 us (25%)
  Pallas kernels  41.8 us (24%)
  local copies, waits for them, and re-layouts  15.1 us (9%)
  waiting for transfers between devices  5.59 us (3%)
    all_to_all x3, blocking collectives, exchange(): return lax.all_to_all(x, axes, split_axis=0, concat_axis=0, tiled=True)  43.5 us
    pallas_call x12, Pallas kernels, call(): pl.pallas_call(kernel, out_shape=out_shape, name=name, interpret=INTERPRE...  41.8 us
    all_to_all x3, starting transfers between devices, exchange(): return lax.all_to_all(x, axes, split_axis=0, concat_axis=0, tiled=True)  34.2 us
    ppermute x8, starting transfers between devices, beside(): return (lax.ppermute(x, axes, up), lax.ppermute(x, axes, down))  28.8 us
    unnamed x37, local copies, waits for them, and re-layouts  10.6 us
  transfers between devices with their start and end apart: 11, of which 3 were waited for; matrix products, arithmetic and copies ran while one was open for 5% of the time, Pallas kernels for 18%

profile of v1, /device:TPU:1, one launch (start us, length us, event | category | flops | bytes accessed | tf_op | source)
XLA Modules:
  0.0 170.5 jit_solution(966768574082821311)
XLA Ops:
  1.9 1.5 copy.23
  3.4 2.2 %first.1 = (bf16[1,224,128]{2,1,0:T(8,128)(2,1)}, f32[16,2,128]{2,1,0:T(2,128)}, f32[128,128]{1,0:T(8,128)}, f32[128,128]{1,0:T(8,128)}) custom-call(f32[192,128]{1,0:T(8,128)} %bitcast.33, bf16[256,96]{1,0:T(8,128)(2,1)} %bitcast.37, f32[3,128]{1,0:T(4,128)} %bitcast.44, f32[3,128,1]{2,1,0:T(8,128)} %constant.30.clone.planes, s32[1,128]{1,0:T(1,128)} %bitcast.45, ...), custom_call_target="tpu_custom_call" | custom-call | flops 67108864 | bytes 1048576 | tf_op jit(solution)/shard_map/first/pallas_call | solution.py:34
  5.6 4.6 %collective-permute-start = (bf16[1,224,128]{2,1,0:T(8,128)(2,1)}, bf16[1,224,128]{2,1,0:T(8,128)(2,1)S(1)}, u32[]{:S(2)}, u32[]{:S(2)}) collective-permute-start(bf16[1,224,128]{2,1,0:T(8,128)(2,1)} %get-tuple-element.22), channel_id=1, source_target_pairs={{0,1},{1,2},{2,3},{3,4},{4,5},{5,6},{6,7},{7,8},{8,9},{9,10},{10,1... | collective-permute-start | bytes 172040 | tf_op jit(solution)/shard_map/ppermute | solution.py:389
  10.2 5.5 %collective-permute-start.1 = (bf16[1,224,128]{2,1,0:T(8,128)(2,1)}, bf16[1,224,128]{2,1,0:T(8,128)(2,1)S(1)}, u32[]{:S(2)}, u32[]{:S(2)}) collective-permute-start(bf16[1,224,128]{2,1,0:T(8,128)(2,1)} %get-tuple-element.22), channel_id=1, source_target_pairs={{1,0},{2,1},{3,2},{4,3},{5,4},{6,5},{7,6},{8,7},{9,8},{10,9},{11,1... | collective-permute-start | bytes 172040 | tf_op jit(solution)/shard_map/ppermute | solution.py:389
  15.7 3.6 %all-to-all-start = ((f32[16,2,128]{2,1,0:T(2,128)}), f32[16,2,128]{2,1,0:T(2,128)S(1)}, u32[]{:S(2)}, u32[]{:S(2)}) async-start(f32[16,2,128]{2,1,0:T(2,128)} %get-tuple-element.21), calls=%async_computation | async-start | bytes 32768 | tf_op jit(solution)/shard_map/all_to_all | solution.py:393
  19.3 1.3 reshape.50.sources
  20.6 1.3 reshape.51.targets
  22.8 1.4 collective-permute-start.3
  24.3 4.6 %collective-permute-start.2 = (bf16[3,224,128]{2,1,0:T(8,128)(2,1)S(1)}, bf16[3,224,128]{2,1,0:T(8,128)(2,1)S(1)}, u32[]{:S(2)}, u32[]{:S(2)}) collective-permute-start(bf16[3,224,128]{2,1,0:T(8,128)(2,1)S(1)} %constant_dynamic-update-slice_fusion.own), channel_id=1, source_target_pairs={{0,32},{32,64},{64,96},{96,128},{128,160},{160,192},{192,224},{224... | collective-permute-start | bytes 516104 | tf_op jit(solution)/shard_map/ppermute | solution.py:389
  28.9 10.4 %counts.1 = bf16[1152,2048]{1,0:T(8,128)(2,1)} custom-call(s32[16,1,256]{2,1,0:T(1,128)} %reshape.50.sources, s32[16,1,256]{2,1,0:T(1,128)} %reshape.51.targets), custom_call_target="tpu_custom_call" | custom-call | flops 2147483648 | bytes 1048576 | tf_op jit(solution)/shard_map/counts/pallas_call | solution.py:34
  39.3 1.6 copy.24.transfer
  41.5 2.4 %window.1 = f32[2,32,16,128]{3,2,1,0:T(8,128)} custom-call(s32[4]{0:T(128)} %pad_add_fusion.place, f32[2,31,63,128]{3,2,1,0:T(8,128)} %copy.24.transfer), custom_call_target="tpu_custom_call" | custom-call | flops 268435456 | bytes 1048576 | tf_op jit(solution)/shard_map/window/pallas_call | solution.py:34
  46.5 2.3 %tables.1 = (bf16[384,144]{1,0:T(8,128)(2,1)}, f32[384,256]{1,0:T(8,128)}, f32[2,96,128]{2,1,0:T(8,128)}) custom-call(s32[1,384]{1,0:T(1,128)} %reshape.53.sources, s32[1,384]{1,0:T(1,128)} %reshape.54.classes, f32[32,256]{1,0:T(8,128)} %bitcast.43, f32[2,12,128]{2,1,0:T(8,128)} %copy.26.mie, f32[96,12]{1,0:T(8,128)} %constant.33.clone.spread), custom_call_target="tpu_custom_call" | custom-call | flops 268435456 | bytes 1048576 | tf_op jit(solution)/shard_map/tables/pallas_call | solution.py:34
  49.4 1.8 %coarse.2 = f32[32,2,128]{2,1,0:T(2,128)} custom-call(f32[16,2,128]{2,1,0:T(2,128)} %copy-done.3, f32[2,32,16,128]{3,2,1,0:T(8,128)} %window.1), custom_call_target="tpu_custom_call" | custom-call | flops 16777216 | bytes 1048576 | tf_op jit(solution)/shard_map/coarse/pallas_call | solution.py:34
  51.2 21.5 %all-to-all-start.1 = ((f32[32,2,128]{2,1,0:T(2,128)}), f32[32,2,128]{2,1,0:T(2,128)S(1)}, u32[]{:S(2)}, u32[]{:S(2)}) async-start(f32[32,2,128]{2,1,0:T(2,128)} %coarse.2), calls=%async_computation.1 | async-start | bytes 65536 | tf_op jit(solution)/shard_map/all_to_all | solution.py:393
  73.4 6.3 %near.2 = (f32[192,256]{1,0:T(8,128)}, f32[16,256]{1,0:T(8,128)}) custom-call(bf16[3,224,128]{2,1,0:T(8,128)(2,1)} %copy-done.11, bf16[3,224,128]{2,1,0:T(8,128)(2,1)} %copy-done.5, bf16[3,224,128]{2,1,0:T(8,128)(2,1)} %copy-done.10, bf16[1152,2048]{1,0:T(8,128)(2,1)} %counts.1, bf16[16,192,96]{2,1,0:T(8,128)(2,1)} %bitcast.48, ...), custom_call_target="tpu_custom_call" | custom-call | flops 2147483648 | bytes 1048576 | tf_op jit(solution)/shard_map/near/pallas_call | solution.py:34
  79.8 1.6 all-to-all-done.1.partial
  82.0 2.7 %middle.1 = (f32[192,128]{1,0:T(8,128)}, bf16[1,224,128]{2,1,0:T(8,128)(2,1)}, f32[16,2,128]{2,1,0:T(2,128)}, f32[1,128]{1,0:T(1,128)}) custom-call(f32[192,128]{1,0:T(8,128)} %bitcast.34, f32[32,2,128]{2,1,0:T(2,128)} %copy-done.2, f32[192,256]{1,0:T(8,128)} %get-tuple-element.25.near, f32[16,256]{1,0:T(8,128)} %get-tuple-element.26.leaf_in, ...), custom_call_target="tpu_custom_call" | custom-call | flops 67108864 | bytes 1048576 | tf_op jit(solution)/shard_map/middle/pallas_call | solution.py:34
  84.6 5.5 %collective-permute-start.4 = (bf16[1,224,128]{2,1,0:T(8,128)(2,1)}, bf16[1,224,128]{2,1,0:T(8,128)(2,1)S(1)}, u32[]{:S(2)}, u32[]{:S(2)}) collective-permute-start(bf16[1,224,128]{2,1,0:T(8,128)(2,1)} %get-tuple-element.32), channel_id=1, source_target_pairs={{0,1},{1,2},{2,3},{3,4},{4,5},{5,6},{6,7},{7,8},{8,9},{9,10},{10,1... | collective-permute-start | bytes 172040 | tf_op jit(solution)/shard_map/ppermute | solution.py:389
  90.2 1.9 %collective-permute-start.5 = (bf16[1,224,128]{2,1,0:T(8,128)(2,1)}, bf16[1,224,128]{2,1,0:T(8,128)(2,1)S(1)}, u32[]{:S(2)}, u32[]{:S(2)}) collective-permute-start(bf16[1,224,128]{2,1,0:T(8,128)(2,1)} %get-tuple-element.32), channel_id=1, source_target_pairs={{1,0},{2,1},{3,2},{4,3},{5,4},{6,5},{7,6},{8,7},{9,8},{10,9},{11,1... | collective-permute-start | bytes 172040 | tf_op jit(solution)/shard_map/ppermute | solution.py:389
  93.0 2.9 %collective-permute-done.5 = bf16[1,224,128]{2,1,0:T(8,128)(2,1)S(1)} collective-permute-done((bf16[1,224,128]{2,1,0:T(8,128)(2,1)}, bf16[1,224,128]{2,1,0:T(8,128)(2,1)S(1)}, u32[]{:S(2)}, u32[]{:S(2)}) %collective-permute-start.5) | collective-permute-done | bytes 57376 | tf_op jit(solution)/shard_map/ppermute | solution.py:389
  95.9 1.3 collective-permute-start.7
  97.2 4.0 %collective-permute-start.6 = (bf16[3,224,128]{2,1,0:T(8,128)(2,1)S(1)}, bf16[3,224,128]{2,1,0:T(8,128)(2,1)S(1)}, u32[]{:S(2)}, u32[]{:S(2)}) collective-permute-start(bf16[3,224,128]{2,1,0:T(8,128)(2,1)S(1)} %constant_dynamic-update-slice_fusion.3.own), channel_id=1, source_target_pairs={{0,32},{32,64},{64,96},{96,128},{128,160},{160,192},{192,224},{224... | collective-permute-start | bytes 516104 | tf_op jit(solution)/shard_map/ppermute | solution.py:389
  101.2 15.0 %all_to_all.30.columns = f32[16,2,128]{2,1,0:T(2,128)} all-to-all(f32[16,2,128]{2,1,0:T(2,128)} %get-tuple-element.31), channel_id=1, replica_groups=mesh['bx_0'=2,'bx_1'=8,'by_0'=4,'by_1'=4,'by_2'=2] {'bx_0','by_1','by_2'}, dimensions={0} | all-to-all | bytes 32768 | tf_op jit(solution)/shard_map/all_to_all | solution.py:393
  116.2 1.8 %coarse.3 = f32[32,2,128]{2,1,0:T(2,128)} custom-call(f32[16,2,128]{2,1,0:T(2,128)} %all_to_all.30.columns, f32[2,32,16,128]{3,2,1,0:T(8,128)} %window.1), custom_call_target="tpu_custom_call" | custom-call | flops 16777216 | bytes 1048576 | tf_op jit(solution)/shard_map/coarse/pallas_call | solution.py:34
  118.0 9.2 %all-to-all-start.3 = ((f32[32,2,128]{2,1,0:T(2,128)}), f32[32,2,128]{2,1,0:T(2,128)S(1)}, u32[]{:S(2)}, u32[]{:S(2)}) async-start(f32[32,2,128]{2,1,0:T(2,128)} %coarse.3), calls=%async_computation.3 | async-start | bytes 65536 | tf_op jit(solution)/shard_map/all_to_all | solution.py:393
  128.5 6.3 %near.3 = (f32[192,256]{1,0:T(8,128)}, f32[16,256]{1,0:T(8,128)}) custom-call(bf16[3,224,128]{2,1,0:T(8,128)(2,1)} %copy-done.13, bf16[3,224,128]{2,1,0:T(8,128)(2,1)} %copy-done.6, bf16[3,224,128]{2,1,0:T(8,128)(2,1)} %copy-done.12, bf16[1152,2048]{1,0:T(8,128)(2,1)} %counts.1, bf16[16,192,96]{2,1,0:T(8,128)(2,1)} %bitcast.49, ...), custom_call_target="tpu_custom_call" | custom-call | flops 2147483648 | bytes 1048576 | tf_op jit(solution)/shard_map/near/pallas_call | solution.py:34
  136.5 2.3 %last.1 = (f32[192,128]{1,0:T(8,128)}, f32[16,1,128]{2,1,0:T(1,128)}) custom-call(f32[192,128]{1,0:T(8,128)} %bitcast.35, f32[192,128]{1,0:T(8,128)} %get-tuple-element.30.scattered, f32[32,2,128]{2,1,0:T(2,128)} %copy-done.1, f32[192,256]{1,0:T(8,128)} %get-tuple-element.33.near, f32[16,256]{1,0:T(8,128)} %get-tuple-element.34.leaf_in, ...), custom_call_target="tpu_custom_call" | custom-call | flops 67108864 | bytes 1048576 | tf_op jit(solution)/shard_map/last/pallas_call | solution.py:34
  138.8 12.6 %all_to_all.31.parts = f32[16,1,128]{2,1,0:T(1,128)} all-to-all(f32[16,1,128]{2,1,0:T(1,128)} %get-tuple-element.36), channel_id=1, replica_groups=mesh['bx_0'=2,'bx_1'=8,'by_0'=4,'by_1'=4,'by_2'=2] {'bx_0','by_1','by_2'}, dimensions={0} | all-to-all | bytes 16384 | tf_op jit(solution)/shard_map/all_to_all | solution.py:393
  151.4 1.3 relay.1
  152.8 15.9 %all_to_all.32.parts = f32[32,1,128]{2,1,0:T(1,128)} all-to-all(f32[32,1,128]{2,1,0:T(1,128)} %relay.1), channel_id=1, replica_groups=mesh['bx_0'=2,'bx_1'=8,'by_0'=4,'by_1'=4,'by_2'=2] {'bx_1','by_0'}, dimensions={0} | all-to-all | bytes 32768 | tf_op jit(solution)/shard_map/all_to_all | solution.py:393
  168.6 1.9 %solve.1 = (f32[192,128]{1,0:T(8,128)}, f32[192,128]{1,0:T(8,128)}) custom-call(f32[32,1,128]{2,1,0:T(1,128)} %all_to_all.32.parts, f32[192,128]{1,0:T(8,128)} %bitcast.36, f32[192,128]{1,0:T(8,128)} %get-tuple-element.30.scattered, f32[192,128]{1,0:T(8,128)} %get-tuple-element.37.twice), custom_call_target="tpu_custom_call" | custom-call | flops 16777216 | bytes 1048576 | tf_op jit(solution)/shard_map/solve/pallas_call | solution.py:34
  (50 shorter events, 11.0 us)
Async XLA Ops:
  5.6 16.3 %collective-permute-start = (bf16[1,224,128]{2,1,0:T(8,128)(2,1)}, bf16[1,224,128]{2,1,0:T(8,128)(2,1)S(1)}, u32[]{:S(2)}, u32[]{:S(2)}) collective-permute-start(bf16[1,224,128]{2,1,0:T(8,128)(2,1)} %get-tuple-element.22), channel_id=1, source_target_pairs={{0,1},{1,2},{2,3},{3,4},{4,5},{5,6},{6,7},{7,8},{8,9},{9,10},{10,1... | collective-permute-start | bytes 172040 | tf_op jit(solution)/shard_map/ppermute | solution.py:389
  10.2 12.6 %collective-permute-start.1 = (bf16[1,224,128]{2,1,0:T(8,128)(2,1)}, bf16[1,224,128]{2,1,0:T(8,128)(2,1)S(1)}, u32[]{:S(2)}, u32[]{:S(2)}) collective-permute-start(bf16[1,224,128]{2,1,0:T(8,128)(2,1)} %get-tuple-element.22), channel_id=1, source_target_pairs={{1,0},{2,1},{3,2},{4,3},{5,4},{6,5},{7,6},{8,7},{9,8},{10,9},{11,1... | collective-permute-start | bytes 172040 | tf_op jit(solution)/shard_map/ppermute | solution.py:389
  15.7 33.1 %all-to-all-start = ((f32[16,2,128]{2,1,0:T(2,128)}), f32[16,2,128]{2,1,0:T(2,128)S(1)}, u32[]{:S(2)}, u32[]{:S(2)}) async-start(f32[16,2,128]{2,1,0:T(2,128)} %get-tuple-element.21), calls=%async_computation | async-start | bytes 32768 | tf_op jit(solution)/shard_map/all_to_all | solution.py:393
  22.8 16.5 %copy-start.5 = (bf16[3,224,128]{2,1,0:T(8,128)(2,1)}, bf16[3,224,128]{2,1,0:T(8,128)(2,1)S(1)}, u32[]{:S(2)}) copy-start(bf16[3,224,128]{2,1,0:T(8,128)(2,1)S(1)} %constant_dynamic-update-slice_fusion.own) | copy-start | bytes 516100
  22.8 16.5 %copy-start = (f32[2,31,63,128]{3,0,2,1:T(2,128)S(1)}, f32[2,31,63,128]{3,0,2,1:T(2,128)}, u32[]{:S(2)}) copy-start(f32[2,31,63,128]{3,0,2,1:T(2,128)} %param.29) | copy-start | bytes 5999620
  22.8 49.8 %collective-permute-start.3 = (bf16[3,224,128]{2,1,0:T(8,128)(2,1)S(1)}, bf16[3,224,128]{2,1,0:T(8,128)(2,1)S(1)}, u32[]{:S(2)}, u32[]{:S(2)}) collective-permute-start(bf16[3,224,128]{2,1,0:T(8,128)(2,1)S(1)} %constant_dynamic-update-slice_fusion.own), channel_id=1, source_target_pairs={{32,0},{64,32},{96,64},{128,96},{160,128},{192,160},{224,192},{256... | collective-permute-start | bytes 516104 | tf_op jit(solution)/shard_map/ppermute | solution.py:389
  24.3 48.4 %collective-permute-start.2 = (bf16[3,224,128]{2,1,0:T(8,128)(2,1)S(1)}, bf16[3,224,128]{2,1,0:T(8,128)(2,1)S(1)}, u32[]{:S(2)}, u32[]{:S(2)}) collective-permute-start(bf16[3,224,128]{2,1,0:T(8,128)(2,1)S(1)} %constant_dynamic-update-slice_fusion.own), channel_id=1, source_target_pairs={{0,32},{32,64},{64,96},{96,128},{128,160},{160,192},{192,224},{224... | collective-permute-start | bytes 516104 | tf_op jit(solution)/shard_map/ppermute | solution.py:389
  40.9 3.1 %copy-start.8 = (s32[1,1,16,24]{3,2,1,0:T(8,128)S(1)}, s32[1,1,16,24]{3,2,1,0:T(8,128)}, u32[]{:S(2)}) copy-start(s32[1,1,16,24]{3,2,1,0:T(8,128)} %param.27) | copy-start | bytes 4612
  40.9 3.7 %copy-start.9 = (s32[1,1,16,24]{3,2,1,0:T(8,128)S(1)}, s32[1,1,16,24]{3,2,1,0:T(8,128)}, u32[]{:S(2)}) copy-start(s32[1,1,16,24]{3,2,1,0:T(8,128)} %param.28) | copy-start | bytes 4612
  40.9 4.3 %copy-start.7 = (f32[2,12,1,1,128]{4,3,2,1,0:T(1,128)S(1)}, f32[2,12,1,1,128]{4,3,2,1,0:T(1,128)}, u32[]{:S(2)}) copy-start(f32[2,12,1,1,128]{4,3,2,1,0:T(1,128)} %param.18) | copy-start | bytes 36868
  41.0 4.9 %copy-start.4 = (f32[32,2,128]{2,1,0:T(2,128)S(1)}, f32[32,2,128]{2,1,0:T(2,128)}, u32[]{:S(2)}) copy-start(f32[32,2,128]{2,1,0:T(2,128)} %param.26) | copy-start | bytes 98308
  48.8 0.6 copy-start.3
  51.2 30.2 %all-to-all-start.1 = ((f32[32,2,128]{2,1,0:T(2,128)}), f32[32,2,128]{2,1,0:T(2,128)S(1)}, u32[]{:S(2)}, u32[]{:S(2)}) async-start(f32[32,2,128]{2,1,0:T(2,128)} %coarse.2), calls=%async_computation.1 | async-start | bytes 65536 | tf_op jit(solution)/shard_map/all_to_all | solution.py:393
  72.7 0.7 copy-start.10
  72.7 0.7 copy-start.11
  81.4 0.6 copy-start.2
  84.6 7.5 %collective-permute-start.4 = (bf16[1,224,128]{2,1,0:T(8,128)(2,1)}, bf16[1,224,128]{2,1,0:T(8,128)(2,1)S(1)}, u32[]{:S(2)}, u32[]{:S(2)}) collective-permute-start(bf16[1,224,128]{2,1,0:T(8,128)(2,1)} %get-tuple-element.32), channel_id=1, source_target_pairs={{0,1},{1,2},{2,3},{3,4},{4,5},{5,6},{6,7},{7,8},{8,9},{9,10},{10,1... | collective-permute-start | bytes 172040 | tf_op jit(solution)/shard_map/ppermute | solution.py:389
  90.2 5.7 %collective-permute-start.5 = (bf16[1,224,128]{2,1,0:T(8,128)(2,1)}, bf16[1,224,128]{2,1,0:T(8,128)(2,1)S(1)}, u32[]{:S(2)}, u32[]{:S(2)}) collective-permute-start(bf16[1,224,128]{2,1,0:T(8,128)(2,1)} %get-tuple-element.32), channel_id=1, source_target_pairs={{1,0},{2,1},{3,2},{4,3},{5,4},{6,5},{7,6},{8,7},{9,8},{10,9},{11,1... | collective-permute-start | bytes 172040 | tf_op jit(solution)/shard_map/ppermute | solution.py:389
  95.9 31.3 %copy-start.6 = (bf16[3,224,128]{2,1,0:T(8,128)(2,1)}, bf16[3,224,128]{2,1,0:T(8,128)(2,1)S(1)}, u32[]{:S(2)}) copy-start(bf16[3,224,128]{2,1,0:T(8,128)(2,1)S(1)} %constant_dynamic-update-slice_fusion.3.own) | copy-start | bytes 516100
  95.9 31.3 %collective-permute-start.7 = (bf16[3,224,128]{2,1,0:T(8,128)(2,1)S(1)}, bf16[3,224,128]{2,1,0:T(8,128)(2,1)S(1)}, u32[]{:S(2)}, u32[]{:S(2)}) collective-permute-start(bf16[3,224,128]{2,1,0:T(8,128)(2,1)S(1)} %constant_dynamic-update-slice_fusion.3.own), channel_id=1, source_target_pairs={{32,0},{64,32},{96,64},{128,96},{160,128},{192,160},{224,192},{256... | collective-permute-start | bytes 516104 | tf_op jit(solution)/shard_map/ppermute | solution.py:389
  97.2 30.0 %collective-permute-start.6 = (bf16[3,224,128]{2,1,0:T(8,128)(2,1)S(1)}, bf16[3,224,128]{2,1,0:T(8,128)(2,1)S(1)}, u32[]{:S(2)}, u32[]{:S(2)}) collective-permute-start(bf16[3,224,128]{2,1,0:T(8,128)(2,1)S(1)} %constant_dynamic-update-slice_fusion.3.own), channel_id=1, source_target_pairs={{0,32},{32,64},{64,96},{96,128},{128,160},{160,192},{192,224},{224... | collective-permute-start | bytes 516104 | tf_op jit(solution)/shard_map/ppermute | solution.py:389
  118.0 17.9 %all-to-all-start.3 = ((f32[32,2,128]{2,1,0:T(2,128)}), f32[32,2,128]{2,1,0:T(2,128)S(1)}, u32[]{:S(2)}, u32[]{:S(2)}) async-start(f32[32,2,128]{2,1,0:T(2,128)} %coarse.3), calls=%async_computation.3 | async-start | bytes 65536 | tf_op jit(solution)/shard_map/all_to_all | solution.py:393
  127.2 0.7 copy-start.12
  127.9 0.7 copy-start.13
  135.9 0.6 copy-start.1

commit v2 on v1

--- a/solution.py
+++ b/solution.py
@@ -25,8 +25,8 @@
 INTERPRET = False
 
 
-def call(kernel, out_shape, operands, name, flops=0, **kw):
-    if not kw.get("grid") and not kw.get("grid_spec"):
+def call(kernel, out_shape, operands, flops=0, **kw):
+    if "grid" not in kw:
         kw["in_specs"] = [
             pl.BlockSpec(memory_space=pltpu.SMEM if op.ndim == 1 else pltpu.VMEM)
             for op in operands
@@ -34,11 +34,18 @@
     return pl.pallas_call(
         kernel,
         out_shape=out_shape,
-        name=name,
         interpret=INTERPRET,
         cost_estimate=pl.CostEstimate(flops=flops, transcendentals=0, bytes_accessed=1 << 20),
         **kw,
     )(*operands)
+
+
+def resident(x):
+    return x if INTERPRET else pltpu.with_memory_space_constraint(x, pltpu.VMEM)
+
+
+def kept(dims, dtype=F32):
+    return shape(dims, dtype) if INTERPRET else pltpu.VMEM(dims, dtype)
 
 
 def shape(dims, dtype=F32):
@@ -91,8 +98,9 @@
     boxes, dirs = leaf_cos.shape
     rounded = vector.astype(BF16)
     halo_ref[0, : 2 * coefs, :] = rounded
-    by_real = dot(pattern, rounded[:coefs])
-    by_imag = dot(pattern, rounded[coefs:])
+    both = jnp.concatenate([pattern[0], pattern[1]], axis=1)
+    by_real = dot(both, rounded[:coefs], TN)
+    by_imag = dot(both, rounded[coefs:], TN)
     real = by_real[:dirs] - by_imag[dirs:]
     imag = by_real[dirs:] + by_imag[:dirs]
     out = jnp.concatenate([real * cosines + imag * sines, imag * cosines - real * sines], axis=0)
@@ -123,7 +131,7 @@
     vector, pattern, offsets, planes, box, leaf_cos, leaf_sin, halo, column, cos_ref, sin_ref
 ):
     phases = KAPPA * (
-        planes[0] * offsets[0:1, :] + planes[1] * offsets[1:2, :] + planes[2] * offsets[2:3, :]
+        planes[0] * offsets[0] + planes[1] * offsets[1] + planes[2] * offsets[2]
     )
     cosines, sines = jnp.cos(phases), jnp.sin(phases)
     cos_ref[...] = cosines
@@ -134,23 +142,46 @@
     )
 
 
-def count_kernel(sources, targets, counts):
-    source_hot = one_hot(counts.shape[0], sources[0]).astype(BF16)
-    target_hot = one_hot(counts.shape[1], targets[0]).astype(BF16)
-    counts[...] = dot(source_hot, target_hot, NT).astype(BF16)
-
-
-def table_kernel(sources, classes, transfer, mie, spread, select, chosen, mie_full):
-    number = select.shape[1]
-    source_hot = one_hot(number, sources[...]).astype(BF16)
-    row = lax.broadcasted_iota(jnp.int32, (number, number), 0)
-    col = lax.broadcasted_iota(jnp.int32, (number, number), 1)
+def mirrored(sources, width, flip_x, flip_y):
+    line = 3 * width
+    flat = jnp.where(sources < line, 0, jnp.where(sources < 2 * line, 1, 2))
+    within = sources - line * flat
+    side = jnp.where(within < width, 0, jnp.where(within < 2 * width, 1, 2))
+    return sources + flip_x * (2 - 2 * flat) * line + flip_y * (2 - 2 * side) * width
+
+
+def count_kernel(place, sources, targets, counts):
+    spheres = counts.shape[0] // 9
+    chunk = counts.shape[1] // spheres
+    for item in range(chunk):
+        at = pl.ds(pl.program_id(0) * chunk + item, 1)
+        source_hot = one_hot(9 * spheres, mirrored(sources[at, :], spheres, place[4], place[5]))
+        target_hot = one_hot(spheres, targets[at, :])
+        counts[:, item * spheres : (item + 1) * spheres] = dot(
+            source_hot.astype(BF16), target_hot.astype(BF16), NT
+        ).astype(BF16)
+
+
+def table_kernel(place, sources, classes, transfer, mie, spread, select, chosen, mie_full):
+    boxes, entries = sources.shape
+    row = lax.broadcasted_iota(jnp.int32, (boxes, boxes), 0)
+    col = lax.broadcasted_iota(jnp.int32, (boxes, boxes), 1)
     unit = jnp.where(row == col, 1.0, 0.0).astype(BF16)
-    select[...] = dot(source_hot, unit, TN).astype(BF16)
-    class_hot = one_hot(transfer.shape[0], classes[...])
-    chosen[...] = dot(class_hot, transfer[...], TN, HIGHEST)
-    mie_full[0] = dot(spread[...], mie[0], precision=HIGHEST)
-    mie_full[1] = dot(spread[...], mie[1], precision=HIGHEST)
+    around = mirrored(sources[...], boxes, place[4], place[5])
+    around = dot(around.astype(F32).astype(BF16), unit, TN)
+    kinds = dot(classes[...].astype(F32).astype(BF16), unit, TN)
+    box_lane = lax.broadcasted_iota(jnp.int32, (entries, select.shape[1]), 1).astype(F32)
+    kind_lane = lax.broadcasted_iota(jnp.int32, (entries, transfer.shape[0]), 1).astype(F32)
+    hots = []
+    for item in range(boxes):
+        at = slice(item * entries, (item + 1) * entries)
+        hots.append(jnp.where(kinds[:, item : item + 1] == kind_lane, 1.0, 0.0))
+        select[at, :] = jnp.where(around[:, item : item + 1] == box_lane, 1.0, 0.0).astype(BF16)
+    hot = jnp.concatenate(hots, axis=0)
+    dirs = transfer.shape[2]
+    chosen[:, :dirs] = dot(hot, transfer[:, 0, :], precision=HIGHEST)
+    chosen[:, dirs:] = dot(hot, transfer[:, 1, :], precision=HIGHEST)
+    mie_full[...] = dot(spread[...], mie[...], precision=HIGHEST)
 
 
 def window_kernel(place, transfer, window, *, near_z, near_x, groups, run, top_x, top_y):
@@ -164,7 +195,7 @@
                 shift = (group - high) * near_z + depth - z
                 keep = (apart_y >= 2) | (jnp.abs(shift) >= 2)
                 for part in range(2):
-                    rows = transfer[part, shift + top_x, pl.ds(start, run), :]
+                    rows = transfer[shift + top_x, pl.ds(start, run), part, :]
                     window[part, z * near_x + x, group * run : (group + 1) * run, :] = jnp.where(
                         keep, rows, 0.0
                     )
@@ -185,11 +216,11 @@
     @pl.when(pl.program_id(0) == 0)
     def _():
         leaves = []
-        for row, part in enumerate((before, own, after)):
-            for col in range(3):
+        for row in range(3):
+            for col, part in enumerate((before, own, after)):
                 place = (row * 3 + col) * spheres
-                columns[:, place : place + spheres] = part[col, : 2 * coefs, :]
-                leaves.append(part[col, 2 * coefs :, :])
+                columns[:, place : place + spheres] = part[row, : 2 * coefs, :]
+                leaves.append(part[row, 2 * coefs :, :])
         around = jnp.concatenate(
             [
                 jnp.concatenate([leaf[:boxes] for leaf in leaves], axis=0),
@@ -216,7 +247,7 @@
 
 
 def arrive(partial, near, leaf_in, receive, cosines, sines, member, leaf_cos, leaf_sin, mie_full):
-    boxes, dirs = leaf_cos.shape
+    _, dirs = leaf_cos.shape
     coefs = near.shape[0] // 2
     column_real = jnp.sum(partial[:, 0, :], axis=0, keepdims=True)
     column_imag = jnp.sum(partial[:, 1, :], axis=0, keepdims=True)
@@ -237,7 +268,7 @@
     half = total.shape[1] // 2
     field_real = total[:coefs, :half] - total[coefs:, half:]
     field_imag = total[coefs:, :half] + total[:coefs, half:]
-    mie_real, mie_imag = mie_full[0], mie_full[1]
+    mie_real, mie_imag = mie_full[:coefs], mie_full[coefs:]
     return jnp.concatenate(
         [
             field_real * mie_real - field_imag * mie_imag,
@@ -252,8 +283,8 @@
     partial,
     near,
     leaf_in,
+    pattern,
     receive,
-    pattern,
     cosines,
     sines,
     box,
@@ -382,11 +413,9 @@
     residual[...] = res_u[0:1] * u + res_d[0:1] * d + res_e[0:1] * e
 
 
-def beside(x, axes):
-    devices = lax.axis_size(axes)
-    up = [(i, i + 1) for i in range(devices - 1)]
-    down = [(j, i) for i, j in up]
-    return lax.ppermute(x, axes, up), lax.ppermute(x, axes, down)
+def swap(x, axes, first):
+    pairs = [(i, i + 1) for i in range(first, lax.axis_size(axes) - 1, 2)]
+    return lax.ppermute(x, axes, pairs + [(j, i) for i, j in pairs])
 
 
 def exchange(x, axes):
@@ -414,7 +443,6 @@
     dirs = pattern.shape[1]
     boxes, entries = far_src.shape[2:]
     classes, pairs = near_src.shape[2:]
-    leaf_classes = leaf_transfer.shape[0]
     high_count, near_z = lax.axis_size("bx_0"), lax.axis_size("bx_1")
     near_x = lax.axis_size("by_0")
     run = lax.axis_size(("by_1", "by_2"))
@@ -425,6 +453,8 @@
             lax.axis_index("bx_1"),
             lax.axis_index("by_0"),
             lax.axis_index(("by_1", "by_2")),
+            lax.axis_index(BX) % 2,
+            lax.axis_index(BY) % 2,
         ]
     ).astype(jnp.int32)
 
@@ -435,79 +465,87 @@
 
     vector = incident.reshape(rows, spheres)
     box = sphere_box.reshape(1, spheres)
-    pattern = pattern.reshape(2 * dirs, coefs)
+    pattern = pattern.transpose(0, 2, 1)
     receive = receive.reshape(rows, dirs)
-    table = near_table.reshape(classes, rows, coefs)
-
-    halo_shape = shape((1, rows + 2 * boxes, spheres), BF16)
-    column_shape = shape((first_count, 2, dirs))
+
+    halo_shape = kept((1, rows + 2 * boxes, spheres), BF16)
+    column_shape = kept((first_count, 2, dirs))
     halo, column, cosines, sines = call(
         first_kernel,
-        (halo_shape, column_shape, shape((dirs, spheres)), shape((dirs, spheres))),
-        (vector, pattern, offsets.reshape(3, spheres), planes, box, leaf_cos, leaf_sin),
-        "first",
+        (halo_shape, column_shape, kept((dirs, spheres)), kept((dirs, spheres))),
+        (vector, pattern, offsets.reshape(3, 1, spheres), planes, box, leaf_cos, leaf_sin),
         flops=1 << 26,
     )
-    counts = call(
-        count_kernel,
-        shape((9 * spheres, classes * spheres), BF16),
-        (near_src.reshape(classes, 1, pairs), near_dst.reshape(classes, 1, pairs)),
-        "counts",
-        flops=1 << 31,
-        grid=(classes,),
-        in_specs=[pl.BlockSpec((1, 1, pairs), lambda k: (k, 0, 0))] * 2,
-        out_specs=pl.BlockSpec((9 * spheres, spheres), lambda k: (0, k)),
-    )
-    select, chosen, mie_full = call(
-        table_kernel,
-        (
-            shape((boxes * entries, 9 * boxes), BF16),
-            shape((boxes * entries, 2 * dirs)),
-            shape((2, coefs, spheres)),
-        ),
-        (
-            far_src.reshape(1, boxes * entries),
-            far_cls.reshape(1, boxes * entries),
-            leaf_transfer.reshape(leaf_classes, 2 * dirs),
-            mie.reshape(2, mie.shape[1], spheres),
-            jnp.asarray(mie_spread(coefs, mie.shape[1])),
-        ),
-        "tables",
-        flops=1 << 28,
-    )
-    window = call(
-        functools.partial(
-            window_kernel,
-            near_z=near_z,
-            near_x=near_x,
-            groups=high_count,
-            run=run,
-            top_x=high_count * near_z - 1,
-            top_y=near_x * run - 1,
-        ),
-        shape((2, second_count, first_count, dirs)),
-        (place, coarse_transfer),
-        "window",
-        flops=1 << 28,
-    )
-
     chunk = 4 if classes % 4 == 0 else 1
+
+    def prepare():
+        counts = call(
+            count_kernel,
+            shape((9 * spheres, classes * spheres), BF16),
+            (place, near_src.reshape(classes, pairs), near_dst.reshape(classes, pairs)),
+            flops=1 << 31,
+            grid=(classes // chunk,),
+            in_specs=[
+                pl.BlockSpec(memory_space=pltpu.SMEM),
+                pl.BlockSpec((classes, pairs), lambda k: (0, 0)),
+                pl.BlockSpec((classes, pairs), lambda k: (0, 0)),
+            ],
+            out_specs=pl.BlockSpec((9 * spheres, chunk * spheres), lambda k: (0, k)),
+        )
+        spread = mie_spread(coefs, mie.shape[1])
+        zero = np.zeros_like(spread)
+        select, chosen, mie_full = call(
+            table_kernel,
+            (
+                shape((boxes * entries, 9 * boxes), BF16),
+                shape((boxes * entries, 2 * dirs)),
+                kept((rows, spheres)),
+            ),
+            (
+                place,
+                far_src.reshape(boxes, entries),
+                far_cls.reshape(boxes, entries),
+                leaf_transfer,
+                mie.reshape(2 * mie.shape[1], spheres),
+                jnp.asarray(np.block([[spread, zero], [zero, spread]])),
+            ),
+            flops=1 << 28,
+        )
+        return counts, select, chosen, mie_full
+
+    def windows():
+        return call(
+            functools.partial(
+                window_kernel,
+                near_z=near_z,
+                near_x=near_x,
+                groups=high_count,
+                run=run,
+                top_x=high_count * near_z - 1,
+                top_y=near_x * run - 1,
+            ),
+            shape((2, second_count, first_count, dirs)),
+            (place, coarse_transfer.transpose(1, 2, 0, 3)),
+            flops=1 << 28,
+        )
+
     whole3 = pl.BlockSpec((3, rows + 2 * boxes, spheres), lambda k: (0, 0, 0))
 
-    def apply(halo, column):
-        before, after = beside(halo, BY)
-        line = jnp.concatenate([before, halo, after], axis=0)
+    def apply(halo, column, window, counts, select, chosen):
         columns = exchange(column, FIRST)
-        up, down = beside(line, BX)
+        ahead = swap(halo, BX, 0)
+        behind = swap(halo, BX, 1)
+        line = jnp.concatenate([behind, halo, ahead], axis=0)
+        right = swap(line, BY, 0)
+        left = swap(line, BY, 1)
         partial = call(
-            coarse_kernel, shape((second_count, 2, dirs)), (columns, window), "coarse", 1 << 24
+            coarse_kernel, kept((second_count, 2, dirs)), (resident(columns), window), 1 << 24
         )
         partial = exchange(partial, SECOND)
         near, leaf_in = call(
             near_kernel,
-            (shape((rows, 2 * spheres)), shape((boxes, 2 * dirs))),
-            (up, line, down, counts, table, select, chosen),
-            "near",
+            (kept((rows, 2 * spheres)), kept((boxes, 2 * dirs))),
+            (left, line, right, counts, near_table.reshape(classes, rows, coefs), select, chosen),
             flops=1 << 31,
             grid=(classes // chunk,),
             in_specs=[
@@ -525,59 +563,32 @@
             ),
             scratch_shapes=[pltpu.VMEM((rows, 9 * spheres), BF16)],
         )
-        return partial, near, leaf_in
-
-    partial, near, leaf_in = apply(halo, column)
+        return resident(partial), near, leaf_in
+
+    window = windows()
+    counts, select, chosen, mie_full = prepare()
+    partial, near, leaf_in = apply(halo, column, window, counts, select, chosen)
+    far = (receive, cosines, sines, box, leaf_cos, leaf_sin, mie_full)
     once, halo, column, sums = call(
         middle_kernel,
-        (shape((rows, spheres)), halo_shape, column_shape, shape((1, 128))),
-        (
-            vector,
-            partial,
-            near,
-            leaf_in,
-            receive,
-            pattern,
-            cosines,
-            sines,
-            box,
-            leaf_cos,
-            leaf_sin,
-            mie_full,
-        ),
-        "middle",
+        (kept((rows, spheres)), halo_shape, column_shape, kept((1, 128))),
+        (vector, partial, near, leaf_in, pattern) + far,
         flops=1 << 26,
     )
-    partial, near, leaf_in = apply(halo, column)
+    partial, near, leaf_in = apply(halo, column, window, counts, select, chosen)
     twice, everyone = call(
         last_kernel,
-        (shape((rows, spheres)), shape((first_count, 1, 128))),
-        (
-            vector,
-            once,
-            partial,
-            near,
-            leaf_in,
-            receive,
-            cosines,
-            sines,
-            box,
-            leaf_cos,
-            leaf_sin,
-            mie_full,
-            sums,
-        ),
-        "last",
+        (kept((rows, spheres)), kept((first_count, 1, 128))),
+        (vector, once, partial, near, leaf_in) + far + (sums,),
         flops=1 << 26,
     )
     everyone = call(
-        relay_kernel, shape((second_count, 1, 128)), (exchange(everyone, FIRST),), "relay", 1 << 20
+        relay_kernel, kept((second_count, 1, 128)), (resident(exchange(everyone, FIRST)),), 1 << 20
     )
     solved, residual = call(
         solve_kernel,
         (shape((rows, spheres)), shape((rows, spheres))),
-        (exchange(everyone, SECOND), vector, once, twice),
-        "solve",
+        (resident(exchange(everyone, SECOND)), vector, once, twice),
         flops=1 << 24,
     )
     return solved.reshape(incident.shape), residual.reshape(incident.shape)

time: 172 us -> 142 us (0.83)
  starting transfers between devices: 63.1 us -> 50.7 us
  Pallas kernels: 41.8 us -> 33.3 us
  local copies, waits for them, and re-layouts: 15.1 us -> 7.19 us
  waiting for transfers between devices: 5.59 us -> 2.85 us
  blocking collectives: 43.5 us -> 46.1 us
    all_to_all x3, starting transfers between devices: 34.2 us -> 23.2 us  [exchange(): return lax.all_to_all(x, axes, split_axis=0, concat_axis=0, tiled=True)]
    pallas_call x12, Pallas kernels: 41.8 us -> 33.3 us  [call(): pl.pallas_call(kernel, out_shape=out_shape, interpret=INTERPRET, cost_est...]
    reshape x5 -> x0, local copies, waits for them, and re-layouts: 4.54 us -> none  [the longest x1 1.33 us: local(): near_src.reshape(classes, 1, pairs)]
    unnamed x37 -> x36, local copies, waits for them, and re-layouts: 10.6 us -> 6.53 us
    all_to_all x3, blocking collectives: 43.5 us -> 46.1 us  [exchange(): return lax.all_to_all(x, axes, split_axis=0, concat_axis=0, tiled=True)]
  transfers between devices with their start and end apart: 11 -> 11, of which waited for: 3 -> 3; matrix products, arithmetic and copies ran while one was open for 5% -> 0% of each run, Pallas kernels for 18% -> 18%
where the time goes in v2:
time: 142 us; the launch traced here: 141 us
  starting transfers between devices  50.7 us (36%)
  blocking collectives  46.1 us (32%)
  Pallas kernels  33.3 us (23%)
  local copies, waits for them, and re-layouts  7.19 us (5%)
  waiting for transfers between devices  2.85 us (2%)
    all_to_all x3, blocking collectives, exchange(): return lax.all_to_all(x, axes, split_axis=0, concat_axis=0, tiled=True)  46.1 us
    pallas_call x12, Pallas kernels, call(): pl.pallas_call(kernel, out_shape=out_shape, interpret=INTERPRET, cost_est...  33.3 us
    ppermute x8, starting transfers between devices, swap(): return lax.ppermute(x, axes, pairs + [(j, i) for i, j in pairs])  27.5 us
    all_to_all x3, starting transfers between devices, exchange(): return lax.all_to_all(x, axes, split_axis=0, concat_axis=0, tiled=True)  23.2 us
    unnamed x36, local copies, waits for them, and re-layouts  6.53 us
  transfers between devices with their start and end apart: 11, of which 3 were waited for; matrix products, arithmetic and copies ran while one was open for 0% of the time, Pallas kernels for 18%

profile of v2, /device:TPU:1, one launch (start us, length us, event | category | flops | bytes accessed | tf_op | source)
XLA Modules:
  0.0 141.0 jit_solution(1194332104378969437)
XLA Ops:
  0.6 2.2 %shard_map.176 = (bf16[1,224,128]{2,1,0:T(8,128)(2,1)S(1)}, f32[16,2,128]{2,1,0:T(2,128)}, f32[128,128]{1,0:T(8,128)S(1)}, f32[128,128]{1,0:T(8,128)S(1)}) custom-call(f32[192,128]{1,0:T(8,128)} %bitcast.25, bf16[2,96,128]{2,1,0:T(8,128)(2,1)} %bitcast.31, f32[3,1,128]{2,1,0:T(1,128)} %bitcast.36, f32[3,128,1]{2,1,0:T(8,128)} %constant.47.clone.planes, ...), custom_call_target="tpu_custom_call" | custom-call | flops 67108864 | bytes 1048576 | tf_op jit(solution)/shard_map/pallas_call | solution.py:34
  2.8 0.7 collective-permute-start
  3.5 8.2 %collective-permute-start.1 = (bf16[1,224,128]{2,1,0:T(8,128)(2,1)S(1)}, bf16[1,224,128]{2,1,0:T(8,128)(2,1)S(1)}, u32[]{:S(2)}, u32[]{:S(2)}) collective-permute-start(bf16[1,224,128]{2,1,0:T(8,128)(2,1)S(1)} %get-tuple-element.22), channel_id=1, source_target_pairs={{0,32},{64,96},{128,160},{192,224},{256,288},{320,352},{384,416},{... | collective-permute-start | bytes 172040 | tf_op jit(solution)/shard_map/ppermute | solution.py:418
  11.7 12.6 %all-to-all-start = ((f32[16,2,128]{2,1,0:T(2,128)}), f32[16,2,128]{2,1,0:T(2,128)S(1)}, u32[]{:S(2)}, u32[]{:S(2)}) async-start(f32[16,2,128]{2,1,0:T(2,128)} %get-tuple-element.21), calls=%async_computation | async-start | bytes 32768 | tf_op jit(solution)/shard_map/all_to_all | solution.py:422
  24.9 2.0 %collective-permute-start.3 = (bf16[3,224,128]{2,1,0:T(8,128)(2,1)S(1)}, bf16[3,224,128]{2,1,0:T(8,128)(2,1)S(1)}, u32[]{:S(2)}, u32[]{:S(2)}) collective-permute-start(bf16[3,224,128]{2,1,0:T(8,128)(2,1)S(1)} %constant_dynamic-update-slice_fusion.own), channel_id=1, source_target_pairs={{0,1},{2,3},{4,5},{6,7},{8,9},{10,11},{12,13},{14,15},{16,17},{18,... | collective-permute-start | bytes 516104 | tf_op jit(solution)/shard_map/ppermute | solution.py:418
  27.0 3.5 %collective-permute-start.2 = (bf16[3,224,128]{2,1,0:T(8,128)(2,1)S(1)}, bf16[3,224,128]{2,1,0:T(8,128)(2,1)S(1)}, u32[]{:S(2)}, u32[]{:S(2)}) collective-permute-start(bf16[3,224,128]{2,1,0:T(8,128)(2,1)S(1)} %constant_dynamic-update-slice_fusion.own), channel_id=1, source_target_pairs={{1,2},{3,4},{5,6},{7,8},{9,10},{11,12},{13,14},{15,16},{17,18},{19... | collective-permute-start | bytes 516104 | tf_op jit(solution)/shard_map/ppermute | solution.py:418
  30.5 5.3 %shard_map.179.counts = bf16[1152,2048]{1,0:T(8,128)(2,1)} custom-call(s32[6]{0:T(128)} %stack.27.place, s32[16,256]{1,0:T(8,128)} %bitcast.41, s32[16,256]{1,0:T(8,128)} %bitcast.42), custom_call_target="tpu_custom_call" | custom-call | flops 2147483648 | bytes 1048576 | tf_op jit(solution)/shard_map/pallas_call | solution.py:34
  35.8 2.7 %shard_map.177.window = f32[2,32,16,128]{3,2,1,0:T(8,128)} custom-call(s32[6]{0:T(128)} %stack.27.place, f32[31,63,2,128]{3,2,1,0:T(2,128)} %bitcast.24), custom_call_target="tpu_custom_call" | custom-call | flops 268435456 | bytes 1048576 | tf_op jit(solution)/shard_map/pallas_call | solution.py:34
  38.5 2.5 %shard_map.180 = (bf16[384,144]{1,0:T(8,128)(2,1)}, f32[384,256]{1,0:T(8,128)}, f32[192,128]{1,0:T(8,128)S(1)}) custom-call(s32[6]{0:T(128)} %stack.27.place, s32[16,24]{1,0:T(8,128)} %bitcast.44, s32[16,24]{1,0:T(8,128)} %bitcast.45, f32[32,2,128]{2,1,0:T(2,128)} %transfer.1, f32[24,128]{1,0:T(8,128)} %bitcast.43, f32[192,24]{1,0:T(8,128)} %constant.50.clone.spread), custom_call_target="tpu_custom_call" | custom-call | flops 268435456 | bytes 1048576 | tf_op jit(solution)/shard_map/pallas_call | solution.py:34
  41.0 0.6 copy-done
  41.7 1.8 %shard_map.178 = f32[32,2,128]{2,1,0:T(2,128)} custom-call(f32[16,2,128]{2,1,0:T(2,128)S(1)} %all-to-all-done.columns, f32[2,32,16,128]{3,2,1,0:T(8,128)} %shard_map.177.window), custom_call_target="tpu_custom_call" | custom-call | flops 16777216 | bytes 1048576 | tf_op jit(solution)/shard_map/pallas_call | solution.py:34
  43.4 6.9 %all-to-all-start.1 = ((f32[32,2,128]{2,1,0:T(2,128)}), f32[32,2,128]{2,1,0:T(2,128)S(1)}, u32[]{:S(2)}, u32[]{:S(2)}) async-start(f32[32,2,128]{2,1,0:T(2,128)} %shard_map.178), calls=%async_computation.1 | async-start | bytes 65536 | tf_op jit(solution)/shard_map/all_to_all | solution.py:422
  51.1 5.7 %shard_map.181 = (f32[192,256]{1,0:T(8,128)S(1)}, f32[16,256]{1,0:T(8,128)S(1)}) custom-call(bf16[3,224,128]{2,1,0:T(8,128)(2,1)} %copy-done.13, bf16[3,224,128]{2,1,0:T(8,128)(2,1)} %copy-done.10, bf16[3,224,128]{2,1,0:T(8,128)(2,1)} %copy-done.12, bf16[1152,2048]{1,0:T(8,128)(2,1)} %shard_map.179.counts, bf16[16,192,96]{2,1,0:T(8,128)(2,1)} %bitcast.37, ...), custom_call_target="tpu_custom_call" | custom-call | flops 2147483648 | bytes 1048576 | tf_op jit(solution)/shard_map/pallas_call | solution.py:34
  56.8 0.7 copy-done.5
  58.0 1.0 all-to-all-done.1.partial
  59.0 2.0 %shard_map.182 = (f32[192,128]{1,0:T(8,128)S(1)}, bf16[1,224,128]{2,1,0:T(8,128)(2,1)S(1)}, f32[16,2,128]{2,1,0:T(2,128)S(1)}, f32[1,128]{1,0:T(1,128)S(1)}) custom-call(f32[192,128]{1,0:T(8,128)} %bitcast.26, f32[32,2,128]{2,1,0:T(2,128)S(1)} %all-to-all-done.1.partial, f32[192,256]{1,0:T(8,128)} %copy-done.5, f32[16,256]{1,0:T(8,128)} %copy-done.8, ...), custom_call_target="tpu_custom_call" | custom-call | flops 67108864 | bytes 1048576 | tf_op jit(solution)/shard_map/pallas_call | solution.py:34
  61.7 0.7 collective-permute-start.4
  62.3 4.6 %collective-permute-start.5 = (bf16[1,224,128]{2,1,0:T(8,128)(2,1)S(1)}, bf16[1,224,128]{2,1,0:T(8,128)(2,1)S(1)}, u32[]{:S(2)}, u32[]{:S(2)}) collective-permute-start(bf16[1,224,128]{2,1,0:T(8,128)(2,1)S(1)} %get-tuple-element.32), channel_id=1, source_target_pairs={{0,32},{64,96},{128,160},{192,224},{256,288},{320,352},{384,416},{... | collective-permute-start | bytes 172040 | tf_op jit(solution)/shard_map/ppermute | solution.py:418
  67.0 1.5 %collective-permute-done.5 = bf16[1,224,128]{2,1,0:T(8,128)(2,1)S(1)} collective-permute-done((bf16[1,224,128]{2,1,0:T(8,128)(2,1)S(1)}, bf16[1,224,128]{2,1,0:T(8,128)(2,1)S(1)}, u32[]{:S(2)}, u32[]{:S(2)}) %collective-permute-start.5) | collective-permute-done | bytes 57376 | tf_op jit(solution)/shard_map/ppermute | solution.py:418
  68.5 5.9 %collective-permute-start.7 = (bf16[3,224,128]{2,1,0:T(8,128)(2,1)S(1)}, bf16[3,224,128]{2,1,0:T(8,128)(2,1)S(1)}, u32[]{:S(2)}, u32[]{:S(2)}) collective-permute-start(bf16[3,224,128]{2,1,0:T(8,128)(2,1)S(1)} %constant_dynamic-update-slice_fusion.3.own), channel_id=1, source_target_pairs={{0,1},{2,3},{4,5},{6,7},{8,9},{10,11},{12,13},{14,15},{16,17},{18,... | collective-permute-start | bytes 516104 | tf_op jit(solution)/shard_map/ppermute | solution.py:418
  74.5 1.9 %collective-permute-start.6 = (bf16[3,224,128]{2,1,0:T(8,128)(2,1)S(1)}, bf16[3,224,128]{2,1,0:T(8,128)(2,1)S(1)}, u32[]{:S(2)}, u32[]{:S(2)}) collective-permute-start(bf16[3,224,128]{2,1,0:T(8,128)(2,1)S(1)} %constant_dynamic-update-slice_fusion.3.own), channel_id=1, source_target_pairs={{1,2},{3,4},{5,6},{7,8},{9,10},{11,12},{13,14},{15,16},{17,18},{19... | collective-permute-start | bytes 516104 | tf_op jit(solution)/shard_map/ppermute | solution.py:418
  76.4 18.4 %all_to_all.30.columns = f32[16,2,128]{2,1,0:T(2,128)S(1)} all-to-all(f32[16,2,128]{2,1,0:T(2,128)S(1)} %get-tuple-element.31), channel_id=1, replica_groups=mesh['bx_0'=2,'bx_1'=8,'by_0'=4,'by_1'=4,'by_2'=2] {'bx_0','by_1','by_2'}, dimensions={0} | all-to-all | bytes 32768 | tf_op jit(solution)/shard_map/all_to_all | solution.py:422
  94.8 1.8 %shard_map.183 = f32[32,2,128]{2,1,0:T(2,128)} custom-call(f32[16,2,128]{2,1,0:T(2,128)S(1)} %all_to_all.30.columns, f32[2,32,16,128]{3,2,1,0:T(8,128)} %shard_map.177.window), custom_call_target="tpu_custom_call" | custom-call | flops 16777216 | bytes 1048576 | tf_op jit(solution)/shard_map/pallas_call | solution.py:34
  96.6 3.8 %all-to-all-start.3 = ((f32[32,2,128]{2,1,0:T(2,128)}), f32[32,2,128]{2,1,0:T(2,128)S(1)}, u32[]{:S(2)}, u32[]{:S(2)}) async-start(f32[32,2,128]{2,1,0:T(2,128)} %shard_map.183), calls=%async_computation.3 | async-start | bytes 65536 | tf_op jit(solution)/shard_map/all_to_all | solution.py:422
  100.5 0.7 copy-done.14
  101.1 0.7 copy-done.15
  101.8 5.7 %shard_map.184 = (f32[192,256]{1,0:T(8,128)S(1)}, f32[16,256]{1,0:T(8,128)S(1)}) custom-call(bf16[3,224,128]{2,1,0:T(8,128)(2,1)} %copy-done.15, bf16[3,224,128]{2,1,0:T(8,128)(2,1)} %copy-done.11, bf16[3,224,128]{2,1,0:T(8,128)(2,1)} %copy-done.14, bf16[1152,2048]{1,0:T(8,128)(2,1)} %shard_map.179.counts, bf16[16,192,96]{2,1,0:T(8,128)(2,1)} %bitcast.38, ...), custom_call_target="tpu_custom_call" | custom-call | flops 2147483648 | bytes 1048576 | tf_op jit(solution)/shard_map/pallas_call | solution.py:34
  107.5 0.7 copy-done.4
  109.1 1.8 %shard_map.185 = (f32[192,128]{1,0:T(8,128)S(1)}, f32[16,1,128]{2,1,0:T(1,128)S(1)}) custom-call(f32[192,128]{1,0:T(8,128)} %bitcast.27, f32[192,128]{1,0:T(8,128)} %copy-done.1, f32[32,2,128]{2,1,0:T(2,128)S(1)} %all-to-all-done.3.partial, f32[192,256]{1,0:T(8,128)} %copy-done.4, f32[16,256]{1,0:T(8,128)} %copy-done.7, bf16[192,128]{1,0:T(8,128)(2,1)} %bitcast.30, ...), custom_call_target="tpu_custom_call" | custom-call | flops 67108864 | bytes 1048576 | tf_op jit(solution)/shard_map/pallas_call | solution.py:34
  111.5 11.3 %all_to_all.31.parts = f32[16,1,128]{2,1,0:T(1,128)S(1)} all-to-all(f32[16,1,128]{2,1,0:T(1,128)S(1)} %get-tuple-element.36), channel_id=1, replica_groups=mesh['bx_0'=2,'bx_1'=8,'by_0'=4,'by_1'=4,'by_2'=2] {'bx_0','by_1','by_2'}, dimensions={0} | all-to-all | bytes 16384 | tf_op jit(solution)/shard_map/all_to_all | solution.py:422
  122.8 16.4 %all_to_all.32.parts = f32[32,1,128]{2,1,0:T(1,128)S(1)} all-to-all(f32[32,1,128]{2,1,0:T(1,128)S(1)} %shard_map.186), channel_id=1, replica_groups=mesh['bx_0'=2,'bx_1'=8,'by_0'=4,'by_1'=4,'by_2'=2] {'bx_1','by_0'}, dimensions={0} | all-to-all | bytes 32768 | tf_op jit(solution)/shard_map/all_to_all | solution.py:422
  139.2 1.8 %shard_map.187 = (f32[192,128]{1,0:T(8,128)}, f32[192,128]{1,0:T(8,128)}) custom-call(f32[32,1,128]{2,1,0:T(1,128)S(1)} %all_to_all.32.parts, f32[192,128]{1,0:T(8,128)} %bitcast.28, f32[192,128]{1,0:T(8,128)} %copy-done.1, f32[192,128]{1,0:T(8,128)} %copy-done.6), custom_call_target="tpu_custom_call" | custom-call | flops 16777216 | bytes 1048576 | tf_op jit(solution)/shard_map/pallas_call | solution.py:34
  (44 shorter events, 4.3 us)
Async XLA Ops:
  2.8 35.7 %copy-start.2 = (f32[128,128]{1,0:T(8,128)}, f32[128,128]{1,0:T(8,128)S(1)}, u32[]{:S(2)}) copy-start(f32[128,128]{1,0:T(8,128)S(1)} %get-tuple-element.27.cosines) | copy-start | bytes 196612
  2.8 35.7 %copy-start.3 = (f32[128,128]{1,0:T(8,128)}, f32[128,128]{1,0:T(8,128)S(1)}, u32[]{:S(2)}) copy-start(f32[128,128]{1,0:T(8,128)S(1)} %get-tuple-element.28.sines) | copy-start | bytes 196612
  2.8 22.0 %collective-permute-start = (bf16[1,224,128]{2,1,0:T(8,128)(2,1)S(1)}, bf16[1,224,128]{2,1,0:T(8,128)(2,1)S(1)}, u32[]{:S(2)}, u32[]{:S(2)}) collective-permute-start(bf16[1,224,128]{2,1,0:T(8,128)(2,1)S(1)} %get-tuple-element.22), channel_id=1, source_target_pairs={{32,64},{96,128},{160,192},{224,256},{288,320},{352,384},{416,448}... | collective-permute-start | bytes 172040 | tf_op jit(solution)/shard_map/ppermute | solution.py:418
  3.5 21.4 %collective-permute-start.1 = (bf16[1,224,128]{2,1,0:T(8,128)(2,1)S(1)}, bf16[1,224,128]{2,1,0:T(8,128)(2,1)S(1)}, u32[]{:S(2)}, u32[]{:S(2)}) collective-permute-start(bf16[1,224,128]{2,1,0:T(8,128)(2,1)S(1)} %get-tuple-element.22), channel_id=1, source_target_pairs={{0,32},{64,96},{128,160},{192,224},{256,288},{320,352},{384,416},{... | collective-permute-start | bytes 172040 | tf_op jit(solution)/shard_map/ppermute | solution.py:418
  11.7 30.0 %all-to-all-start = ((f32[16,2,128]{2,1,0:T(2,128)}), f32[16,2,128]{2,1,0:T(2,128)S(1)}, u32[]{:S(2)}, u32[]{:S(2)}) async-start(f32[16,2,128]{2,1,0:T(2,128)} %get-tuple-element.21), calls=%async_computation | async-start | bytes 32768 | tf_op jit(solution)/shard_map/all_to_all | solution.py:422
  24.9 13.6 %copy-start.10 = (bf16[3,224,128]{2,1,0:T(8,128)(2,1)}, bf16[3,224,128]{2,1,0:T(8,128)(2,1)S(1)}, u32[]{:S(2)}) copy-start(bf16[3,224,128]{2,1,0:T(8,128)(2,1)S(1)} %constant_dynamic-update-slice_fusion.own) | copy-start | bytes 516100
  24.9 25.4 %collective-permute-start.3 = (bf16[3,224,128]{2,1,0:T(8,128)(2,1)S(1)}, bf16[3,224,128]{2,1,0:T(8,128)(2,1)S(1)}, u32[]{:S(2)}, u32[]{:S(2)}) collective-permute-start(bf16[3,224,128]{2,1,0:T(8,128)(2,1)S(1)} %constant_dynamic-update-slice_fusion.own), channel_id=1, source_target_pairs={{0,1},{2,3},{4,5},{6,7},{8,9},{10,11},{12,13},{14,15},{16,17},{18,... | collective-permute-start | bytes 516104 | tf_op jit(solution)/shard_map/ppermute | solution.py:418
  27.0 23.4 %collective-permute-start.2 = (bf16[3,224,128]{2,1,0:T(8,128)(2,1)S(1)}, bf16[3,224,128]{2,1,0:T(8,128)(2,1)S(1)}, u32[]{:S(2)}, u32[]{:S(2)}) collective-permute-start(bf16[3,224,128]{2,1,0:T(8,128)(2,1)S(1)} %constant_dynamic-update-slice_fusion.own), channel_id=1, source_target_pairs={{1,2},{3,4},{5,6},{7,8},{9,10},{11,12},{13,14},{15,16},{17,18},{19... | collective-permute-start | bytes 516104 | tf_op jit(solution)/shard_map/ppermute | solution.py:418
  41.0 0.6 copy-start
  43.4 15.5 %all-to-all-start.1 = ((f32[32,2,128]{2,1,0:T(2,128)}), f32[32,2,128]{2,1,0:T(2,128)S(1)}, u32[]{:S(2)}, u32[]{:S(2)}) async-start(f32[32,2,128]{2,1,0:T(2,128)} %shard_map.178), calls=%async_computation.1 | async-start | bytes 65536 | tf_op jit(solution)/shard_map/all_to_all | solution.py:422
  50.3 0.7 copy-start.12
  50.3 0.7 copy-start.13
  56.7 0.7 copy-start.5
  57.4 0.6 copy-start.8
  61.0 0.6 copy-start.1
  61.7 14.7 %copy-start.9 = (f32[1,128]{1,0:T(1,128)}, f32[1,128]{1,0:T(1,128)S(1)}, u32[]{:S(2)}) copy-start(f32[1,128]{1,0:T(1,128)S(1)} %get-tuple-element.35.sums) | copy-start | bytes 1540
  61.7 5.3 %collective-permute-start.4 = (bf16[1,224,128]{2,1,0:T(8,128)(2,1)S(1)}, bf16[1,224,128]{2,1,0:T(8,128)(2,1)S(1)}, u32[]{:S(2)}, u32[]{:S(2)}) collective-permute-start(bf16[1,224,128]{2,1,0:T(8,128)(2,1)S(1)} %get-tuple-element.32), channel_id=1, source_target_pairs={{32,64},{96,128},{160,192},{224,256},{288,320},{352,384},{416,448}... | collective-permute-start | bytes 172040 | tf_op jit(solution)/shard_map/ppermute | solution.py:418
  62.3 6.1 %collective-permute-start.5 = (bf16[1,224,128]{2,1,0:T(8,128)(2,1)S(1)}, bf16[1,224,128]{2,1,0:T(8,128)(2,1)S(1)}, u32[]{:S(2)}, u32[]{:S(2)}) collective-permute-start(bf16[1,224,128]{2,1,0:T(8,128)(2,1)S(1)} %get-tuple-element.32), channel_id=1, source_target_pairs={{0,32},{64,96},{128,160},{192,224},{256,288},{320,352},{384,416},{... | collective-permute-start | bytes 172040 | tf_op jit(solution)/shard_map/ppermute | solution.py:418
  68.5 32.0 %copy-start.11 = (bf16[3,224,128]{2,1,0:T(8,128)(2,1)}, bf16[3,224,128]{2,1,0:T(8,128)(2,1)S(1)}, u32[]{:S(2)}) copy-start(bf16[3,224,128]{2,1,0:T(8,128)(2,1)S(1)} %constant_dynamic-update-slice_fusion.3.own) | copy-start | bytes 516100
  68.5 31.9 %collective-permute-start.7 = (bf16[3,224,128]{2,1,0:T(8,128)(2,1)S(1)}, bf16[3,224,128]{2,1,0:T(8,128)(2,1)S(1)}, u32[]{:S(2)}, u32[]{:S(2)}) collective-permute-start(bf16[3,224,128]{2,1,0:T(8,128)(2,1)S(1)} %constant_dynamic-update-slice_fusion.3.own), channel_id=1, source_target_pairs={{0,1},{2,3},{4,5},{6,7},{8,9},{10,11},{12,13},{14,15},{16,17},{18,... | collective-permute-start | bytes 516104 | tf_op jit(solution)/shard_map/ppermute | solution.py:418
  74.5 26.0 %collective-permute-start.6 = (bf16[3,224,128]{2,1,0:T(8,128)(2,1)S(1)}, bf16[3,224,128]{2,1,0:T(8,128)(2,1)S(1)}, u32[]{:S(2)}, u32[]{:S(2)}) collective-permute-start(bf16[3,224,128]{2,1,0:T(8,128)(2,1)S(1)} %constant_dynamic-update-slice_fusion.3.own), channel_id=1, source_target_pairs={{1,2},{3,4},{5,6},{7,8},{9,10},{11,12},{13,14},{15,16},{17,18},{19... | collective-permute-start | bytes 516104 | tf_op jit(solution)/shard_map/ppermute | solution.py:418
  96.6 12.5 %all-to-all-start.3 = ((f32[32,2,128]{2,1,0:T(2,128)}), f32[32,2,128]{2,1,0:T(2,128)S(1)}, u32[]{:S(2)}, u32[]{:S(2)}) async-start(f32[32,2,128]{2,1,0:T(2,128)} %shard_map.183), calls=%async_computation.3 | async-start | bytes 65536 | tf_op jit(solution)/shard_map/all_to_all | solution.py:422
  100.4 0.7 copy-start.14
  101.1 0.7 copy-start.15
  107.5 0.7 copy-start.4
  108.1 0.6 copy-start.7
  110.9 0.6 copy-start.6

commit v3 on v2

--- a/solution.py
+++ b/solution.py
@@ -98,9 +98,8 @@
     boxes, dirs = leaf_cos.shape
     rounded = vector.astype(BF16)
     halo_ref[0, : 2 * coefs, :] = rounded
-    both = jnp.concatenate([pattern[0], pattern[1]], axis=1)
-    by_real = dot(both, rounded[:coefs], TN)
-    by_imag = dot(both, rounded[coefs:], TN)
+    by_real = dot(pattern, rounded[:coefs])
+    by_imag = dot(pattern, rounded[coefs:])
     real = by_real[:dirs] - by_imag[dirs:]
     imag = by_real[dirs:] + by_imag[:dirs]
     out = jnp.concatenate([real * cosines + imag * sines, imag * cosines - real * sines], axis=0)
@@ -128,8 +127,10 @@
 
 
 def first_kernel(
-    vector, pattern, offsets, planes, box, leaf_cos, leaf_sin, halo, column, cos_ref, sin_ref
+    vector, pattern, offsets, planes, box, leaf_cos, leaf_sin, halo, column, cos_ref, sin_ref, send
 ):
+    turned = jnp.concatenate([pattern[0].T, pattern[1].T], axis=0)
+    send[...] = turned
     phases = KAPPA * (
         planes[0] * offsets[0] + planes[1] * offsets[1] + planes[2] * offsets[2]
     )
@@ -137,9 +138,7 @@
     cos_ref[...] = cosines
     sin_ref[...] = sines
     member = one_hot(leaf_cos.shape[0], box[...]).astype(BF16)
-    emit(
-        vector[...], pattern[...], cosines, sines, member, leaf_cos[...], leaf_sin[...], halo, column
-    )
+    emit(vector[...], turned, cosines, sines, member, leaf_cos[...], leaf_sin[...], halo, column)
 
 
 def mirrored(sources, width, flip_x, flip_y):
@@ -150,24 +149,45 @@
     return sources + flip_x * (2 - 2 * flat) * line + flip_y * (2 - 2 * side) * width
 
 
-def count_kernel(place, sources, targets, counts):
+def count_kernel(
+    index,
+    sources,
+    targets,
+    far_sources,
+    kinds,
+    transfer,
+    mie,
+    spread,
+    counts,
+    select,
+    chosen,
+    mie_full,
+    *,
+    across_y,
+):
+    flips = lax.rem(lax.div(index[0], across_y), 2), lax.rem(index[0], 2)
+
+    @pl.when(pl.program_id(0) == 0)
+    def _():
+        fill_tables(flips, far_sources, kinds, transfer, mie, spread, select, chosen, mie_full)
+
     spheres = counts.shape[0] // 9
     chunk = counts.shape[1] // spheres
     for item in range(chunk):
         at = pl.ds(pl.program_id(0) * chunk + item, 1)
-        source_hot = one_hot(9 * spheres, mirrored(sources[at, :], spheres, place[4], place[5]))
+        source_hot = one_hot(9 * spheres, mirrored(sources[at, :], spheres, *flips))
         target_hot = one_hot(spheres, targets[at, :])
         counts[:, item * spheres : (item + 1) * spheres] = dot(
             source_hot.astype(BF16), target_hot.astype(BF16), NT
         ).astype(BF16)
 
 
-def table_kernel(place, sources, classes, transfer, mie, spread, select, chosen, mie_full):
+def fill_tables(flips, sources, classes, transfer, mie, spread, select, chosen, mie_full):
     boxes, entries = sources.shape
     row = lax.broadcasted_iota(jnp.int32, (boxes, boxes), 0)
     col = lax.broadcasted_iota(jnp.int32, (boxes, boxes), 1)
     unit = jnp.where(row == col, 1.0, 0.0).astype(BF16)
-    around = mirrored(sources[...], boxes, place[4], place[5])
+    around = mirrored(sources[...], boxes, *flips)
     around = dot(around.astype(F32).astype(BF16), unit, TN)
     kinds = dot(classes[...].astype(F32).astype(BF16), unit, TN)
     box_lane = lax.broadcasted_iota(jnp.int32, (entries, select.shape[1]), 1).astype(F32)
@@ -184,8 +204,10 @@
     mie_full[...] = dot(spread[...], mie[...], precision=HIGHEST)
 
 
-def window_kernel(place, transfer, window, *, near_z, near_x, groups, run, top_x, top_y):
-    high, depth, across, lane = (place[i] for i in range(4))
+def window_kernel(index, transfer, window, *, near_z, near_x, groups, run, top_x, top_y):
+    row, col = lax.div(index[0], near_x * run), lax.rem(index[0], near_x * run)
+    high, depth = lax.div(row, near_z), lax.rem(row, near_z)
+    across, lane = lax.div(col, run), lax.rem(col, run)
     ordinal = lax.broadcasted_iota(jnp.int32, (run, 128), 0)
     for z in range(near_z):
         for x in range(near_x):
@@ -278,8 +300,12 @@
     )
 
 
+def sums_kernel(vector, scattered, sums):
+    u, d = vector[...], scattered[...]
+    sums[...] = lanes([(0, inner(u, u)), (1, inner(u, d)), (2, inner(d, d))])
+
+
 def middle_kernel(
-    vector,
     partial,
     near,
     leaf_in,
@@ -294,7 +320,6 @@
     applied,
     halo,
     column,
-    sums,
 ):
     member = one_hot(leaf_cos.shape[0], box[...]).astype(BF16)
     scattered = arrive(
@@ -320,10 +345,6 @@
         leaf_sin[...],
         halo,
         column,
-    )
-    start = vector[...]
-    sums[...] = lanes(
-        [(0, inner(start, start)), (1, inner(start, scattered)), (2, inner(scattered, scattered))]
     )
 
 
@@ -447,16 +468,7 @@
     near_x = lax.axis_size("by_0")
     run = lax.axis_size(("by_1", "by_2"))
     first_count, second_count = lax.axis_size(FIRST), lax.axis_size(SECOND)
-    place = jnp.stack(
-        [
-            lax.axis_index("bx_0"),
-            lax.axis_index("bx_1"),
-            lax.axis_index("by_0"),
-            lax.axis_index(("by_1", "by_2")),
-            lax.axis_index(BX) % 2,
-            lax.axis_index(BY) % 2,
-        ]
-    ).astype(jnp.int32)
+    index = lax.axis_index(BX + BY).astype(jnp.int32).reshape(1)
 
     planes = jnp.asarray(directions(dirs)[:, :, None].astype(np.float32))
     centre = KAPPA * (leaf_centers(boxes).T @ directions(dirs))
@@ -470,48 +482,52 @@
 
     halo_shape = kept((1, rows + 2 * boxes, spheres), BF16)
     column_shape = kept((first_count, 2, dirs))
-    halo, column, cosines, sines = call(
+    halo, column, cosines, sines, send = call(
         first_kernel,
-        (halo_shape, column_shape, kept((dirs, spheres)), kept((dirs, spheres))),
+        (
+            halo_shape,
+            column_shape,
+            kept((dirs, spheres)),
+            kept((dirs, spheres)),
+            kept((2 * dirs, coefs), BF16),
+        ),
         (vector, pattern, offsets.reshape(3, 1, spheres), planes, box, leaf_cos, leaf_sin),
         flops=1 << 26,
     )
-    chunk = 4 if classes % 4 == 0 else 1
+    chunk = classes // 2
+    whole = pl.BlockSpec(memory_space=pltpu.VMEM)
 
     def prepare():
-        counts = call(
-            count_kernel,
-            shape((9 * spheres, classes * spheres), BF16),
-            (place, near_src.reshape(classes, pairs), near_dst.reshape(classes, pairs)),
-            flops=1 << 31,
-            grid=(classes // chunk,),
-            in_specs=[
-                pl.BlockSpec(memory_space=pltpu.SMEM),
-                pl.BlockSpec((classes, pairs), lambda k: (0, 0)),
-                pl.BlockSpec((classes, pairs), lambda k: (0, 0)),
-            ],
-            out_specs=pl.BlockSpec((9 * spheres, chunk * spheres), lambda k: (0, k)),
-        )
         spread = mie_spread(coefs, mie.shape[1])
         zero = np.zeros_like(spread)
-        select, chosen, mie_full = call(
-            table_kernel,
+        return call(
+            functools.partial(count_kernel, across_y=near_x * run),
             (
-                shape((boxes * entries, 9 * boxes), BF16),
-                shape((boxes * entries, 2 * dirs)),
+                shape((9 * spheres, classes * spheres), BF16),
+                kept((boxes * entries, 9 * boxes), BF16),
+                kept((boxes * entries, 2 * dirs)),
                 kept((rows, spheres)),
             ),
             (
-                place,
+                index,
+                near_src.reshape(classes, pairs),
+                near_dst.reshape(classes, pairs),
                 far_src.reshape(boxes, entries),
                 far_cls.reshape(boxes, entries),
                 leaf_transfer,
                 mie.reshape(2 * mie.shape[1], spheres),
                 jnp.asarray(np.block([[spread, zero], [zero, spread]])),
             ),
-            flops=1 << 28,
+            flops=1 << 31,
+            grid=(classes // chunk,),
+            in_specs=[pl.BlockSpec(memory_space=pltpu.SMEM)] + [whole] * 7,
+            out_specs=(
+                pl.BlockSpec((9 * spheres, chunk * spheres), lambda k: (0, k)),
+                whole,
+                whole,
+                whole,
+            ),
         )
-        return counts, select, chosen, mie_full
 
     def windows():
         return call(
@@ -524,12 +540,10 @@
                 top_x=high_count * near_z - 1,
                 top_y=near_x * run - 1,
             ),
-            shape((2, second_count, first_count, dirs)),
-            (place, coarse_transfer.transpose(1, 2, 0, 3)),
+            kept((2, second_count, first_count, dirs)),
+            (index, coarse_transfer.transpose(1, 2, 0, 3)),
             flops=1 << 28,
         )
-
-    whole3 = pl.BlockSpec((3, rows + 2 * boxes, spheres), lambda k: (0, 0, 0))
 
     def apply(halo, column, window, counts, select, chosen):
         columns = exchange(column, FIRST)
@@ -539,47 +553,65 @@
         right = swap(line, BY, 0)
         left = swap(line, BY, 1)
         partial = call(
-            coarse_kernel, kept((second_count, 2, dirs)), (resident(columns), window), 1 << 24
+            coarse_kernel,
+            kept((second_count, 2, dirs)),
+            (resident(columns), resident(window)),
+            1 << 24,
         )
         partial = exchange(partial, SECOND)
         near, leaf_in = call(
             near_kernel,
             (kept((rows, 2 * spheres)), kept((boxes, 2 * dirs))),
-            (left, line, right, counts, near_table.reshape(classes, rows, coefs), select, chosen),
+            (
+                resident(left),
+                resident(line),
+                resident(right),
+                counts,
+                near_table.reshape(classes, rows, coefs),
+                resident(select),
+                resident(chosen),
+            ),
             flops=1 << 31,
             grid=(classes // chunk,),
             in_specs=[
-                whole3,
-                whole3,
-                whole3,
+                whole,
+                whole,
+                whole,
                 pl.BlockSpec((9 * spheres, chunk * spheres), lambda k: (0, k)),
                 pl.BlockSpec((chunk, rows, coefs), lambda k: (k, 0, 0)),
-                pl.BlockSpec((boxes * entries, 9 * boxes), lambda k: (0, 0)),
-                pl.BlockSpec((boxes * entries, 2 * dirs), lambda k: (0, 0)),
+                whole,
+                whole,
             ],
-            out_specs=(
-                pl.BlockSpec((rows, 2 * spheres), lambda k: (0, 0)),
-                pl.BlockSpec((boxes, 2 * dirs), lambda k: (0, 0)),
-            ),
+            out_specs=(whole, whole),
             scratch_shapes=[pltpu.VMEM((rows, 9 * spheres), BF16)],
         )
-        return resident(partial), near, leaf_in
+        return resident(partial), resident(near), resident(leaf_in)
 
     window = windows()
     counts, select, chosen, mie_full = prepare()
     partial, near, leaf_in = apply(halo, column, window, counts, select, chosen)
-    far = (receive, cosines, sines, box, leaf_cos, leaf_sin, mie_full)
-    once, halo, column, sums = call(
+    far = (
+        receive,
+        resident(cosines),
+        resident(sines),
+        box,
+        leaf_cos,
+        leaf_sin,
+        resident(mie_full),
+    )
+    once, halo, column = call(
         middle_kernel,
-        (kept((rows, spheres)), halo_shape, column_shape, kept((1, 128))),
-        (vector, partial, near, leaf_in, pattern) + far,
+        (kept((rows, spheres)), halo_shape, column_shape),
+        (partial, near, leaf_in, resident(send)) + far,
         flops=1 << 26,
     )
+    sums = call(sums_kernel, kept((1, 128)), (vector, resident(once)), 1 << 24)
     partial, near, leaf_in = apply(halo, column, window, counts, select, chosen)
+    once = resident(once)
     twice, everyone = call(
         last_kernel,
         (kept((rows, spheres)), kept((first_count, 1, 128))),
-        (vector, once, partial, near, leaf_in) + far + (sums,),
+        (vector, once, partial, near, leaf_in) + far + (resident(sums),),
         flops=1 << 26,
     )
     everyone = call(
@@ -588,7 +620,7 @@
     solved, residual = call(
         solve_kernel,
         (shape((rows, spheres)), shape((rows, spheres))),
-        (resident(exchange(everyone, SECOND)), vector, once, twice),
+        (resident(exchange(everyone, SECOND)), vector, once, resident(twice)),
         flops=1 << 24,
     )
     return solved.reshape(incident.shape), residual.reshape(incident.shape)

time: 142 us -> 131 us (0.923)
  blocking collectives: 46.1 us -> 23.4 us
  waiting for transfers between devices: 2.85 us -> 16.7 us
  starting transfers between devices: 50.7 us -> 62 us
  local copies, waits for them, and re-layouts: 7.19 us -> 0.06 us
  Pallas kernels: 33.3 us -> 26.8 us
    all_to_all x3 -> x2, blocking collectives: 46.1 us -> 23.4 us  [exchange(): return lax.all_to_all(x, axes, split_axis=0, concat_axis=0, tiled=True)]
    all_to_all x3 -> x4, waiting for transfers between devices: 1.32 us -> 15.2 us  [exchange(): return lax.all_to_all(x, axes, split_axis=0, concat_axis=0, tiled=True)]
    all_to_all x3 -> x4, starting transfers between devices: 23.2 us -> 34.5 us  [exchange(): return lax.all_to_all(x, axes, split_axis=0, concat_axis=0, tiled=True)]
    unnamed x36 -> x4, local copies, waits for them, and re-layouts: 6.53 us -> 0.04 us
    pallas_call x12, Pallas kernels: 33.3 us -> 26.8 us  [call(): pl.pallas_call(kernel, out_shape=out_shape, interpret=INTERPRET, cost_est...]
  transfers between devices with their start and end apart: 11 -> 12, of which waited for: 3 -> 4; matrix products, arithmetic and copies ran while one was open for 0% -> 0% of each run, Pallas kernels for 18% -> 15%
where the time goes in v3:
time: 131 us; the launch traced here: 130 us
  starting transfers between devices  62 us (47%)
  Pallas kernels  26.8 us (20%)
  blocking collectives  23.4 us (18%)
  waiting for transfers between devices  16.7 us (13%)
    all_to_all x4, starting transfers between devices, exchange(): return lax.all_to_all(x, axes, split_axis=0, concat_axis=0, tiled=True)  34.5 us
    ppermute x8, starting transfers between devices, swap(): return lax.ppermute(x, axes, pairs + [(j, i) for i, j in pairs])  27.5 us
    pallas_call x12, Pallas kernels, call(): pl.pallas_call(kernel, out_shape=out_shape, interpret=INTERPRET, cost_est...  26.8 us
    all_to_all x2, blocking collectives, exchange(): return lax.all_to_all(x, axes, split_axis=0, concat_axis=0, tiled=True)  23.4 us
    all_to_all x4, waiting for transfers between devices, exchange(): return lax.all_to_all(x, axes, split_axis=0, concat_axis=0, tiled=True)  15.2 us
  transfers between devices with their start and end apart: 12, of which 4 were waited for; matrix products, arithmetic and copies ran while one was open for 0% of the time, Pallas kernels for 15%

profile of v3, /device:TPU:1, one launch (start us, length us, event | category | flops | bytes accessed | tf_op | source)
XLA Modules:
  0.0 129.8 jit_solution(17770930296723272767)
XLA Ops:
  0.6 2.2 %shard_map.176 = (bf16[1,224,128]{2,1,0:T(8,128)(2,1)S(1)}, f32[16,2,128]{2,1,0:T(2,128)}, f32[128,128]{1,0:T(8,128)S(1)}, f32[128,128]{1,0:T(8,128)S(1)}, bf16[256,96]{1,0:T(8,128)(2,1)S(1)}) custom-call(f32[192,128]{1,0:T(8,128)} %bitcast.20, bf16[2,96,128]{2,1,0:T(8,128)(2,1)} %bitcast.26, f32[3,1,128]{2,1,0:T(1,128)} %bitcast.30, ...), custom_call_target="tpu_custom_call" | custom-call | flops 67108864 | bytes 1048576 | tf_op jit(solution)/shard_map/pallas_call | solution.py:34
  2.8 0.7 collective-permute-start
  3.5 8.2 %collective-permute-start.1 = (bf16[1,224,128]{2,1,0:T(8,128)(2,1)S(1)}, bf16[1,224,128]{2,1,0:T(8,128)(2,1)S(1)}, u32[]{:S(2)}, u32[]{:S(2)}) collective-permute-start(bf16[1,224,128]{2,1,0:T(8,128)(2,1)S(1)} %get-tuple-element.23), channel_id=1, source_target_pairs={{0,32},{64,96},{128,160},{192,224},{256,288},{320,352},{384,416},{... | collective-permute-start | bytes 172040 | tf_op jit(solution)/shard_map/ppermute | solution.py:439
  11.7 12.6 %all-to-all-start = ((f32[16,2,128]{2,1,0:T(2,128)}), f32[16,2,128]{2,1,0:T(2,128)S(1)}, u32[]{:S(2)}, u32[]{:S(2)}) async-start(f32[16,2,128]{2,1,0:T(2,128)} %get-tuple-element.22), calls=%async_computation | async-start | bytes 32768 | tf_op jit(solution)/shard_map/all_to_all | solution.py:443
  24.2 0.0 collective-permute-done
  24.3 2.0 %collective-permute-start.3 = (bf16[3,224,128]{2,1,0:T(8,128)(2,1)S(1)}, bf16[3,224,128]{2,1,0:T(8,128)(2,1)S(1)}, u32[]{:S(2)}, u32[]{:S(2)}) collective-permute-start(bf16[3,224,128]{2,1,0:T(8,128)(2,1)S(1)} %constant_dynamic-update-slice_fusion.own), channel_id=1, source_target_pairs={{0,1},{2,3},{4,5},{6,7},{8,9},{10,11},{12,13},{14,15},{16,17},{18,... | collective-permute-start | bytes 516104 | tf_op jit(solution)/shard_map/ppermute | solution.py:439
  26.3 3.5 %collective-permute-start.2 = (bf16[3,224,128]{2,1,0:T(8,128)(2,1)S(1)}, bf16[3,224,128]{2,1,0:T(8,128)(2,1)S(1)}, u32[]{:S(2)}, u32[]{:S(2)}) collective-permute-start(bf16[3,224,128]{2,1,0:T(8,128)(2,1)S(1)} %constant_dynamic-update-slice_fusion.own), channel_id=1, source_target_pairs={{1,2},{3,4},{5,6},{7,8},{9,10},{11,12},{13,14},{15,16},{17,18},{19... | collective-permute-start | bytes 516104 | tf_op jit(solution)/shard_map/ppermute | solution.py:439
  29.9 6.2 %shard_map.179 = (bf16[1152,2048]{1,0:T(8,128)(2,1)}, bf16[384,144]{1,0:T(8,128)(2,1)S(1)}, f32[384,256]{1,0:T(8,128)S(1)}, f32[192,128]{1,0:T(8,128)S(1)}) custom-call(s32[1]{0:T(128)} %bitcast.4.index, s32[16,256]{1,0:T(8,128)} %bitcast.35, s32[16,256]{1,0:T(8,128)} %bitcast.36, s32[16,24]{1,0:T(8,128)} %bitcast.38, s32[16,24]{1,0:T(8,128)} %bitcast.39, ...), custom_call_target="tpu_custom_call" | custom-call | flops 2147483648 | bytes 1048576 | tf_op jit(solution)/shard_map/pallas_call | solution.py:34
  36.0 1.9 %shard_map.177.window = f32[2,32,16,128]{3,2,1,0:T(8,128)S(1)} custom-call(s32[1]{0:T(128)} %bitcast.4.index, f32[31,63,2,128]{3,2,1,0:T(2,128)} %bitcast.19), custom_call_target="tpu_custom_call" | custom-call | flops 268435456 | bytes 1048576 | tf_op jit(solution)/shard_map/pallas_call | solution.py:34
  37.9 0.0 all-to-all-done.columns
  37.9 0.7 shard_map.178
  38.6 6.9 %all-to-all-start.1 = ((f32[32,2,128]{2,1,0:T(2,128)}), f32[32,2,128]{2,1,0:T(2,128)S(1)}, u32[]{:S(2)}, u32[]{:S(2)}) async-start(f32[32,2,128]{2,1,0:T(2,128)} %shard_map.178), calls=%async_computation.1 | async-start | bytes 65536 | tf_op jit(solution)/shard_map/all_to_all | solution.py:443
  45.5 0.0 collective-permute-done.3.after
  45.5 4.3 %shard_map.180 = (f32[192,256]{1,0:T(8,128)S(1)}, f32[16,256]{1,0:T(8,128)S(1)}) custom-call(bf16[3,224,128]{2,1,0:T(8,128)(2,1)S(1)} %collective-permute-done.2.before, bf16[3,224,128]{2,1,0:T(8,128)(2,1)S(1)} %constant_dynamic-update-slice_fusion.own, bf16[3,224,128]{2,1,0:T(8,128)(2,1)S(1)} %collective-permute-done.3.after, ...), custom_call_target="tpu_custom_call" | custom-call | flops 2147483648 | bytes 1048576 | tf_op jit(solution)/shard_map/pallas_call | solution.py:34
  49.8 4.4 %all-to-all-done.1.partial = f32[32,2,128]{2,1,0:T(2,128)S(1)} async-done(((f32[32,2,128]{2,1,0:T(2,128)}), f32[32,2,128]{2,1,0:T(2,128)S(1)}, u32[]{:S(2)}, u32[]{:S(2)}) %all-to-all-start.1) | async-done | bytes 32800 | tf_op jit(solution)/shard_map/all_to_all | solution.py:443
  54.2 2.3 %shard_map.181 = (f32[192,128]{1,0:T(8,128)S(1)}, bf16[1,224,128]{2,1,0:T(8,128)(2,1)S(1)}, f32[16,2,128]{2,1,0:T(2,128)}) custom-call(f32[32,2,128]{2,1,0:T(2,128)S(1)} %all-to-all-done.1.partial, f32[192,256]{1,0:T(8,128)S(1)} %get-tuple-element.27.near, f32[16,256]{1,0:T(8,128)S(1)} %get-tuple-element.28.leaf_in, ...), custom_call_target="tpu_custom_call" | custom-call | flops 67108864 | bytes 1048576 | tf_op jit(solution)/shard_map/pallas_call | solution.py:34
  56.5 0.7 collective-permute-start.4
  57.1 3.9 %collective-permute-start.5 = (bf16[1,224,128]{2,1,0:T(8,128)(2,1)S(1)}, bf16[1,224,128]{2,1,0:T(8,128)(2,1)S(1)}, u32[]{:S(2)}, u32[]{:S(2)}) collective-permute-start(bf16[1,224,128]{2,1,0:T(8,128)(2,1)S(1)} %get-tuple-element.35), channel_id=1, source_target_pairs={{0,32},{64,96},{128,160},{192,224},{256,288},{320,352},{384,416},{... | collective-permute-start | bytes 172040 | tf_op jit(solution)/shard_map/ppermute | solution.py:439
  61.0 1.5 %collective-permute-done.5 = bf16[1,224,128]{2,1,0:T(8,128)(2,1)S(1)} collective-permute-done((bf16[1,224,128]{2,1,0:T(8,128)(2,1)S(1)}, bf16[1,224,128]{2,1,0:T(8,128)(2,1)S(1)}, u32[]{:S(2)}, u32[]{:S(2)}) %collective-permute-start.5) | collective-permute-done | bytes 57376 | tf_op jit(solution)/shard_map/ppermute | solution.py:439
  62.6 6.7 %collective-permute-start.7 = (bf16[3,224,128]{2,1,0:T(8,128)(2,1)S(1)}, bf16[3,224,128]{2,1,0:T(8,128)(2,1)S(1)}, u32[]{:S(2)}, u32[]{:S(2)}) collective-permute-start(bf16[3,224,128]{2,1,0:T(8,128)(2,1)S(1)} %constant_dynamic-update-slice_fusion.3.own), channel_id=1, source_target_pairs={{0,1},{2,3},{4,5},{6,7},{8,9},{10,11},{12,13},{14,15},{16,17},{18,... | collective-permute-start | bytes 516104 | tf_op jit(solution)/shard_map/ppermute | solution.py:439
  69.3 1.9 %collective-permute-start.6 = (bf16[3,224,128]{2,1,0:T(8,128)(2,1)S(1)}, bf16[3,224,128]{2,1,0:T(8,128)(2,1)S(1)}, u32[]{:S(2)}, u32[]{:S(2)}) collective-permute-start(bf16[3,224,128]{2,1,0:T(8,128)(2,1)S(1)} %constant_dynamic-update-slice_fusion.3.own), channel_id=1, source_target_pairs={{1,2},{3,4},{5,6},{7,8},{9,10},{11,12},{13,14},{15,16},{17,18},{19... | collective-permute-start | bytes 516104 | tf_op jit(solution)/shard_map/ppermute | solution.py:439
  71.2 11.3 %all-to-all-start.2 = ((f32[16,2,128]{2,1,0:T(2,128)}), f32[16,2,128]{2,1,0:T(2,128)S(1)}, u32[]{:S(2)}, u32[]{:S(2)}) async-start(f32[16,2,128]{2,1,0:T(2,128)} %get-tuple-element.34), calls=%async_computation.2 | async-start | bytes 32768 | tf_op jit(solution)/shard_map/all_to_all | solution.py:443
  82.4 1.0 shard_map.184.sums
  83.5 6.3 %all-to-all-done.2.columns = f32[16,2,128]{2,1,0:T(2,128)S(1)} async-done(((f32[16,2,128]{2,1,0:T(2,128)}), f32[16,2,128]{2,1,0:T(2,128)S(1)}, u32[]{:S(2)}, u32[]{:S(2)}) %all-to-all-start.2) | async-done | bytes 16416 | tf_op jit(solution)/shard_map/all_to_all | solution.py:443
  89.8 0.7 shard_map.182
  90.5 3.9 %all-to-all-start.3 = ((f32[32,2,128]{2,1,0:T(2,128)}), f32[32,2,128]{2,1,0:T(2,128)S(1)}, u32[]{:S(2)}, u32[]{:S(2)}) async-start(f32[32,2,128]{2,1,0:T(2,128)} %shard_map.182), calls=%async_computation.3 | async-start | bytes 65536 | tf_op jit(solution)/shard_map/all_to_all | solution.py:443
  94.4 4.3 %shard_map.183 = (f32[192,256]{1,0:T(8,128)S(1)}, f32[16,256]{1,0:T(8,128)S(1)}) custom-call(bf16[3,224,128]{2,1,0:T(8,128)(2,1)S(1)} %collective-permute-done.6.before, bf16[3,224,128]{2,1,0:T(8,128)(2,1)S(1)} %constant_dynamic-update-slice_fusion.3.own, bf16[3,224,128]{2,1,0:T(8,128)(2,1)S(1)} %collective-permute-done.7.after, ...), custom_call_target="tpu_custom_call" | custom-call | flops 2147483648 | bytes 1048576 | tf_op jit(solution)/shard_map/pallas_call | solution.py:34
  98.7 4.4 %all-to-all-done.3.partial = f32[32,2,128]{2,1,0:T(2,128)S(1)} async-done(((f32[32,2,128]{2,1,0:T(2,128)}), f32[32,2,128]{2,1,0:T(2,128)S(1)}, u32[]{:S(2)}, u32[]{:S(2)}) %all-to-all-start.3) | async-done | bytes 32800 | tf_op jit(solution)/shard_map/all_to_all | solution.py:443
  103.1 1.5 %shard_map.185 = (f32[192,128]{1,0:T(8,128)S(1)}, f32[16,1,128]{2,1,0:T(1,128)S(1)}) custom-call(f32[192,128]{1,0:T(8,128)} %bitcast.22, f32[192,128]{1,0:T(8,128)S(1)} %get-tuple-element.33.scattered, f32[32,2,128]{2,1,0:T(2,128)S(1)} %all-to-all-done.3.partial, f32[192,256]{1,0:T(8,128)S(1)} %get-tuple-element.36.near, ...), custom_call_target="tpu_custom_call" | custom-call | flops 67108864 | bytes 1048576 | tf_op jit(solution)/shard_map/pallas_call | solution.py:34
  104.6 10.9 %all_to_all.30.parts = f32[16,1,128]{2,1,0:T(1,128)S(1)} all-to-all(f32[16,1,128]{2,1,0:T(1,128)S(1)} %get-tuple-element.38), channel_id=1, replica_groups=mesh['bx_0'=2,'bx_1'=8,'by_0'=4,'by_1'=4,'by_2'=2] {'bx_0','by_1','by_2'}, dimensions={0} | all-to-all | bytes 16384 | tf_op jit(solution)/shard_map/all_to_all | solution.py:443
  115.6 12.4 %all_to_all.31.parts = f32[32,1,128]{2,1,0:T(1,128)S(1)} all-to-all(f32[32,1,128]{2,1,0:T(1,128)S(1)} %shard_map.186), channel_id=1, replica_groups=mesh['bx_0'=2,'bx_1'=8,'by_0'=4,'by_1'=4,'by_2'=2] {'bx_1','by_0'}, dimensions={0} | all-to-all | bytes 32768 | tf_op jit(solution)/shard_map/all_to_all | solution.py:443
  128.0 1.8 %shard_map.187 = (f32[192,128]{1,0:T(8,128)}, f32[192,128]{1,0:T(8,128)}) custom-call(f32[32,1,128]{2,1,0:T(1,128)S(1)} %all_to_all.31.parts, f32[192,128]{1,0:T(8,128)} %bitcast.23, f32[192,128]{1,0:T(8,128)S(1)} %get-tuple-element.33.scattered, f32[192,128]{1,0:T(8,128)S(1)} %get-tuple-element.39.twice), custom_call_target="tpu_custom_call" | custom-call | flops 16777216 | bytes 1048576 | tf_op jit(solution)/shard_map/pallas_call | solution.py:34
  (12 shorter events, 0.1 us)
Async XLA Ops:
  2.8 21.4 %collective-permute-start = (bf16[1,224,128]{2,1,0:T(8,128)(2,1)S(1)}, bf16[1,224,128]{2,1,0:T(8,128)(2,1)S(1)}, u32[]{:S(2)}, u32[]{:S(2)}) collective-permute-start(bf16[1,224,128]{2,1,0:T(8,128)(2,1)S(1)} %get-tuple-element.23), channel_id=1, source_target_pairs={{32,64},{96,128},{160,192},{224,256},{288,320},{352,384},{416,448}... | collective-permute-start | bytes 172040 | tf_op jit(solution)/shard_map/ppermute | solution.py:439
  3.5 20.8 %collective-permute-start.1 = (bf16[1,224,128]{2,1,0:T(8,128)(2,1)S(1)}, bf16[1,224,128]{2,1,0:T(8,128)(2,1)S(1)}, u32[]{:S(2)}, u32[]{:S(2)}) collective-permute-start(bf16[1,224,128]{2,1,0:T(8,128)(2,1)S(1)} %get-tuple-element.23), channel_id=1, source_target_pairs={{0,32},{64,96},{128,160},{192,224},{256,288},{320,352},{384,416},{... | collective-permute-start | bytes 172040 | tf_op jit(solution)/shard_map/ppermute | solution.py:439
  11.7 26.2 %all-to-all-start = ((f32[16,2,128]{2,1,0:T(2,128)}), f32[16,2,128]{2,1,0:T(2,128)S(1)}, u32[]{:S(2)}, u32[]{:S(2)}) async-start(f32[16,2,128]{2,1,0:T(2,128)} %get-tuple-element.22), calls=%async_computation | async-start | bytes 32768 | tf_op jit(solution)/shard_map/all_to_all | solution.py:443
  24.3 21.2 %collective-permute-start.3 = (bf16[3,224,128]{2,1,0:T(8,128)(2,1)S(1)}, bf16[3,224,128]{2,1,0:T(8,128)(2,1)S(1)}, u32[]{:S(2)}, u32[]{:S(2)}) collective-permute-start(bf16[3,224,128]{2,1,0:T(8,128)(2,1)S(1)} %constant_dynamic-update-slice_fusion.own), channel_id=1, source_target_pairs={{0,1},{2,3},{4,5},{6,7},{8,9},{10,11},{12,13},{14,15},{16,17},{18,... | collective-permute-start | bytes 516104 | tf_op jit(solution)/shard_map/ppermute | solution.py:439
  26.3 19.2 %collective-permute-start.2 = (bf16[3,224,128]{2,1,0:T(8,128)(2,1)S(1)}, bf16[3,224,128]{2,1,0:T(8,128)(2,1)S(1)}, u32[]{:S(2)}, u32[]{:S(2)}) collective-permute-start(bf16[3,224,128]{2,1,0:T(8,128)(2,1)S(1)} %constant_dynamic-update-slice_fusion.own), channel_id=1, source_target_pairs={{1,2},{3,4},{5,6},{7,8},{9,10},{11,12},{13,14},{15,16},{17,18},{19... | collective-permute-start | bytes 516104 | tf_op jit(solution)/shard_map/ppermute | solution.py:439
  38.6 15.6 %all-to-all-start.1 = ((f32[32,2,128]{2,1,0:T(2,128)}), f32[32,2,128]{2,1,0:T(2,128)S(1)}, u32[]{:S(2)}, u32[]{:S(2)}) async-start(f32[32,2,128]{2,1,0:T(2,128)} %shard_map.178), calls=%async_computation.1 | async-start | bytes 65536 | tf_op jit(solution)/shard_map/all_to_all | solution.py:443
  56.5 4.5 %collective-permute-start.4 = (bf16[1,224,128]{2,1,0:T(8,128)(2,1)S(1)}, bf16[1,224,128]{2,1,0:T(8,128)(2,1)S(1)}, u32[]{:S(2)}, u32[]{:S(2)}) collective-permute-start(bf16[1,224,128]{2,1,0:T(8,128)(2,1)S(1)} %get-tuple-element.35), channel_id=1, source_target_pairs={{32,64},{96,128},{160,192},{224,256},{288,320},{352,384},{416,448}... | collective-permute-start | bytes 172040 | tf_op jit(solution)/shard_map/ppermute | solution.py:439
  57.1 5.4 %collective-permute-start.5 = (bf16[1,224,128]{2,1,0:T(8,128)(2,1)S(1)}, bf16[1,224,128]{2,1,0:T(8,128)(2,1)S(1)}, u32[]{:S(2)}, u32[]{:S(2)}) collective-permute-start(bf16[1,224,128]{2,1,0:T(8,128)(2,1)S(1)} %get-tuple-element.35), channel_id=1, source_target_pairs={{0,32},{64,96},{128,160},{192,224},{256,288},{320,352},{384,416},{... | collective-permute-start | bytes 172040 | tf_op jit(solution)/shard_map/ppermute | solution.py:439
  62.6 31.8 %collective-permute-start.7 = (bf16[3,224,128]{2,1,0:T(8,128)(2,1)S(1)}, bf16[3,224,128]{2,1,0:T(8,128)(2,1)S(1)}, u32[]{:S(2)}, u32[]{:S(2)}) collective-permute-start(bf16[3,224,128]{2,1,0:T(8,128)(2,1)S(1)} %constant_dynamic-update-slice_fusion.3.own), channel_id=1, source_target_pairs={{0,1},{2,3},{4,5},{6,7},{8,9},{10,11},{12,13},{14,15},{16,17},{18,... | collective-permute-start | bytes 516104 | tf_op jit(solution)/shard_map/ppermute | solution.py:439
  69.3 25.1 %collective-permute-start.6 = (bf16[3,224,128]{2,1,0:T(8,128)(2,1)S(1)}, bf16[3,224,128]{2,1,0:T(8,128)(2,1)S(1)}, u32[]{:S(2)}, u32[]{:S(2)}) collective-permute-start(bf16[3,224,128]{2,1,0:T(8,128)(2,1)S(1)} %constant_dynamic-update-slice_fusion.3.own), channel_id=1, source_target_pairs={{1,2},{3,4},{5,6},{7,8},{9,10},{11,12},{13,14},{15,16},{17,18},{19... | collective-permute-start | bytes 516104 | tf_op jit(solution)/shard_map/ppermute | solution.py:439
  71.2 18.6 %all-to-all-start.2 = ((f32[16,2,128]{2,1,0:T(2,128)}), f32[16,2,128]{2,1,0:T(2,128)S(1)}, u32[]{:S(2)}, u32[]{:S(2)}) async-start(f32[16,2,128]{2,1,0:T(2,128)} %get-tuple-element.34), calls=%async_computation.2 | async-start | bytes 32768 | tf_op jit(solution)/shard_map/all_to_all | solution.py:443
  90.5 12.6 %all-to-all-start.3 = ((f32[32,2,128]{2,1,0:T(2,128)}), f32[32,2,128]{2,1,0:T(2,128)S(1)}, u32[]{:S(2)}, u32[]{:S(2)}) async-start(f32[32,2,128]{2,1,0:T(2,128)} %shard_map.182), calls=%async_computation.3 | async-start | bytes 65536 | tf_op jit(solution)/shard_map/all_to_all | solution.py:443

commit v4 on v3

--- a/solution.py
+++ b/solution.py
@@ -110,8 +110,13 @@
     halo_ref[0, 2 * coefs + boxes :, :] = leaf_imag.astype(BF16)
     column_real = jnp.sum(leaf_real * leaf_cos + leaf_imag * leaf_sin, axis=0, keepdims=True)
     column_imag = jnp.sum(leaf_imag * leaf_cos - leaf_real * leaf_sin, axis=0, keepdims=True)
-    pair = jnp.concatenate([column_real, column_imag], axis=0)
-    column_ref[...] = jnp.broadcast_to(pair[None], column_ref.shape)
+    tile = (16, dirs)
+    even = lax.rem(lax.broadcasted_iota(jnp.int32, tile, 0), 2) == 0
+    pairs = jnp.where(
+        even, jnp.broadcast_to(column_real, tile), jnp.broadcast_to(column_imag, tile)
+    ).astype(BF16)
+    for item in range(column_ref.shape[0] // 16):
+        column_ref[item * 16 : (item + 1) * 16, :] = pairs
 
 
 def lanes(values):
@@ -202,31 +207,6 @@
     chosen[:, :dirs] = dot(hot, transfer[:, 0, :], precision=HIGHEST)
     chosen[:, dirs:] = dot(hot, transfer[:, 1, :], precision=HIGHEST)
     mie_full[...] = dot(spread[...], mie[...], precision=HIGHEST)
-
-
-def window_kernel(index, transfer, window, *, near_z, near_x, groups, run, top_x, top_y):
-    row, col = lax.div(index[0], near_x * run), lax.rem(index[0], near_x * run)
-    high, depth = lax.div(row, near_z), lax.rem(row, near_z)
-    across, lane = lax.div(col, run), lax.rem(col, run)
-    ordinal = lax.broadcasted_iota(jnp.int32, (run, 128), 0)
-    for z in range(near_z):
-        for x in range(near_x):
-            start = (across - x) * run - lane + top_y
-            apart_y = jnp.abs(ordinal + (start - top_y))
-            for group in range(groups):
-                shift = (group - high) * near_z + depth - z
-                keep = (apart_y >= 2) | (jnp.abs(shift) >= 2)
-                for part in range(2):
-                    rows = transfer[shift + top_x, pl.ds(start, run), part, :]
-                    window[part, z * near_x + x, group * run : (group + 1) * run, :] = jnp.where(
-                        keep, rows, 0.0
-                    )
-
-
-def coarse_kernel(columns, window, partial):
-    real, imag = columns[:, 0, :][None], columns[:, 1, :][None]
-    partial[:, 0, :] = jnp.sum(real * window[0] - imag * window[1], axis=1)
-    partial[:, 1, :] = jnp.sum(imag * window[0] + real * window[1], axis=1)
 
 
 def near_kernel(before, own, after, counts, table, select, chosen, near, leaf_in, columns):
@@ -268,11 +248,20 @@
     near[...] = total
 
 
-def arrive(partial, near, leaf_in, receive, cosines, sines, member, leaf_cos, leaf_sin, mie_full):
+def coarse(columns, window):
+    rows = columns.shape[0]
+    values = columns.astype(F32)
+    even = lax.rem(lax.broadcasted_iota(jnp.int32, values.shape, 0), 2) == 0
+    turned = jnp.where(even, pltpu.roll(values, rows - 1, 0), pltpu.roll(values, 1, 0))
+    real = window * jnp.where(even, values, -values)
+    imag = window * turned
+    return jnp.sum(real, axis=0, keepdims=True), jnp.sum(imag, axis=0, keepdims=True)
+
+
+def arrive(columns, window, near, leaf_in, receive, cosines, sines, member, leaf_cos, leaf_sin, mie_full):
     _, dirs = leaf_cos.shape
     coefs = near.shape[0] // 2
-    column_real = jnp.sum(partial[:, 0, :], axis=0, keepdims=True)
-    column_imag = jnp.sum(partial[:, 1, :], axis=0, keepdims=True)
+    column_real, column_imag = coarse(columns, window)
     incoming = leaf_in + jnp.concatenate(
         [
             column_real * leaf_cos - column_imag * leaf_sin,
@@ -306,7 +295,8 @@
 
 
 def middle_kernel(
-    partial,
+    columns,
+    window,
     near,
     leaf_in,
     pattern,
@@ -323,7 +313,8 @@
 ):
     member = one_hot(leaf_cos.shape[0], box[...]).astype(BF16)
     scattered = arrive(
-        partial[...],
+        columns[...],
+        window[...],
         near[...],
         leaf_in[...],
         receive[...],
@@ -351,7 +342,8 @@
 def last_kernel(
     vector,
     scattered,
-    partial,
+    columns,
+    window,
     near,
     leaf_in,
     receive,
@@ -367,7 +359,8 @@
 ):
     member = one_hot(leaf_cos.shape[0], box[...]).astype(BF16)
     twice = arrive(
-        partial[...],
+        columns[...],
+        window[...],
         near[...],
         leaf_in[...],
         receive[...],
@@ -464,9 +457,8 @@
     dirs = pattern.shape[1]
     boxes, entries = far_src.shape[2:]
     classes, pairs = near_src.shape[2:]
-    high_count, near_z = lax.axis_size("bx_0"), lax.axis_size("bx_1")
-    near_x = lax.axis_size("by_0")
-    run = lax.axis_size(("by_1", "by_2"))
+    across_x, across_y = lax.axis_size(BX), lax.axis_size(BY)
+    first_pos, second_pos = lax.axis_index(BX), lax.axis_index(BY)
     first_count, second_count = lax.axis_size(FIRST), lax.axis_size(SECOND)
     index = lax.axis_index(BX + BY).astype(jnp.int32).reshape(1)
 
@@ -481,7 +473,7 @@
     receive = receive.reshape(rows, dirs)
 
     halo_shape = kept((1, rows + 2 * boxes, spheres), BF16)
-    column_shape = kept((first_count, 2, dirs))
+    column_shape = kept((2 * across_x * across_y, dirs), BF16)
     halo, column, cosines, sines, send = call(
         first_kernel,
         (
@@ -501,7 +493,7 @@
         spread = mie_spread(coefs, mie.shape[1])
         zero = np.zeros_like(spread)
         return call(
-            functools.partial(count_kernel, across_y=near_x * run),
+            functools.partial(count_kernel, across_y=across_y),
             (
                 shape((9 * spheres, classes * spheres), BF16),
                 kept((boxes * entries, 9 * boxes), BF16),
@@ -530,35 +522,24 @@
         )
 
     def windows():
-        return call(
-            functools.partial(
-                window_kernel,
-                near_z=near_z,
-                near_x=near_x,
-                groups=high_count,
-                run=run,
-                top_x=high_count * near_z - 1,
-                top_y=near_x * run - 1,
-            ),
-            kept((2, second_count, first_count, dirs)),
-            (index, coarse_transfer.transpose(1, 2, 0, 3)),
-            flops=1 << 28,
+        taken = lax.dynamic_slice(
+            coarse_transfer.transpose(1, 2, 0, 3),
+            (across_x - 1 - first_pos, across_y - 1 - second_pos, 0, 0),
+            (across_x, across_y, 2, dirs),
         )
-
-    def apply(halo, column, window, counts, select, chosen):
-        columns = exchange(column, FIRST)
+        apart_x = jnp.abs(jnp.arange(across_x, dtype=jnp.int32) - first_pos)[:, None]
+        apart_y = jnp.abs(jnp.arange(across_y, dtype=jnp.int32) - second_pos)[None]
+        keep = (apart_x >= 2) | (apart_y >= 2)
+        taken = jnp.where(keep[:, :, None, None], taken, 0.0)
+        return taken.reshape(2 * across_x * across_y, dirs)
+
+    def apply(halo, column, counts, select, chosen):
+        columns = exchange(column.reshape(-1, 2, dirs), BX + BY).reshape(-1, dirs)
         ahead = swap(halo, BX, 0)
         behind = swap(halo, BX, 1)
         line = jnp.concatenate([behind, halo, ahead], axis=0)
         right = swap(line, BY, 0)
         left = swap(line, BY, 1)
-        partial = call(
-            coarse_kernel,
-            kept((second_count, 2, dirs)),
-            (resident(columns), resident(window)),
-            1 << 24,
-        )
-        partial = exchange(partial, SECOND)
         near, leaf_in = call(
             near_kernel,
             (kept((rows, 2 * spheres)), kept((boxes, 2 * dirs))),
@@ -585,11 +566,11 @@
             out_specs=(whole, whole),
             scratch_shapes=[pltpu.VMEM((rows, 9 * spheres), BF16)],
         )
-        return resident(partial), resident(near), resident(leaf_in)
+        return resident(columns), resident(window), resident(near), resident(leaf_in)
 
     window = windows()
     counts, select, chosen, mie_full = prepare()
-    partial, near, leaf_in = apply(halo, column, window, counts, select, chosen)
+    inward = apply(halo, column, counts, select, chosen)
     far = (
         receive,
         resident(cosines),
@@ -602,16 +583,16 @@
     once, halo, column = call(
         middle_kernel,
         (kept((rows, spheres)), halo_shape, column_shape),
-        (partial, near, leaf_in, resident(send)) + far,
+        inward + (resident(send),) + far,
         flops=1 << 26,
     )
     sums = call(sums_kernel, kept((1, 128)), (vector, resident(once)), 1 << 24)
-    partial, near, leaf_in = apply(halo, column, window, counts, select, chosen)
+    inward = apply(halo, column, counts, select, chosen)
     once = resident(once)
     twice, everyone = call(
         last_kernel,
         (kept((rows, spheres)), kept((first_count, 1, 128))),
-        (vector, once, partial, near, leaf_in) + far + (resident(sums),),
+        (vector, once) + inward + far + (resident(sums),),
         flops=1 << 26,
     )
     everyone = call(

time: 131 us -> 130 us (level)
  waiting for transfers between devices: 16.7 us -> 4.77 us
  blocking collectives: 23.4 us -> 30.7 us
  starting transfers between devices: 62 us -> 66.6 us
  Pallas kernels: 26.8 us -> 24.4 us
  other arithmetic: 0 us -> 1.76 us
    all_to_all x4 -> x2, waiting for transfers between devices: 15.2 us -> 4.75 us  [exchange(): return lax.all_to_all(x, axes, split_axis=0, concat_axis=0, tiled=True)]
    all_to_all x2, blocking collectives: 23.4 us -> 30.7 us  [exchange(): return lax.all_to_all(x, axes, split_axis=0, concat_axis=0, tiled=True)]
    all_to_all x4 -> x2, starting transfers between devices: 34.5 us -> 38.3 us  [exchange(): return lax.all_to_all(x, axes, split_axis=0, concat_axis=0, tiled=True)]
    pallas_call x12 -> x9, Pallas kernels: 26.8 us -> 24.4 us  [call(): pl.pallas_call(kernel, out_shape=out_shape, interpret=INTERPRET, cost_est...]
    select_n x0 -> x1, other arithmetic: none -> 1.67 us  [windows(): taken = jnp.where(keep[:, :, None, None], taken, 0.0)]
    ppermute x8, waiting for transfers between devices: 1.53 us -> 0.02 us  [swap(): return lax.ppermute(x, axes, pairs + [(j, i) for i, j in pairs])]
  transfers between devices with their start and end apart: 12 -> 10, of which waited for: 4 -> 1; matrix products, arithmetic and copies ran while one was open for 0% -> 1% of each run, Pallas kernels for 15% -> 12%
where the time goes in v4:
time: 130 us; the launch traced here: 129 us
  starting transfers between devices  66.6 us (51%)
  blocking collectives  30.7 us (24%)
  Pallas kernels  24.4 us (19%)
  waiting for transfers between devices  4.77 us (4%)
  other arithmetic  1.76 us (1%)
    all_to_all x2, starting transfers between devices, exchange(): return lax.all_to_all(x, axes, split_axis=0, concat_axis=0, tiled=True)  38.3 us
    all_to_all x2, blocking collectives, exchange(): return lax.all_to_all(x, axes, split_axis=0, concat_axis=0, tiled=True)  30.7 us
    ppermute x8, starting transfers between devices, swap(): return lax.ppermute(x, axes, pairs + [(j, i) for i, j in pairs])  28.3 us
    pallas_call x9, Pallas kernels, call(): pl.pallas_call(kernel, out_shape=out_shape, interpret=INTERPRET, cost_est...  24.4 us
    all_to_all x2, waiting for transfers between devices, exchange(): return lax.all_to_all(x, axes, split_axis=0, concat_axis=0, tiled=True)  4.75 us
  transfers between devices with their start and end apart: 10, of which 1 were waited for; matrix products, arithmetic and copies ran while one was open for 1% of the time, Pallas kernels for 12%

profile of v4, /device:TPU:1, one launch (start us, length us, event | category | flops | bytes accessed | tf_op | source)
XLA Modules:
  0.0 129.2 jit_solution(11253019418008185310)
XLA Ops:
  0.6 2.3 %shard_map.176 = (bf16[1,224,128]{2,1,0:T(8,128)(2,1)S(1)}, bf16[1024,128]{1,0:T(8,128)(2,1)}, f32[128,128]{1,0:T(8,128)S(1)}, f32[128,128]{1,0:T(8,128)S(1)}, bf16[256,96]{1,0:T(8,128)(2,1)S(1)}) custom-call(f32[192,128]{1,0:T(8,128)} %bitcast.29, bf16[2,96,128]{2,1,0:T(8,128)(2,1)} %bitcast.35, f32[3,1,128]{2,1,0:T(1,128)} %bitcast.39, ...), custom_call_target="tpu_custom_call" | custom-call | flops 67108864 | bytes 1048576 | tf_op jit(solution)/shard_map/pallas_call | solution.py:34
  3.0 0.7 collective-permute-start
  3.6 8.2 %collective-permute-start.1 = (bf16[1,224,128]{2,1,0:T(8,128)(2,1)S(1)}, bf16[1,224,128]{2,1,0:T(8,128)(2,1)S(1)}, u32[]{:S(2)}, u32[]{:S(2)}) collective-permute-start(bf16[1,224,128]{2,1,0:T(8,128)(2,1)S(1)} %get-tuple-element.23), channel_id=1, source_target_pairs={{0,32},{64,96},{128,160},{192,224},{256,288},{320,352},{384,416},{... | collective-permute-start | bytes 172040 | tf_op jit(solution)/shard_map/ppermute | solution.py:432
  11.8 20.1 %all-to-all-start = ((bf16[512,2,128]{2,1,0:T(2,128)(2,1)}), bf16[512,2,128]{2,1,0:T(2,128)(2,1)S(1)}, u32[]{:S(2)}, u32[]{:S(2)}) async-start(bf16[512,2,128]{2,1,0:T(2,128)(2,1)} %bitcast.4), calls=%async_computation | async-start | bytes 524288 | tf_op jit(solution)/shard_map/all_to_all | solution.py:436
  31.9 0.1 broadcast_or_fusion
  32.0 1.7 %dynamic-slice_select_fusion = f32[2,16,32,128]{3,0,2,1:T(2,128)S(1)} fusion(f32[2,31,63,128]{3,0,2,1:T(2,128)} %param.29, s32[]{:T(128)S(6)} %select_n.13, s32[]{:T(128)S(6)} %select_n.14, pred[16,32]{1,0:T(8,128)(4,1)S(1)} %broadcast_or_fusion), kind=kLoop, calls=%fused_computation | loop fusion | flops 131072 | bytes 1049096 | tf_op jit(solution)/shard_map/jit(_where)/select_n | solution.py:533
  33.7 0.0 collective-permute-done
  33.7 0.0 collective-permute-done.1
  33.7 3.5 %collective-permute-start.2 = (bf16[3,224,128]{2,1,0:T(8,128)(2,1)S(1)}, bf16[3,224,128]{2,1,0:T(8,128)(2,1)S(1)}, u32[]{:S(2)}, u32[]{:S(2)}) collective-permute-start(bf16[3,224,128]{2,1,0:T(8,128)(2,1)S(1)} %constant_dynamic-update-slice_fusion.own), channel_id=1, source_target_pairs={{1,2},{3,4},{5,6},{7,8},{9,10},{11,12},{13,14},{15,16},{17,18},{19... | collective-permute-start | bytes 516104 | tf_op jit(solution)/shard_map/ppermute | solution.py:432
  37.3 3.3 %collective-permute-start.3 = (bf16[3,224,128]{2,1,0:T(8,128)(2,1)S(1)}, bf16[3,224,128]{2,1,0:T(8,128)(2,1)S(1)}, u32[]{:S(2)}, u32[]{:S(2)}) collective-permute-start(bf16[3,224,128]{2,1,0:T(8,128)(2,1)S(1)} %constant_dynamic-update-slice_fusion.own), channel_id=1, source_target_pairs={{0,1},{2,3},{4,5},{6,7},{8,9},{10,11},{12,13},{14,15},{16,17},{18,... | collective-permute-start | bytes 516104 | tf_op jit(solution)/shard_map/ppermute | solution.py:432
  40.6 6.2 %shard_map.177 = (bf16[1152,2048]{1,0:T(8,128)(2,1)}, bf16[384,144]{1,0:T(8,128)(2,1)S(1)}, f32[384,256]{1,0:T(8,128)S(1)}, f32[192,128]{1,0:T(8,128)S(1)}) custom-call(s32[1]{0:T(128)} %bitcast.8.index, s32[16,256]{1,0:T(8,128)} %bitcast.44, s32[16,256]{1,0:T(8,128)} %bitcast.45, s32[16,24]{1,0:T(8,128)} %bitcast.47, s32[16,24]{1,0:T(8,128)} %bitcast.48, ...), custom_call_target="tpu_custom_call" | custom-call | flops 2147483648 | bytes 1048576 | tf_op jit(solution)/shard_map/pallas_call | solution.py:34
  46.8 0.0 collective-permute-done.2.before
  46.8 0.0 collective-permute-done.3.after
  46.8 4.3 %shard_map.178 = (f32[192,256]{1,0:T(8,128)S(1)}, f32[16,256]{1,0:T(8,128)S(1)}) custom-call(bf16[3,224,128]{2,1,0:T(8,128)(2,1)S(1)} %collective-permute-done.2.before, bf16[3,224,128]{2,1,0:T(8,128)(2,1)S(1)} %constant_dynamic-update-slice_fusion.own, bf16[3,224,128]{2,1,0:T(8,128)(2,1)S(1)} %collective-permute-done.3.after, ...), custom_call_target="tpu_custom_call" | custom-call | flops 2147483648 | bytes 1048576 | tf_op jit(solution)/shard_map/pallas_call | solution.py:34
  51.1 0.0 all-to-all-done
  51.1 2.7 %shard_map.179 = (f32[192,128]{1,0:T(8,128)S(1)}, bf16[1,224,128]{2,1,0:T(8,128)(2,1)S(1)}, bf16[1024,128]{1,0:T(8,128)(2,1)}) custom-call(bf16[1024,128]{1,0:T(8,128)(2,1)S(1)} %bitcast.27, f32[1024,128]{1,0:T(8,128)S(1)} %bitcast.25, f32[192,256]{1,0:T(8,128)S(1)} %get-tuple-element.27.near, f32[16,256]{1,0:T(8,128)S(1)} %get-tuple-element.28.leaf_in, ...), custom_call_target="tpu_custom_call" | custom-call | flops 67108864 | bytes 1048576 | tf_op jit(solution)/shard_map/pallas_call | solution.py:34
  53.8 0.7 collective-permute-start.4
  54.5 5.1 %collective-permute-start.5 = (bf16[1,224,128]{2,1,0:T(8,128)(2,1)S(1)}, bf16[1,224,128]{2,1,0:T(8,128)(2,1)S(1)}, u32[]{:S(2)}, u32[]{:S(2)}) collective-permute-start(bf16[1,224,128]{2,1,0:T(8,128)(2,1)S(1)} %get-tuple-element.35), channel_id=1, source_target_pairs={{0,32},{64,96},{128,160},{192,224},{256,288},{320,352},{384,416},{... | collective-permute-start | bytes 172040 | tf_op jit(solution)/shard_map/ppermute | solution.py:432
  59.6 18.2 %all-to-all-start.1 = ((bf16[512,2,128]{2,1,0:T(2,128)(2,1)}), bf16[512,2,128]{2,1,0:T(2,128)(2,1)S(1)}, u32[]{:S(2)}, u32[]{:S(2)}) async-start(bf16[512,2,128]{2,1,0:T(2,128)(2,1)} %bitcast.16), calls=%async_computation.1 | async-start | bytes 524288 | tf_op jit(solution)/shard_map/all_to_all | solution.py:436
  77.8 0.0 collective-permute-done.4
  77.9 0.0 collective-permute-done.5
  77.9 3.5 %collective-permute-start.6 = (bf16[3,224,128]{2,1,0:T(8,128)(2,1)S(1)}, bf16[3,224,128]{2,1,0:T(8,128)(2,1)S(1)}, u32[]{:S(2)}, u32[]{:S(2)}) collective-permute-start(bf16[3,224,128]{2,1,0:T(8,128)(2,1)S(1)} %constant_dynamic-update-slice_fusion.3.own), channel_id=1, source_target_pairs={{1,2},{3,4},{5,6},{7,8},{9,10},{11,12},{13,14},{15,16},{17,18},{19... | collective-permute-start | bytes 516104 | tf_op jit(solution)/shard_map/ppermute | solution.py:432
  81.4 3.3 %collective-permute-start.7 = (bf16[3,224,128]{2,1,0:T(8,128)(2,1)S(1)}, bf16[3,224,128]{2,1,0:T(8,128)(2,1)S(1)}, u32[]{:S(2)}, u32[]{:S(2)}) collective-permute-start(bf16[3,224,128]{2,1,0:T(8,128)(2,1)S(1)} %constant_dynamic-update-slice_fusion.3.own), channel_id=1, source_target_pairs={{0,1},{2,3},{4,5},{6,7},{8,9},{10,11},{12,13},{14,15},{16,17},{18,... | collective-permute-start | bytes 516104 | tf_op jit(solution)/shard_map/ppermute | solution.py:432
  84.8 1.0 shard_map.181.sums
  85.8 0.0 collective-permute-done.6.before
  85.8 0.0 collective-permute-done.7.after
  85.8 4.3 %shard_map.180 = (f32[192,256]{1,0:T(8,128)S(1)}, f32[16,256]{1,0:T(8,128)S(1)}) custom-call(bf16[3,224,128]{2,1,0:T(8,128)(2,1)S(1)} %collective-permute-done.6.before, bf16[3,224,128]{2,1,0:T(8,128)(2,1)S(1)} %constant_dynamic-update-slice_fusion.3.own, bf16[3,224,128]{2,1,0:T(8,128)(2,1)S(1)} %collective-permute-done.7.after, ...), custom_call_target="tpu_custom_call" | custom-call | flops 2147483648 | bytes 1048576 | tf_op jit(solution)/shard_map/pallas_call | solution.py:34
  90.1 4.7 %all-to-all-done.1 = bf16[512,2,128]{2,1,0:T(2,128)(2,1)S(1)} async-done(((bf16[512,2,128]{2,1,0:T(2,128)(2,1)}), bf16[512,2,128]{2,1,0:T(2,128)(2,1)S(1)}, u32[]{:S(2)}, u32[]{:S(2)}) %all-to-all-start.1) | async-done | bytes 262176 | tf_op jit(solution)/shard_map/all_to_all | solution.py:436
  94.8 1.8 %shard_map.182 = (f32[192,128]{1,0:T(8,128)S(1)}, f32[16,1,128]{2,1,0:T(1,128)S(1)}) custom-call(f32[192,128]{1,0:T(8,128)} %bitcast.31, f32[192,128]{1,0:T(8,128)S(1)} %get-tuple-element.33.scattered, bf16[1024,128]{1,0:T(8,128)(2,1)S(1)} %bitcast.28, f32[1024,128]{1,0:T(8,128)S(1)} %bitcast.26, f32[192,256]{1,0:T(8,128)S(1)} %get-tuple-element.36.near, ...), custom_call_target="tpu_custom_call" | custom-call | flops 67108864 | bytes 1048576 | tf_op jit(solution)/shard_map/pallas_call | solution.py:34
  96.7 10.5 %all_to_all.20.parts = f32[16,1,128]{2,1,0:T(1,128)S(1)} all-to-all(f32[16,1,128]{2,1,0:T(1,128)S(1)} %get-tuple-element.38), channel_id=1, replica_groups=mesh['bx_0'=2,'bx_1'=8,'by_0'=4,'by_1'=4,'by_2'=2] {'bx_0','by_1','by_2'}, dimensions={0} | all-to-all | bytes 16384 | tf_op jit(solution)/shard_map/all_to_all | solution.py:436
  107.2 20.2 %all_to_all.21.parts = f32[32,1,128]{2,1,0:T(1,128)S(1)} all-to-all(f32[32,1,128]{2,1,0:T(1,128)S(1)} %shard_map.183), channel_id=1, replica_groups=mesh['bx_0'=2,'bx_1'=8,'by_0'=4,'by_1'=4,'by_2'=2] {'bx_1','by_0'}, dimensions={0} | all-to-all | bytes 32768 | tf_op jit(solution)/shard_map/all_to_all | solution.py:436
  127.4 1.8 %shard_map.184 = (f32[192,128]{1,0:T(8,128)}, f32[192,128]{1,0:T(8,128)}) custom-call(f32[32,1,128]{2,1,0:T(1,128)S(1)} %all_to_all.21.parts, f32[192,128]{1,0:T(8,128)} %bitcast.32, f32[192,128]{1,0:T(8,128)S(1)} %get-tuple-element.33.scattered, f32[192,128]{1,0:T(8,128)S(1)} %get-tuple-element.39.twice), custom_call_target="tpu_custom_call" | custom-call | flops 16777216 | bytes 1048576 | tf_op jit(solution)/shard_map/pallas_call | solution.py:34
  (9 shorter events, 0.1 us)
Async XLA Ops:
  3.0 30.7 %collective-permute-start = (bf16[1,224,128]{2,1,0:T(8,128)(2,1)S(1)}, bf16[1,224,128]{2,1,0:T(8,128)(2,1)S(1)}, u32[]{:S(2)}, u32[]{:S(2)}) collective-permute-start(bf16[1,224,128]{2,1,0:T(8,128)(2,1)S(1)} %get-tuple-element.23), channel_id=1, source_target_pairs={{32,64},{96,128},{160,192},{224,256},{288,320},{352,384},{416,448}... | collective-permute-start | bytes 172040 | tf_op jit(solution)/shard_map/ppermute | solution.py:432
  3.6 30.1 %collective-permute-start.1 = (bf16[1,224,128]{2,1,0:T(8,128)(2,1)S(1)}, bf16[1,224,128]{2,1,0:T(8,128)(2,1)S(1)}, u32[]{:S(2)}, u32[]{:S(2)}) collective-permute-start(bf16[1,224,128]{2,1,0:T(8,128)(2,1)S(1)} %get-tuple-element.23), channel_id=1, source_target_pairs={{0,32},{64,96},{128,160},{192,224},{256,288},{320,352},{384,416},{... | collective-permute-start | bytes 172040 | tf_op jit(solution)/shard_map/ppermute | solution.py:432
  11.8 39.3 %all-to-all-start = ((bf16[512,2,128]{2,1,0:T(2,128)(2,1)}), bf16[512,2,128]{2,1,0:T(2,128)(2,1)S(1)}, u32[]{:S(2)}, u32[]{:S(2)}) async-start(bf16[512,2,128]{2,1,0:T(2,128)(2,1)} %bitcast.4), calls=%async_computation | async-start | bytes 524288 | tf_op jit(solution)/shard_map/all_to_all | solution.py:436
  33.7 13.1 %collective-permute-start.2 = (bf16[3,224,128]{2,1,0:T(8,128)(2,1)S(1)}, bf16[3,224,128]{2,1,0:T(8,128)(2,1)S(1)}, u32[]{:S(2)}, u32[]{:S(2)}) collective-permute-start(bf16[3,224,128]{2,1,0:T(8,128)(2,1)S(1)} %constant_dynamic-update-slice_fusion.own), channel_id=1, source_target_pairs={{1,2},{3,4},{5,6},{7,8},{9,10},{11,12},{13,14},{15,16},{17,18},{19... | collective-permute-start | bytes 516104 | tf_op jit(solution)/shard_map/ppermute | solution.py:432
  37.3 9.5 %collective-permute-start.3 = (bf16[3,224,128]{2,1,0:T(8,128)(2,1)S(1)}, bf16[3,224,128]{2,1,0:T(8,128)(2,1)S(1)}, u32[]{:S(2)}, u32[]{:S(2)}) collective-permute-start(bf16[3,224,128]{2,1,0:T(8,128)(2,1)S(1)} %constant_dynamic-update-slice_fusion.own), channel_id=1, source_target_pairs={{0,1},{2,3},{4,5},{6,7},{8,9},{10,11},{12,13},{14,15},{16,17},{18,... | collective-permute-start | bytes 516104 | tf_op jit(solution)/shard_map/ppermute | solution.py:432
  53.8 24.0 %collective-permute-start.4 = (bf16[1,224,128]{2,1,0:T(8,128)(2,1)S(1)}, bf16[1,224,128]{2,1,0:T(8,128)(2,1)S(1)}, u32[]{:S(2)}, u32[]{:S(2)}) collective-permute-start(bf16[1,224,128]{2,1,0:T(8,128)(2,1)S(1)} %get-tuple-element.35), channel_id=1, source_target_pairs={{32,64},{96,128},{160,192},{224,256},{288,320},{352,384},{416,448}... | collective-permute-start | bytes 172040 | tf_op jit(solution)/shard_map/ppermute | solution.py:432
  54.5 23.4 %collective-permute-start.5 = (bf16[1,224,128]{2,1,0:T(8,128)(2,1)S(1)}, bf16[1,224,128]{2,1,0:T(8,128)(2,1)S(1)}, u32[]{:S(2)}, u32[]{:S(2)}) collective-permute-start(bf16[1,224,128]{2,1,0:T(8,128)(2,1)S(1)} %get-tuple-element.35), channel_id=1, source_target_pairs={{0,32},{64,96},{128,160},{192,224},{256,288},{320,352},{384,416},{... | collective-permute-start | bytes 172040 | tf_op jit(solution)/shard_map/ppermute | solution.py:432
  59.6 35.3 %all-to-all-start.1 = ((bf16[512,2,128]{2,1,0:T(2,128)(2,1)}), bf16[512,2,128]{2,1,0:T(2,128)(2,1)S(1)}, u32[]{:S(2)}, u32[]{:S(2)}) async-start(bf16[512,2,128]{2,1,0:T(2,128)(2,1)} %bitcast.16), calls=%async_computation.1 | async-start | bytes 524288 | tf_op jit(solution)/shard_map/all_to_all | solution.py:436
  77.9 7.9 %collective-permute-start.6 = (bf16[3,224,128]{2,1,0:T(8,128)(2,1)S(1)}, bf16[3,224,128]{2,1,0:T(8,128)(2,1)S(1)}, u32[]{:S(2)}, u32[]{:S(2)}) collective-permute-start(bf16[3,224,128]{2,1,0:T(8,128)(2,1)S(1)} %constant_dynamic-update-slice_fusion.3.own), channel_id=1, source_target_pairs={{1,2},{3,4},{5,6},{7,8},{9,10},{11,12},{13,14},{15,16},{17,18},{19... | collective-permute-start | bytes 516104 | tf_op jit(solution)/shard_map/ppermute | solution.py:432
  81.4 4.4 %collective-permute-start.7 = (bf16[3,224,128]{2,1,0:T(8,128)(2,1)S(1)}, bf16[3,224,128]{2,1,0:T(8,128)(2,1)S(1)}, u32[]{:S(2)}, u32[]{:S(2)}) collective-permute-start(bf16[3,224,128]{2,1,0:T(8,128)(2,1)S(1)} %constant_dynamic-update-slice_fusion.3.own), channel_id=1, source_target_pairs={{0,1},{2,3},{4,5},{6,7},{8,9},{10,11},{12,13},{14,15},{16,17},{18,... | collective-permute-start | bytes 516104 | tf_op jit(solution)/shard_map/ppermute | solution.py:432

commit v5 on v3

--- a/solution.py
+++ b/solution.py
@@ -500,6 +500,7 @@
     def prepare():
         spread = mie_spread(coefs, mie.shape[1])
         zero = np.zeros_like(spread)
+        spread = jnp.asarray(np.block([[spread, zero], [zero, spread]]))
         return call(
             functools.partial(count_kernel, across_y=near_x * run),
             (
@@ -516,7 +517,7 @@
                 far_cls.reshape(boxes, entries),
                 leaf_transfer,
                 mie.reshape(2 * mie.shape[1], spheres),
-                jnp.asarray(np.block([[spread, zero], [zero, spread]])),
+                spread,
             ),
             flops=1 << 31,
             grid=(classes // chunk,),
@@ -590,15 +591,10 @@
     window = windows()
     counts, select, chosen, mie_full = prepare()
     partial, near, leaf_in = apply(halo, column, window, counts, select, chosen)
-    far = (
-        receive,
-        resident(cosines),
-        resident(sines),
-        box,
-        leaf_cos,
-        leaf_sin,
-        resident(mie_full),
-    )
+    far = tuple(
+        resident(item) for item in (receive, cosines, sines, box, leaf_cos, leaf_sin, mie_full)
+    )
+    vector = resident(vector)
     once, halo, column = call(
         middle_kernel,
         (kept((rows, spheres)), halo_shape, column_shape),

time: 131 us -> 128 us (0.977)
  Pallas kernels: 26.8 us -> 23.3 us
    pallas_call x12, Pallas kernels: 26.8 us -> 23.3 us  [call(): pl.pallas_call(kernel, out_shape=out_shape, interpret=INTERPRET, cost_est...]
  transfers between devices with their start and end apart: 12 -> 12, of which waited for: 4 -> 4; matrix products, arithmetic and copies ran while one was open for 0% -> 0% of each run, Pallas kernels for 15% -> 14%
where the time goes in v5:
time: 128 us; the launch traced here: 127 us
  starting transfers between devices  62 us (48%)
  blocking collectives  23.4 us (18%)
  Pallas kernels  23.3 us (18%)
  waiting for transfers between devices  17.6 us (14%)
    all_to_all x4, starting transfers between devices, exchange(): return lax.all_to_all(x, axes, split_axis=0, concat_axis=0, tiled=True)  34.5 us
    ppermute x8, starting transfers between devices, swap(): return lax.ppermute(x, axes, pairs + [(j, i) for i, j in pairs])  27.5 us
    all_to_all x2, blocking collectives, exchange(): return lax.all_to_all(x, axes, split_axis=0, concat_axis=0, tiled=True)  23.4 us
    pallas_call x12, Pallas kernels, call(): pl.pallas_call(kernel, out_shape=out_shape, interpret=INTERPRET, cost_est...  23.3 us
    all_to_all x4, waiting for transfers between devices, exchange(): return lax.all_to_all(x, axes, split_axis=0, concat_axis=0, tiled=True)  16 us
  transfers between devices with their start and end apart: 12, of which 4 were waited for; matrix products, arithmetic and copies ran while one was open for 0% of the time, Pallas kernels for 14%

profile of v5, /device:TPU:1, one launch (start us, length us, event | category | flops | bytes accessed | tf_op | source)
XLA Modules:
  0.0 127.2 jit_solution(11206446924933198013)
XLA Ops:
  0.6 2.2 %shard_map.176 = (bf16[1,224,128]{2,1,0:T(8,128)(2,1)S(1)}, f32[16,2,128]{2,1,0:T(2,128)}, f32[128,128]{1,0:T(8,128)S(1)}, f32[128,128]{1,0:T(8,128)S(1)}, bf16[256,96]{1,0:T(8,128)(2,1)S(1)}) custom-call(f32[192,128]{1,0:T(8,128)} %bitcast.19, bf16[2,96,128]{2,1,0:T(8,128)(2,1)} %bitcast.29, f32[3,1,128]{2,1,0:T(1,128)} %bitcast.30, ...), custom_call_target="tpu_custom_call" | custom-call | flops 67108864 | bytes 1048576 | tf_op jit(solution)/shard_map/pallas_call | solution.py:34
  2.8 0.7 collective-permute-start
  3.5 8.2 %collective-permute-start.1 = (bf16[1,224,128]{2,1,0:T(8,128)(2,1)S(1)}, bf16[1,224,128]{2,1,0:T(8,128)(2,1)S(1)}, u32[]{:S(2)}, u32[]{:S(2)}) collective-permute-start(bf16[1,224,128]{2,1,0:T(8,128)(2,1)S(1)} %get-tuple-element.23), channel_id=1, source_target_pairs={{0,32},{64,96},{128,160},{192,224},{256,288},{320,352},{384,416},{... | collective-permute-start | bytes 172040 | tf_op jit(solution)/shard_map/ppermute | solution.py:439
  11.7 12.6 %all-to-all-start = ((f32[16,2,128]{2,1,0:T(2,128)}), f32[16,2,128]{2,1,0:T(2,128)S(1)}, u32[]{:S(2)}, u32[]{:S(2)}) async-start(f32[16,2,128]{2,1,0:T(2,128)} %get-tuple-element.22), calls=%async_computation | async-start | bytes 32768 | tf_op jit(solution)/shard_map/all_to_all | solution.py:443
  24.3 2.0 %collective-permute-start.3 = (bf16[3,224,128]{2,1,0:T(8,128)(2,1)S(1)}, bf16[3,224,128]{2,1,0:T(8,128)(2,1)S(1)}, u32[]{:S(2)}, u32[]{:S(2)}) collective-permute-start(bf16[3,224,128]{2,1,0:T(8,128)(2,1)S(1)} %constant_dynamic-update-slice_fusion.own), channel_id=1, source_target_pairs={{0,1},{2,3},{4,5},{6,7},{8,9},{10,11},{12,13},{14,15},{16,17},{18,... | collective-permute-start | bytes 516104 | tf_op jit(solution)/shard_map/ppermute | solution.py:439
  26.3 3.5 %collective-permute-start.2 = (bf16[3,224,128]{2,1,0:T(8,128)(2,1)S(1)}, bf16[3,224,128]{2,1,0:T(8,128)(2,1)S(1)}, u32[]{:S(2)}, u32[]{:S(2)}) collective-permute-start(bf16[3,224,128]{2,1,0:T(8,128)(2,1)S(1)} %constant_dynamic-update-slice_fusion.own), channel_id=1, source_target_pairs={{1,2},{3,4},{5,6},{7,8},{9,10},{11,12},{13,14},{15,16},{17,18},{19... | collective-permute-start | bytes 516104 | tf_op jit(solution)/shard_map/ppermute | solution.py:439
  29.9 6.2 %shard_map.179 = (bf16[1152,2048]{1,0:T(8,128)(2,1)}, bf16[384,144]{1,0:T(8,128)(2,1)S(1)}, f32[384,256]{1,0:T(8,128)S(1)}, f32[192,128]{1,0:T(8,128)S(1)}) custom-call(s32[1]{0:T(128)} %bitcast.4.index, s32[16,256]{1,0:T(8,128)} %bitcast.35, s32[16,256]{1,0:T(8,128)} %bitcast.36, s32[16,24]{1,0:T(8,128)} %bitcast.38, s32[16,24]{1,0:T(8,128)} %bitcast.39, ...), custom_call_target="tpu_custom_call" | custom-call | flops 2147483648 | bytes 1048576 | tf_op jit(solution)/shard_map/pallas_call | solution.py:34
  36.0 1.9 %shard_map.177.window = f32[2,32,16,128]{3,2,1,0:T(8,128)S(1)} custom-call(s32[1]{0:T(128)} %bitcast.4.index, f32[31,63,2,128]{3,2,1,0:T(2,128)} %bitcast.28), custom_call_target="tpu_custom_call" | custom-call | flops 268435456 | bytes 1048576 | tf_op jit(solution)/shard_map/pallas_call | solution.py:34
  37.9 0.0 copy-start.2
  37.9 0.0 copy-start.3
  37.9 0.0 copy-start.4
  38.0 0.7 shard_map.178
  38.7 6.9 %all-to-all-start.1 = ((f32[32,2,128]{2,1,0:T(2,128)}), f32[32,2,128]{2,1,0:T(2,128)S(1)}, u32[]{:S(2)}, u32[]{:S(2)}) async-start(f32[32,2,128]{2,1,0:T(2,128)} %shard_map.178), calls=%async_computation.1 | async-start | bytes 65536 | tf_op jit(solution)/shard_map/all_to_all | solution.py:443
  45.6 4.3 %shard_map.180 = (f32[192,256]{1,0:T(8,128)S(1)}, f32[16,256]{1,0:T(8,128)S(1)}) custom-call(bf16[3,224,128]{2,1,0:T(8,128)(2,1)S(1)} %collective-permute-done.2.before, bf16[3,224,128]{2,1,0:T(8,128)(2,1)S(1)} %constant_dynamic-update-slice_fusion.own, bf16[3,224,128]{2,1,0:T(8,128)(2,1)S(1)} %collective-permute-done.3.after, ...), custom_call_target="tpu_custom_call" | custom-call | flops 2147483648 | bytes 1048576 | tf_op jit(solution)/shard_map/pallas_call | solution.py:34
  49.9 4.4 %all-to-all-done.1.partial = f32[32,2,128]{2,1,0:T(2,128)S(1)} async-done(((f32[32,2,128]{2,1,0:T(2,128)}), f32[32,2,128]{2,1,0:T(2,128)S(1)}, u32[]{:S(2)}, u32[]{:S(2)}) %all-to-all-start.1) | async-done | bytes 32800 | tf_op jit(solution)/shard_map/all_to_all | solution.py:443
  54.3 1.4 %shard_map.181 = (f32[192,128]{1,0:T(8,128)S(1)}, bf16[1,224,128]{2,1,0:T(8,128)(2,1)S(1)}, f32[16,2,128]{2,1,0:T(2,128)}) custom-call(f32[32,2,128]{2,1,0:T(2,128)S(1)} %all-to-all-done.1.partial, f32[192,256]{1,0:T(8,128)S(1)} %get-tuple-element.27.near, f32[16,256]{1,0:T(8,128)S(1)} %get-tuple-element.28.leaf_in, ...), custom_call_target="tpu_custom_call" | custom-call | flops 67108864 | bytes 1048576 | tf_op jit(solution)/shard_map/pallas_call | solution.py:34
  55.7 0.7 collective-permute-start.4
  56.4 3.9 %collective-permute-start.5 = (bf16[1,224,128]{2,1,0:T(8,128)(2,1)S(1)}, bf16[1,224,128]{2,1,0:T(8,128)(2,1)S(1)}, u32[]{:S(2)}, u32[]{:S(2)}) collective-permute-start(bf16[1,224,128]{2,1,0:T(8,128)(2,1)S(1)} %get-tuple-element.35), channel_id=1, source_target_pairs={{0,32},{64,96},{128,160},{192,224},{256,288},{320,352},{384,416},{... | collective-permute-start | bytes 172040 | tf_op jit(solution)/shard_map/ppermute | solution.py:439
  60.3 1.5 %collective-permute-done.5 = bf16[1,224,128]{2,1,0:T(8,128)(2,1)S(1)} collective-permute-done((bf16[1,224,128]{2,1,0:T(8,128)(2,1)S(1)}, bf16[1,224,128]{2,1,0:T(8,128)(2,1)S(1)}, u32[]{:S(2)}, u32[]{:S(2)}) %collective-permute-start.5) | collective-permute-done | bytes 57376 | tf_op jit(solution)/shard_map/ppermute | solution.py:439
  61.8 6.7 %collective-permute-start.7 = (bf16[3,224,128]{2,1,0:T(8,128)(2,1)S(1)}, bf16[3,224,128]{2,1,0:T(8,128)(2,1)S(1)}, u32[]{:S(2)}, u32[]{:S(2)}) collective-permute-start(bf16[3,224,128]{2,1,0:T(8,128)(2,1)S(1)} %constant_dynamic-update-slice_fusion.3.own), channel_id=1, source_target_pairs={{0,1},{2,3},{4,5},{6,7},{8,9},{10,11},{12,13},{14,15},{16,17},{18,... | collective-permute-start | bytes 516104 | tf_op jit(solution)/shard_map/ppermute | solution.py:439
  68.5 1.9 %collective-permute-start.6 = (bf16[3,224,128]{2,1,0:T(8,128)(2,1)S(1)}, bf16[3,224,128]{2,1,0:T(8,128)(2,1)S(1)}, u32[]{:S(2)}, u32[]{:S(2)}) collective-permute-start(bf16[3,224,128]{2,1,0:T(8,128)(2,1)S(1)} %constant_dynamic-update-slice_fusion.3.own), channel_id=1, source_target_pairs={{1,2},{3,4},{5,6},{7,8},{9,10},{11,12},{13,14},{15,16},{17,18},{19... | collective-permute-start | bytes 516104 | tf_op jit(solution)/shard_map/ppermute | solution.py:439
  70.5 11.3 %all-to-all-start.2 = ((f32[16,2,128]{2,1,0:T(2,128)}), f32[16,2,128]{2,1,0:T(2,128)S(1)}, u32[]{:S(2)}, u32[]{:S(2)}) async-start(f32[16,2,128]{2,1,0:T(2,128)} %get-tuple-element.34), calls=%async_computation.2 | async-start | bytes 32768 | tf_op jit(solution)/shard_map/all_to_all | solution.py:443
  81.7 0.1 shard_map.184.sums
  81.8 7.2 %all-to-all-done.2.columns = f32[16,2,128]{2,1,0:T(2,128)S(1)} async-done(((f32[16,2,128]{2,1,0:T(2,128)}), f32[16,2,128]{2,1,0:T(2,128)S(1)}, u32[]{:S(2)}, u32[]{:S(2)}) %all-to-all-start.2) | async-done | bytes 16416 | tf_op jit(solution)/shard_map/all_to_all | solution.py:443
  89.1 0.7 shard_map.182
  89.8 3.9 %all-to-all-start.3 = ((f32[32,2,128]{2,1,0:T(2,128)}), f32[32,2,128]{2,1,0:T(2,128)S(1)}, u32[]{:S(2)}, u32[]{:S(2)}) async-start(f32[32,2,128]{2,1,0:T(2,128)} %shard_map.182), calls=%async_computation.3 | async-start | bytes 65536 | tf_op jit(solution)/shard_map/all_to_all | solution.py:443
  93.7 4.3 %shard_map.183 = (f32[192,256]{1,0:T(8,128)S(1)}, f32[16,256]{1,0:T(8,128)S(1)}) custom-call(bf16[3,224,128]{2,1,0:T(8,128)(2,1)S(1)} %collective-permute-done.6.before, bf16[3,224,128]{2,1,0:T(8,128)(2,1)S(1)} %constant_dynamic-update-slice_fusion.3.own, bf16[3,224,128]{2,1,0:T(8,128)(2,1)S(1)} %collective-permute-done.7.after, ...), custom_call_target="tpu_custom_call" | custom-call | flops 2147483648 | bytes 1048576 | tf_op jit(solution)/shard_map/pallas_call | solution.py:34
  98.0 4.4 %all-to-all-done.3.partial = f32[32,2,128]{2,1,0:T(2,128)S(1)} async-done(((f32[32,2,128]{2,1,0:T(2,128)}), f32[32,2,128]{2,1,0:T(2,128)S(1)}, u32[]{:S(2)}, u32[]{:S(2)}) %all-to-all-start.3) | async-done | bytes 32800 | tf_op jit(solution)/shard_map/all_to_all | solution.py:443
  102.4 0.6 shard_map.185
  102.9 10.9 %all_to_all.30.parts = f32[16,1,128]{2,1,0:T(1,128)S(1)} all-to-all(f32[16,1,128]{2,1,0:T(1,128)S(1)} %get-tuple-element.38), channel_id=1, replica_groups=mesh['bx_0'=2,'bx_1'=8,'by_0'=4,'by_1'=4,'by_2'=2] {'bx_0','by_1','by_2'}, dimensions={0} | all-to-all | bytes 16384 | tf_op jit(solution)/shard_map/all_to_all | solution.py:443
  113.9 12.4 %all_to_all.31.parts = f32[32,1,128]{2,1,0:T(1,128)S(1)} all-to-all(f32[32,1,128]{2,1,0:T(1,128)S(1)} %shard_map.186), channel_id=1, replica_groups=mesh['bx_0'=2,'bx_1'=8,'by_0'=4,'by_1'=4,'by_2'=2] {'bx_1','by_0'}, dimensions={0} | all-to-all | bytes 32768 | tf_op jit(solution)/shard_map/all_to_all | solution.py:443
  126.3 0.9 shard_map.187
  (22 shorter events, 0.1 us)
Async XLA Ops:
  2.8 21.4 %collective-permute-start = (bf16[1,224,128]{2,1,0:T(8,128)(2,1)S(1)}, bf16[1,224,128]{2,1,0:T(8,128)(2,1)S(1)}, u32[]{:S(2)}, u32[]{:S(2)}) collective-permute-start(bf16[1,224,128]{2,1,0:T(8,128)(2,1)S(1)} %get-tuple-element.23), channel_id=1, source_target_pairs={{32,64},{96,128},{160,192},{224,256},{288,320},{352,384},{416,448}... | collective-permute-start | bytes 172040 | tf_op jit(solution)/shard_map/ppermute | solution.py:439
  3.5 20.8 %collective-permute-start.1 = (bf16[1,224,128]{2,1,0:T(8,128)(2,1)S(1)}, bf16[1,224,128]{2,1,0:T(8,128)(2,1)S(1)}, u32[]{:S(2)}, u32[]{:S(2)}) collective-permute-start(bf16[1,224,128]{2,1,0:T(8,128)(2,1)S(1)} %get-tuple-element.23), channel_id=1, source_target_pairs={{0,32},{64,96},{128,160},{192,224},{256,288},{320,352},{384,416},{... | collective-permute-start | bytes 172040 | tf_op jit(solution)/shard_map/ppermute | solution.py:439
  11.7 26.3 %all-to-all-start = ((f32[16,2,128]{2,1,0:T(2,128)}), f32[16,2,128]{2,1,0:T(2,128)S(1)}, u32[]{:S(2)}, u32[]{:S(2)}) async-start(f32[16,2,128]{2,1,0:T(2,128)} %get-tuple-element.22), calls=%async_computation | async-start | bytes 32768 | tf_op jit(solution)/shard_map/all_to_all | solution.py:443
  24.3 21.3 %collective-permute-start.3 = (bf16[3,224,128]{2,1,0:T(8,128)(2,1)S(1)}, bf16[3,224,128]{2,1,0:T(8,128)(2,1)S(1)}, u32[]{:S(2)}, u32[]{:S(2)}) collective-permute-start(bf16[3,224,128]{2,1,0:T(8,128)(2,1)S(1)} %constant_dynamic-update-slice_fusion.own), channel_id=1, source_target_pairs={{0,1},{2,3},{4,5},{6,7},{8,9},{10,11},{12,13},{14,15},{16,17},{18,... | collective-permute-start | bytes 516104 | tf_op jit(solution)/shard_map/ppermute | solution.py:439
  26.3 19.3 %collective-permute-start.2 = (bf16[3,224,128]{2,1,0:T(8,128)(2,1)S(1)}, bf16[3,224,128]{2,1,0:T(8,128)(2,1)S(1)}, u32[]{:S(2)}, u32[]{:S(2)}) collective-permute-start(bf16[3,224,128]{2,1,0:T(8,128)(2,1)S(1)} %constant_dynamic-update-slice_fusion.own), channel_id=1, source_target_pairs={{1,2},{3,4},{5,6},{7,8},{9,10},{11,12},{13,14},{15,16},{17,18},{19... | collective-permute-start | bytes 516104 | tf_op jit(solution)/shard_map/ppermute | solution.py:439
  37.9 16.4 %copy-start.1 = (bf16[2,96,128]{2,1,0:T(8,128)(2,1)S(1)}, bf16[2,96,128]{2,1,0:T(8,128)(2,1)}, u32[]{:S(2)}) copy-start(bf16[2,96,128]{2,1,0:T(8,128)(2,1)} %param.25) | copy-start | bytes 147460
  37.9 16.4 %copy-start.2 = (f32[16,128]{1,0:T(8,128)S(1)}, f32[16,128]{1,0:T(8,128)}, u32[]{:S(2)}) copy-start(f32[16,128]{1,0:T(8,128)} %constant.38.clone.leaf_sin) | copy-start | bytes 24580
  37.9 16.4 %copy-start.3 = (f32[16,128]{1,0:T(8,128)S(1)}, f32[16,128]{1,0:T(8,128)}, u32[]{:S(2)}) copy-start(f32[16,128]{1,0:T(8,128)} %constant.37.clone.leaf_cos) | copy-start | bytes 24580
  37.9 16.4 %copy-start.4 = (s32[1,1,128]{2,1,0:T(1,128)S(1)}, s32[1,1,128]{2,1,0:T(1,128)}, u32[]{:S(2)}) copy-start(s32[1,1,128]{2,1,0:T(1,128)} %param.20) | copy-start | bytes 1540
  37.9 43.8 %copy-start = (f32[2,96,1,1,128]{4,3,2,1,0:T(1,128)S(1)}, f32[2,96,1,1,128]{4,3,2,1,0:T(1,128)}, u32[]{:S(2)}) copy-start(f32[2,96,1,1,128]{4,3,2,1,0:T(1,128)} %param.17) | copy-start | bytes 294916
  38.7 15.6 %all-to-all-start.1 = ((f32[32,2,128]{2,1,0:T(2,128)}), f32[32,2,128]{2,1,0:T(2,128)S(1)}, u32[]{:S(2)}, u32[]{:S(2)}) async-start(f32[32,2,128]{2,1,0:T(2,128)} %shard_map.178), calls=%async_computation.1 | async-start | bytes 65536 | tf_op jit(solution)/shard_map/all_to_all | solution.py:443
  55.7 4.5 %collective-permute-start.4 = (bf16[1,224,128]{2,1,0:T(8,128)(2,1)S(1)}, bf16[1,224,128]{2,1,0:T(8,128)(2,1)S(1)}, u32[]{:S(2)}, u32[]{:S(2)}) collective-permute-start(bf16[1,224,128]{2,1,0:T(8,128)(2,1)S(1)} %get-tuple-element.35), channel_id=1, source_target_pairs={{32,64},{96,128},{160,192},{224,256},{288,320},{352,384},{416,448}... | collective-permute-start | bytes 172040 | tf_op jit(solution)/shard_map/ppermute | solution.py:439
  56.4 5.4 %collective-permute-start.5 = (bf16[1,224,128]{2,1,0:T(8,128)(2,1)S(1)}, bf16[1,224,128]{2,1,0:T(8,128)(2,1)S(1)}, u32[]{:S(2)}, u32[]{:S(2)}) collective-permute-start(bf16[1,224,128]{2,1,0:T(8,128)(2,1)S(1)} %get-tuple-element.35), channel_id=1, source_target_pairs={{0,32},{64,96},{128,160},{192,224},{256,288},{320,352},{384,416},{... | collective-permute-start | bytes 172040 | tf_op jit(solution)/shard_map/ppermute | solution.py:439
  61.8 31.8 %collective-permute-start.7 = (bf16[3,224,128]{2,1,0:T(8,128)(2,1)S(1)}, bf16[3,224,128]{2,1,0:T(8,128)(2,1)S(1)}, u32[]{:S(2)}, u32[]{:S(2)}) collective-permute-start(bf16[3,224,128]{2,1,0:T(8,128)(2,1)S(1)} %constant_dynamic-update-slice_fusion.3.own), channel_id=1, source_target_pairs={{0,1},{2,3},{4,5},{6,7},{8,9},{10,11},{12,13},{14,15},{16,17},{18,... | collective-permute-start | bytes 516104 | tf_op jit(solution)/shard_map/ppermute | solution.py:439
  68.5 25.1 %collective-permute-start.6 = (bf16[3,224,128]{2,1,0:T(8,128)(2,1)S(1)}, bf16[3,224,128]{2,1,0:T(8,128)(2,1)S(1)}, u32[]{:S(2)}, u32[]{:S(2)}) collective-permute-start(bf16[3,224,128]{2,1,0:T(8,128)(2,1)S(1)} %constant_dynamic-update-slice_fusion.3.own), channel_id=1, source_target_pairs={{1,2},{3,4},{5,6},{7,8},{9,10},{11,12},{13,14},{15,16},{17,18},{19... | collective-permute-start | bytes 516104 | tf_op jit(solution)/shard_map/ppermute | solution.py:439
  70.5 18.6 %all-to-all-start.2 = ((f32[16,2,128]{2,1,0:T(2,128)}), f32[16,2,128]{2,1,0:T(2,128)S(1)}, u32[]{:S(2)}, u32[]{:S(2)}) async-start(f32[16,2,128]{2,1,0:T(2,128)} %get-tuple-element.34), calls=%async_computation.2 | async-start | bytes 32768 | tf_op jit(solution)/shard_map/all_to_all | solution.py:443
  89.8 12.6 %all-to-all-start.3 = ((f32[32,2,128]{2,1,0:T(2,128)}), f32[32,2,128]{2,1,0:T(2,128)S(1)}, u32[]{:S(2)}, u32[]{:S(2)}) async-start(f32[32,2,128]{2,1,0:T(2,128)} %shard_map.182), calls=%async_computation.3 | async-start | bytes 65536 | tf_op jit(solution)/shard_map/all_to_all | solution.py:443

commit v6 on v5

--- a/solution.py
+++ b/solution.py
@@ -26,7 +26,9 @@
 
 
 def call(kernel, out_shape, operands, flops=0, **kw):
-    if "grid" not in kw:
+    if "specs" in kw:
+        kw["in_specs"] = kw.pop("specs")
+    elif "grid" not in kw:
         kw["in_specs"] = [
             pl.BlockSpec(memory_space=pltpu.SMEM if op.ndim == 1 else pltpu.VMEM)
             for op in operands
@@ -149,46 +151,12 @@
     return sources + flip_x * (2 - 2 * flat) * line + flip_y * (2 - 2 * side) * width
 
 
-def count_kernel(
-    index,
-    sources,
-    targets,
-    far_sources,
-    kinds,
-    transfer,
-    mie,
-    spread,
-    counts,
-    select,
-    chosen,
-    mie_full,
-    *,
-    across_y,
-):
-    flips = lax.rem(lax.div(index[0], across_y), 2), lax.rem(index[0], 2)
-
-    @pl.when(pl.program_id(0) == 0)
-    def _():
-        fill_tables(flips, far_sources, kinds, transfer, mie, spread, select, chosen, mie_full)
-
-    spheres = counts.shape[0] // 9
-    chunk = counts.shape[1] // spheres
-    for item in range(chunk):
-        at = pl.ds(pl.program_id(0) * chunk + item, 1)
-        source_hot = one_hot(9 * spheres, mirrored(sources[at, :], spheres, *flips))
-        target_hot = one_hot(spheres, targets[at, :])
-        counts[:, item * spheres : (item + 1) * spheres] = dot(
-            source_hot.astype(BF16), target_hot.astype(BF16), NT
-        ).astype(BF16)
-
-
-def fill_tables(flips, sources, classes, transfer, mie, spread, select, chosen, mie_full):
+def fill_tables(sources, classes, transfer, mie, spread, select, chosen, mie_full):
     boxes, entries = sources.shape
     row = lax.broadcasted_iota(jnp.int32, (boxes, boxes), 0)
     col = lax.broadcasted_iota(jnp.int32, (boxes, boxes), 1)
     unit = jnp.where(row == col, 1.0, 0.0).astype(BF16)
-    around = mirrored(sources[...], boxes, *flips)
-    around = dot(around.astype(F32).astype(BF16), unit, TN)
+    around = dot(sources[...].astype(F32).astype(BF16), unit, TN)
     kinds = dot(classes[...].astype(F32).astype(BF16), unit, TN)
     box_lane = lax.broadcasted_iota(jnp.int32, (entries, select.shape[1]), 1).astype(F32)
     kind_lane = lax.broadcasted_iota(jnp.int32, (entries, transfer.shape[0]), 1).astype(F32)
@@ -204,8 +172,29 @@
     mie_full[...] = dot(spread[...], mie[...], precision=HIGHEST)
 
 
-def window_kernel(index, transfer, window, *, near_z, near_x, groups, run, top_x, top_y):
+def window_kernel(
+    index,
+    transfer,
+    near_sources,
+    far_sources,
+    *rest,
+    spheres,
+    boxes,
+    near_z,
+    near_x,
+    groups,
+    run,
+    top_x,
+    top_y,
+):
+    copied = len(rest) // 2 - 1
+    window, near_out, far_out = rest[copied : copied + 3]
     row, col = lax.div(index[0], near_x * run), lax.rem(index[0], near_x * run)
+    flips = lax.rem(row, 2), lax.rem(col, 2)
+    near_out[...] = mirrored(near_sources[...], spheres, *flips)
+    far_out[...] = mirrored(far_sources[...], boxes, *flips)
+    for source, target in zip(rest[:copied], rest[copied + 3 :]):
+        target[...] = source[...]
     high, depth = lax.div(row, near_z), lax.rem(row, near_z)
     across, lane = lax.div(col, run), lax.rem(col, run)
     ordinal = lax.broadcasted_iota(jnp.int32, (run, 128), 0)
@@ -229,43 +218,104 @@
     partial[:, 1, :] = jnp.sum(imag * window[0] + real * window[1], axis=1)
 
 
-def near_kernel(before, own, after, counts, table, select, chosen, near, leaf_in, columns):
+def near_start(before, own, after, select, chosen, near, leaf_in, columns):
     coefs = near.shape[0] // 2
-    classes = table.shape[0]
     spheres = near.shape[1] // 2
     boxes, dirs = leaf_in.shape[0], leaf_in.shape[1] // 2
-
-    @pl.when(pl.program_id(0) == 0)
-    def _():
-        leaves = []
-        for row in range(3):
-            for col, part in enumerate((before, own, after)):
-                place = (row * 3 + col) * spheres
-                columns[:, place : place + spheres] = part[row, : 2 * coefs, :]
-                leaves.append(part[row, 2 * coefs :, :])
-        around = jnp.concatenate(
-            [
-                jnp.concatenate([leaf[:boxes] for leaf in leaves], axis=0),
-                jnp.concatenate([leaf[boxes:] for leaf in leaves], axis=0),
-            ],
-            axis=1,
-        )
-        picked = dot(select[...], around)
-        pick_real, pick_imag = picked[:, :dirs], picked[:, dirs:]
-        move_real, move_imag = chosen[:, :dirs], chosen[:, dirs:]
-        got_real = pick_real * move_real - pick_imag * move_imag
-        got_imag = pick_imag * move_real + pick_real * move_imag
-        leaf_in[:, :dirs] = jnp.sum(got_real.reshape(boxes, -1, dirs), axis=1)
-        leaf_in[:, dirs:] = jnp.sum(got_imag.reshape(boxes, -1, dirs), axis=1)
-        near[...] = jnp.zeros(near.shape, F32)
-
-    gathered = dot(columns[...], counts[...]).astype(BF16)
+    leaves = []
+    for row in range(3):
+        for col, part in enumerate((before, own, after)):
+            place = (row * 3 + col) * spheres
+            columns[:, place : place + spheres] = part[row, : 2 * coefs, :]
+            leaves.append(part[row, 2 * coefs :, :])
+    around = jnp.concatenate(
+        [
+            jnp.concatenate([leaf[:boxes] for leaf in leaves], axis=0),
+            jnp.concatenate([leaf[boxes:] for leaf in leaves], axis=0),
+        ],
+        axis=1,
+    )
+    picked = dot(select[...], around)
+    pick_real, pick_imag = picked[:, :dirs], picked[:, dirs:]
+    move_real, move_imag = chosen[:, :dirs], chosen[:, dirs:]
+    got_real = pick_real * move_real - pick_imag * move_imag
+    got_imag = pick_imag * move_real + pick_real * move_imag
+    leaf_in[:, :dirs] = jnp.sum(got_real.reshape(boxes, -1, dirs), axis=1)
+    leaf_in[:, dirs:] = jnp.sum(got_imag.reshape(boxes, -1, dirs), axis=1)
+    near[...] = jnp.zeros(near.shape, F32)
+
+
+def near_step(columns, counts, table, near):
+    coefs = near.shape[0] // 2
+    spheres = near.shape[1] // 2
+    gathered = dot(columns[...], counts).astype(BF16)
     total = near[...]
-    for item in range(classes):
+    for item in range(table.shape[0]):
         at = slice(item * spheres, (item + 1) * spheres)
         pair = jnp.concatenate([gathered[:coefs, at], gathered[coefs:, at]], axis=1)
         total = total + dot(table[item], pair)
     near[...] = total
+
+
+def near_kernel(before, own, after, counts, table, select, chosen, near, leaf_in, columns):
+    @pl.when(pl.program_id(0) == 0)
+    def _():
+        near_start(before, own, after, select, chosen, near, leaf_in, columns)
+
+    near_step(columns, counts[...], table, near)
+
+
+def both_kernel(
+    sources,
+    far_sources,
+    targets,
+    kinds,
+    transfer,
+    mie,
+    spread,
+    before,
+    own,
+    after,
+    table_hbm,
+    near,
+    leaf_in,
+    counts_hbm,
+    select,
+    chosen,
+    mie_full,
+    columns,
+    block,
+    table,
+    sems,
+):
+    groups, long, wide = block.shape
+    spheres = long // 9
+    chunk = wide // spheres
+    loading = pltpu.make_async_copy(table_hbm, table, sems.at[groups])
+    loading.start()
+    storing = []
+    for group in range(groups):
+        for item in range(chunk):
+            at = slice(group * chunk + item, group * chunk + item + 1)
+            source_hot = one_hot(long, sources[at, :]).astype(BF16)
+            target_hot = one_hot(spheres, targets[at, :]).astype(BF16)
+            block[group, :, item * spheres : (item + 1) * spheres] = dot(
+                source_hot, target_hot, NT
+            ).astype(BF16)
+        keep = pltpu.make_async_copy(
+            block.at[group], counts_hbm.at[:, pl.ds(group * wide, wide)], sems.at[group]
+        )
+        keep.start()
+        storing.append(keep)
+        if group == 0:
+            fill_tables(far_sources, kinds, transfer, mie, spread, select, chosen, mie_full)
+            near_start(before, own, after, select, chosen, near, leaf_in, columns)
+            loading.wait()
+        near_step(
+            columns, block[group], table.at[pl.ds(group * chunk, chunk)], near
+        )
+    for keep in storing:
+        keep.wait()
 
 
 def arrive(partial, near, leaf_in, receive, cosines, sines, member, leaf_cos, leaf_sin, mie_full):
@@ -497,43 +547,21 @@
     chunk = classes // 2
     whole = pl.BlockSpec(memory_space=pltpu.VMEM)
 
-    def prepare():
+    def windows():
         spread = mie_spread(coefs, mie.shape[1])
         zero = np.zeros_like(spread)
-        spread = jnp.asarray(np.block([[spread, zero], [zero, spread]]))
-        return call(
-            functools.partial(count_kernel, across_y=near_x * run),
-            (
-                shape((9 * spheres, classes * spheres), BF16),
-                kept((boxes * entries, 9 * boxes), BF16),
-                kept((boxes * entries, 2 * dirs)),
-                kept((rows, spheres)),
-            ),
-            (
-                index,
-                near_src.reshape(classes, pairs),
-                near_dst.reshape(classes, pairs),
-                far_src.reshape(boxes, entries),
-                far_cls.reshape(boxes, entries),
-                leaf_transfer,
-                mie.reshape(2 * mie.shape[1], spheres),
-                spread,
-            ),
-            flops=1 << 31,
-            grid=(classes // chunk,),
-            in_specs=[pl.BlockSpec(memory_space=pltpu.SMEM)] + [whole] * 7,
-            out_specs=(
-                pl.BlockSpec((9 * spheres, chunk * spheres), lambda k: (0, k)),
-                whole,
-                whole,
-                whole,
-            ),
+        copied = (
+            near_dst.reshape(classes, pairs),
+            far_cls.reshape(boxes, entries),
+            leaf_transfer,
+            mie.reshape(2 * mie.shape[1], spheres),
+            jnp.asarray(np.block([[spread, zero], [zero, spread]])),
         )
-
-    def windows():
         return call(
             functools.partial(
                 window_kernel,
+                spheres=spheres,
+                boxes=boxes,
                 near_z=near_z,
                 near_x=near_x,
                 groups=high_count,
@@ -541,12 +569,23 @@
                 top_x=high_count * near_z - 1,
                 top_y=near_x * run - 1,
             ),
-            kept((2, second_count, first_count, dirs)),
-            (index, coarse_transfer.transpose(1, 2, 0, 3)),
+            (
+                kept((2, second_count, first_count, dirs)),
+                kept((classes, pairs), jnp.int32),
+                kept((boxes, entries), jnp.int32),
+            )
+            + tuple(kept(item.shape, item.dtype) for item in copied),
+            (
+                index,
+                coarse_transfer.transpose(1, 2, 0, 3),
+                near_src.reshape(classes, pairs),
+                far_src.reshape(boxes, entries),
+            )
+            + copied,
             flops=1 << 28,
         )
 
-    def apply(halo, column, window, counts, select, chosen):
+    def apply(halo, column, window, prepared, tables=None):
         columns = exchange(column, FIRST)
         ahead = swap(halo, BX, 0)
         behind = swap(halo, BX, 1)
@@ -560,37 +599,57 @@
             1 << 24,
         )
         partial = exchange(partial, SECOND)
-        near, leaf_in = call(
-            near_kernel,
-            (kept((rows, 2 * spheres)), kept((boxes, 2 * dirs))),
-            (
-                resident(left),
-                resident(line),
-                resident(right),
-                counts,
-                near_table.reshape(classes, rows, coefs),
-                resident(select),
-                resident(chosen),
-            ),
-            flops=1 << 31,
-            grid=(classes // chunk,),
-            in_specs=[
-                whole,
-                whole,
-                whole,
-                pl.BlockSpec((9 * spheres, chunk * spheres), lambda k: (0, k)),
-                pl.BlockSpec((chunk, rows, coefs), lambda k: (k, 0, 0)),
-                whole,
-                whole,
-            ],
-            out_specs=(whole, whole),
-            scratch_shapes=[pltpu.VMEM((rows, 9 * spheres), BF16)],
-        )
-        return resident(partial), resident(near), resident(leaf_in)
-
-    window = windows()
-    counts, select, chosen, mie_full = prepare()
-    partial, near, leaf_in = apply(halo, column, window, counts, select, chosen)
+        lines = resident(left), resident(line), resident(right)
+        table = near_table.reshape(classes, rows, coefs)
+        sums = (kept((rows, 2 * spheres)), kept((boxes, 2 * dirs)))
+        if tables is None:
+            groups = classes // 4
+            any_spec = pl.BlockSpec(memory_space=pl.ANY)
+            near, leaf_in, *tables = call(
+                both_kernel,
+                sums
+                + (
+                    shape((9 * spheres, classes * spheres), BF16),
+                    kept((boxes * entries, 9 * boxes), BF16),
+                    kept((boxes * entries, 2 * dirs)),
+                    kept((rows, spheres)),
+                ),
+                tuple(resident(item) for item in prepared) + lines + (table,),
+                flops=1 << 31,
+                specs=[whole] * 10 + [any_spec],
+                out_specs=(whole, whole, any_spec, whole, whole, whole),
+                scratch_shapes=[
+                    pltpu.VMEM((rows, 9 * spheres), BF16),
+                    pltpu.VMEM((groups, 9 * spheres, 4 * spheres), BF16),
+                    pltpu.VMEM((classes, rows, coefs), BF16),
+                    pltpu.SemaphoreType.DMA((groups + 1,)),
+                ],
+            )
+        else:
+            counts, select, chosen, _ = tables
+            near, leaf_in = call(
+                near_kernel,
+                sums,
+                lines + (counts, table, resident(select), resident(chosen)),
+                flops=1 << 31,
+                grid=(classes // chunk,),
+                in_specs=[
+                    whole,
+                    whole,
+                    whole,
+                    pl.BlockSpec((9 * spheres, chunk * spheres), lambda k: (0, k)),
+                    pl.BlockSpec((chunk, rows, coefs), lambda k: (k, 0, 0)),
+                    whole,
+                    whole,
+                ],
+                out_specs=(whole, whole),
+                scratch_shapes=[pltpu.VMEM((rows, 9 * spheres), BF16)],
+            )
+        return (resident(partial), resident(near), resident(leaf_in)), tables
+
+    window, *prepared = windows()
+    inward, tables = apply(halo, column, window, prepared)
+    mie_full = tables[3]
     far = tuple(
         resident(item) for item in (receive, cosines, sines, box, leaf_cos, leaf_sin, mie_full)
     )
@@ -598,16 +657,16 @@
     once, halo, column = call(
         middle_kernel,
         (kept((rows, spheres)), halo_shape, column_shape),
-        (partial, near, leaf_in, resident(send)) + far,
+        inward + (resident(send),) + far,
         flops=1 << 26,
     )
     sums = call(sums_kernel, kept((1, 128)), (vector, resident(once)), 1 << 24)
-    partial, near, leaf_in = apply(halo, column, window, counts, select, chosen)
+    inward, _ = apply(halo, column, window, None, tables)
     once = resident(once)
     twice, everyone = call(
         last_kernel,
         (kept((rows, spheres)), kept((first_count, 1, 128))),
-        (vector, once, partial, near, leaf_in) + far + (resident(sums),),
+        (vector, once) + inward + far + (resident(sums),),
         flops=1 << 26,
     )
     everyone = call(

time: 128 us -> 128 us (level)
  waiting for transfers between devices: 17.6 us -> 21.6 us
  Pallas kernels: 23.3 us -> 20 us
    pallas_call x12 -> x11, Pallas kernels: 23.3 us -> 20 us  [call(): pl.pallas_call(kernel, out_shape=out_shape, interpret=INTERPRET, cost_est...]
    all_to_all x4, waiting for transfers between devices: 16 us -> 18.5 us  [exchange(): return lax.all_to_all(x, axes, split_axis=0, concat_axis=0, tiled=True)]
    ppermute x8, waiting for transfers between devices: 1.53 us -> 3.03 us  [swap(): return lax.ppermute(x, axes, pairs + [(j, i) for i, j in pairs])]
  transfers between devices with their start and end apart: 12 -> 12, of which waited for: 4 -> 6; matrix products, arithmetic and copies ran while one was open for 0% -> 0% of each run, Pallas kernels for 14% -> 12%
where the time goes in v6:
time: 128 us; the launch traced here: 127 us
  starting transfers between devices  60.9 us (48%)
  blocking collectives  23.7 us (19%)
  waiting for transfers between devices  21.6 us (17%)
  Pallas kernels  20 us (16%)
    all_to_all x4, starting transfers between devices, exchange(): return lax.all_to_all(x, axes, split_axis=0, concat_axis=0, tiled=True)  33.9 us
    ppermute x8, starting transfers between devices, swap(): return lax.ppermute(x, axes, pairs + [(j, i) for i, j in pairs])  27 us
    all_to_all x2, blocking collectives, exchange(): return lax.all_to_all(x, axes, split_axis=0, concat_axis=0, tiled=True)  23.7 us
    pallas_call x11, Pallas kernels, call(): pl.pallas_call(kernel, out_shape=out_shape, interpret=INTERPRET, cost_est...  20 us
    all_to_all x4, waiting for transfers between devices, exchange(): return lax.all_to_all(x, axes, split_axis=0, concat_axis=0, tiled=True)  18.5 us
    ppermute x8, waiting for transfers between devices, swap(): return lax.ppermute(x, axes, pairs + [(j, i) for i, j in pairs])  3.03 us
  transfers between devices with their start and end apart: 12, of which 6 were waited for; matrix products, arithmetic and copies ran while one was open for 0% of the time, Pallas kernels for 12%

profile of v6, /device:TPU:1, one launch (start us, length us, event | category | flops | bytes accessed | tf_op | source)
XLA Modules:
  0.0 127.1 jit_solution(13708164574566586074)
XLA Ops:
  0.6 2.2 %shard_map.176 = (bf16[1,224,128]{2,1,0:T(8,128)(2,1)S(1)}, f32[16,2,128]{2,1,0:T(2,128)}, f32[128,128]{1,0:T(8,128)S(1)}, f32[128,128]{1,0:T(8,128)S(1)}, bf16[256,96]{1,0:T(8,128)(2,1)S(1)}) custom-call(f32[192,128]{1,0:T(8,128)} %bitcast.19, bf16[2,96,128]{2,1,0:T(8,128)(2,1)} %bitcast.29, f32[3,1,128]{2,1,0:T(1,128)} %bitcast.35, ...), custom_call_target="tpu_custom_call" | custom-call | flops 67108864 | bytes 1048576 | tf_op jit(solution)/shard_map/pallas_call | solution.py:36
  2.8 0.7 collective-permute-start
  3.5 8.2 %collective-permute-start.1 = (bf16[1,224,128]{2,1,0:T(8,128)(2,1)S(1)}, bf16[1,224,128]{2,1,0:T(8,128)(2,1)S(1)}, u32[]{:S(2)}, u32[]{:S(2)}) collective-permute-start(bf16[1,224,128]{2,1,0:T(8,128)(2,1)S(1)} %get-tuple-element.39), channel_id=1, source_target_pairs={{0,32},{64,96},{128,160},{192,224},{256,288},{320,352},{384,416},{... | collective-permute-start | bytes 172040 | tf_op jit(solution)/shard_map/ppermute | solution.py:489
  11.7 1.5 %collective-permute-done.1 = bf16[1,224,128]{2,1,0:T(8,128)(2,1)S(1)} collective-permute-done((bf16[1,224,128]{2,1,0:T(8,128)(2,1)S(1)}, bf16[1,224,128]{2,1,0:T(8,128)(2,1)S(1)}, u32[]{:S(2)}, u32[]{:S(2)}) %collective-permute-start.1) | collective-permute-done | bytes 57376 | tf_op jit(solution)/shard_map/ppermute | solution.py:489
  13.2 4.9 %collective-permute-start.2 = (bf16[3,224,128]{2,1,0:T(8,128)(2,1)S(1)}, bf16[3,224,128]{2,1,0:T(8,128)(2,1)S(1)}, u32[]{:S(2)}, u32[]{:S(2)}) collective-permute-start(bf16[3,224,128]{2,1,0:T(8,128)(2,1)S(1)} %constant_dynamic-update-slice_fusion.own), channel_id=1, source_target_pairs={{1,2},{3,4},{5,6},{7,8},{9,10},{11,12},{13,14},{15,16},{17,18},{19... | collective-permute-start | bytes 516104 | tf_op jit(solution)/shard_map/ppermute | solution.py:489
  18.1 1.9 %collective-permute-start.3 = (bf16[3,224,128]{2,1,0:T(8,128)(2,1)S(1)}, bf16[3,224,128]{2,1,0:T(8,128)(2,1)S(1)}, u32[]{:S(2)}, u32[]{:S(2)}) collective-permute-start(bf16[3,224,128]{2,1,0:T(8,128)(2,1)S(1)} %constant_dynamic-update-slice_fusion.own), channel_id=1, source_target_pairs={{0,1},{2,3},{4,5},{6,7},{8,9},{10,11},{12,13},{14,15},{16,17},{18,... | collective-permute-start | bytes 516104 | tf_op jit(solution)/shard_map/ppermute | solution.py:489
  20.1 13.7 %all-to-all-start = ((f32[16,2,128]{2,1,0:T(2,128)}), f32[16,2,128]{2,1,0:T(2,128)S(1)}, u32[]{:S(2)}, u32[]{:S(2)}) async-start(f32[16,2,128]{2,1,0:T(2,128)} %get-tuple-element.30), calls=%async_computation | async-start | bytes 32768 | tf_op jit(solution)/shard_map/all_to_all | solution.py:493
  33.8 1.9 %shard_map.177 = (f32[2,32,16,128]{3,2,1,0:T(8,128)S(1)}, s32[16,256]{1,0:T(8,128)S(1)}, s32[16,24]{1,0:T(8,128)S(1)}, s32[16,256]{1,0:T(8,128)S(1)}, s32[16,24]...) custom-call(s32[1]{0:T(128)} %bitcast.4.index, ...), custom_call_target="tpu_custom_call" | custom-call | flops 268435456 | bytes 1048576 | tf_op jit(solution)/shard_map/pallas_call | solution.py:36
  35.7 0.0 copy-start.2
  35.8 0.0 copy-start.3
  35.8 5.3 %all-to-all-done.columns = f32[16,2,128]{2,1,0:T(2,128)S(1)} async-done(((f32[16,2,128]{2,1,0:T(2,128)}), f32[16,2,128]{2,1,0:T(2,128)S(1)}, u32[]{:S(2)}, u32[]{:S(2)}) %all-to-all-start) | async-done | bytes 16416 | tf_op jit(solution)/shard_map/all_to_all | solution.py:493
  41.1 0.7 shard_map.178
  41.9 5.4 %all-to-all-start.1 = ((f32[32,2,128]{2,1,0:T(2,128)}), f32[32,2,128]{2,1,0:T(2,128)S(1)}, u32[]{:S(2)}, u32[]{:S(2)}) async-start(f32[32,2,128]{2,1,0:T(2,128)} %shard_map.178), calls=%async_computation.1 | async-start | bytes 65536 | tf_op jit(solution)/shard_map/all_to_all | solution.py:493
  47.3 7.1 %shard_map.179 = (f32[192,256]{1,0:T(8,128)S(1)}, f32[16,256]{1,0:T(8,128)S(1)}, bf16[1152,2048]{1,0:T(8,128)(2,1)}, bf16[384,144]{1,0:T(8,128)(2,1)S(1)}, f32[3...) custom-call(s32[16,256]{1,0:T(8,128)S(1)} %get-tuple-element.32.sources, s32[16,24]{1,0:T(8,128)S(1)} %get-tuple-element.33.far_sources, ...), custom_call_target="tpu_custom_call" | custom-call | flops 2147483648 | bytes 1048576 | tf_op jit(solution)/shard_map/pallas_call | solution.py:36
  54.4 1.6 %all-to-all-done.1.partial = f32[32,2,128]{2,1,0:T(2,128)S(1)} async-done(((f32[32,2,128]{2,1,0:T(2,128)}), f32[32,2,128]{2,1,0:T(2,128)S(1)}, u32[]{:S(2)}, u32[]{:S(2)}) %all-to-all-start.1) | async-done | bytes 32800 | tf_op jit(solution)/shard_map/all_to_all | solution.py:493
  56.0 1.4 %shard_map.180 = (f32[192,128]{1,0:T(8,128)S(1)}, bf16[1,224,128]{2,1,0:T(8,128)(2,1)S(1)}, f32[16,2,128]{2,1,0:T(2,128)}) custom-call(f32[32,2,128]{2,1,0:T(2,128)S(1)} %all-to-all-done.1.partial, f32[192,256]{1,0:T(8,128)S(1)} %get-tuple-element.40.near, f32[16,256]{1,0:T(8,128)S(1)} %get-tuple-element.41.leaf_in, ...), custom_call_target="tpu_custom_call" | custom-call | flops 67108864 | bytes 1048576 | tf_op jit(solution)/shard_map/pallas_call | solution.py:36
  57.4 0.7 collective-permute-start.4
  58.1 4.0 %collective-permute-start.5 = (bf16[1,224,128]{2,1,0:T(8,128)(2,1)S(1)}, bf16[1,224,128]{2,1,0:T(8,128)(2,1)S(1)}, u32[]{:S(2)}, u32[]{:S(2)}) collective-permute-start(bf16[1,224,128]{2,1,0:T(8,128)(2,1)S(1)} %get-tuple-element.48), channel_id=1, source_target_pairs={{0,32},{64,96},{128,160},{192,224},{256,288},{320,352},{384,416},{... | collective-permute-start | bytes 172040 | tf_op jit(solution)/shard_map/ppermute | solution.py:489
  62.1 1.5 %collective-permute-done.5 = bf16[1,224,128]{2,1,0:T(8,128)(2,1)S(1)} collective-permute-done((bf16[1,224,128]{2,1,0:T(8,128)(2,1)S(1)}, bf16[1,224,128]{2,1,0:T(8,128)(2,1)S(1)}, u32[]{:S(2)}, u32[]{:S(2)}) %collective-permute-start.5) | collective-permute-done | bytes 57376 | tf_op jit(solution)/shard_map/ppermute | solution.py:489
  63.7 4.8 %collective-permute-start.6 = (bf16[3,224,128]{2,1,0:T(8,128)(2,1)S(1)}, bf16[3,224,128]{2,1,0:T(8,128)(2,1)S(1)}, u32[]{:S(2)}, u32[]{:S(2)}) collective-permute-start(bf16[3,224,128]{2,1,0:T(8,128)(2,1)S(1)} %constant_dynamic-update-slice_fusion.3.own), channel_id=1, source_target_pairs={{1,2},{3,4},{5,6},{7,8},{9,10},{11,12},{13,14},{15,16},{17,18},{19... | collective-permute-start | bytes 516104 | tf_op jit(solution)/shard_map/ppermute | solution.py:489
  68.5 1.9 %collective-permute-start.7 = (bf16[3,224,128]{2,1,0:T(8,128)(2,1)S(1)}, bf16[3,224,128]{2,1,0:T(8,128)(2,1)S(1)}, u32[]{:S(2)}, u32[]{:S(2)}) collective-permute-start(bf16[3,224,128]{2,1,0:T(8,128)(2,1)S(1)} %constant_dynamic-update-slice_fusion.3.own), channel_id=1, source_target_pairs={{0,1},{2,3},{4,5},{6,7},{8,9},{10,11},{12,13},{14,15},{16,17},{18,... | collective-permute-start | bytes 516104 | tf_op jit(solution)/shard_map/ppermute | solution.py:489
  70.4 9.3 %all-to-all-start.2 = ((f32[16,2,128]{2,1,0:T(2,128)}), f32[16,2,128]{2,1,0:T(2,128)S(1)}, u32[]{:S(2)}, u32[]{:S(2)}) async-start(f32[16,2,128]{2,1,0:T(2,128)} %get-tuple-element.47), calls=%async_computation.2 | async-start | bytes 32768 | tf_op jit(solution)/shard_map/all_to_all | solution.py:493
  79.7 0.1 shard_map.183.sums
  79.8 7.2 %all-to-all-done.2.columns = f32[16,2,128]{2,1,0:T(2,128)S(1)} async-done(((f32[16,2,128]{2,1,0:T(2,128)}), f32[16,2,128]{2,1,0:T(2,128)S(1)}, u32[]{:S(2)}, u32[]{:S(2)}) %all-to-all-start.2) | async-done | bytes 16416 | tf_op jit(solution)/shard_map/all_to_all | solution.py:493
  87.0 0.7 shard_map.181
  87.8 5.5 %all-to-all-start.3 = ((f32[32,2,128]{2,1,0:T(2,128)}), f32[32,2,128]{2,1,0:T(2,128)S(1)}, u32[]{:S(2)}, u32[]{:S(2)}) async-start(f32[32,2,128]{2,1,0:T(2,128)} %shard_map.181), calls=%async_computation.3 | async-start | bytes 65536 | tf_op jit(solution)/shard_map/all_to_all | solution.py:493
  93.3 4.3 %shard_map.182 = (f32[192,256]{1,0:T(8,128)S(1)}, f32[16,256]{1,0:T(8,128)S(1)}) custom-call(bf16[3,224,128]{2,1,0:T(8,128)(2,1)S(1)} %collective-permute-done.6.before, bf16[3,224,128]{2,1,0:T(8,128)(2,1)S(1)} %constant_dynamic-update-slice_fusion.3.own, bf16[3,224,128]{2,1,0:T(8,128)(2,1)S(1)} %collective-permute-done.7.after, ...), custom_call_target="tpu_custom_call" | custom-call | flops 2147483648 | bytes 1048576 | tf_op jit(solution)/shard_map/pallas_call | solution.py:36
  97.6 4.4 %all-to-all-done.3.partial = f32[32,2,128]{2,1,0:T(2,128)S(1)} async-done(((f32[32,2,128]{2,1,0:T(2,128)}), f32[32,2,128]{2,1,0:T(2,128)S(1)}, u32[]{:S(2)}, u32[]{:S(2)}) %all-to-all-start.3) | async-done | bytes 32800 | tf_op jit(solution)/shard_map/all_to_all | solution.py:493
  102.0 0.6 shard_map.184
  102.6 11.2 %all_to_all.30.parts = f32[16,1,128]{2,1,0:T(1,128)S(1)} all-to-all(f32[16,1,128]{2,1,0:T(1,128)S(1)} %get-tuple-element.54), channel_id=1, replica_groups=mesh['bx_0'=2,'bx_1'=8,'by_0'=4,'by_1'=4,'by_2'=2] {'bx_0','by_1','by_2'}, dimensions={0} | all-to-all | bytes 16384 | tf_op jit(solution)/shard_map/all_to_all | solution.py:493
  113.8 12.4 %all_to_all.31.parts = f32[32,1,128]{2,1,0:T(1,128)S(1)} all-to-all(f32[32,1,128]{2,1,0:T(1,128)S(1)} %shard_map.185), channel_id=1, replica_groups=mesh['bx_0'=2,'bx_1'=8,'by_0'=4,'by_1'=4,'by_2'=2] {'bx_1','by_0'}, dimensions={0} | all-to-all | bytes 32768 | tf_op jit(solution)/shard_map/all_to_all | solution.py:493
  126.3 0.9 shard_map.186
  (21 shorter events, 0.1 us)
Async XLA Ops:
  2.8 8.8 %collective-permute-start = (bf16[1,224,128]{2,1,0:T(8,128)(2,1)S(1)}, bf16[1,224,128]{2,1,0:T(8,128)(2,1)S(1)}, u32[]{:S(2)}, u32[]{:S(2)}) collective-permute-start(bf16[1,224,128]{2,1,0:T(8,128)(2,1)S(1)} %get-tuple-element.39), channel_id=1, source_target_pairs={{32,64},{96,128},{160,192},{224,256},{288,320},{352,384},{416,448}... | collective-permute-start | bytes 172040 | tf_op jit(solution)/shard_map/ppermute | solution.py:489
  3.5 9.7 %collective-permute-start.1 = (bf16[1,224,128]{2,1,0:T(8,128)(2,1)S(1)}, bf16[1,224,128]{2,1,0:T(8,128)(2,1)S(1)}, u32[]{:S(2)}, u32[]{:S(2)}) collective-permute-start(bf16[1,224,128]{2,1,0:T(8,128)(2,1)S(1)} %get-tuple-element.39), channel_id=1, source_target_pairs={{0,32},{64,96},{128,160},{192,224},{256,288},{320,352},{384,416},{... | collective-permute-start | bytes 172040 | tf_op jit(solution)/shard_map/ppermute | solution.py:489
  13.2 34.0 %collective-permute-start.2 = (bf16[3,224,128]{2,1,0:T(8,128)(2,1)S(1)}, bf16[3,224,128]{2,1,0:T(8,128)(2,1)S(1)}, u32[]{:S(2)}, u32[]{:S(2)}) collective-permute-start(bf16[3,224,128]{2,1,0:T(8,128)(2,1)S(1)} %constant_dynamic-update-slice_fusion.own), channel_id=1, source_target_pairs={{1,2},{3,4},{5,6},{7,8},{9,10},{11,12},{13,14},{15,16},{17,18},{19... | collective-permute-start | bytes 516104 | tf_op jit(solution)/shard_map/ppermute | solution.py:489
  18.1 29.1 %collective-permute-start.3 = (bf16[3,224,128]{2,1,0:T(8,128)(2,1)S(1)}, bf16[3,224,128]{2,1,0:T(8,128)(2,1)S(1)}, u32[]{:S(2)}, u32[]{:S(2)}) collective-permute-start(bf16[3,224,128]{2,1,0:T(8,128)(2,1)S(1)} %constant_dynamic-update-slice_fusion.own), channel_id=1, source_target_pairs={{0,1},{2,3},{4,5},{6,7},{8,9},{10,11},{12,13},{14,15},{16,17},{18,... | collective-permute-start | bytes 516104 | tf_op jit(solution)/shard_map/ppermute | solution.py:489
  20.1 21.0 %all-to-all-start = ((f32[16,2,128]{2,1,0:T(2,128)}), f32[16,2,128]{2,1,0:T(2,128)S(1)}, u32[]{:S(2)}, u32[]{:S(2)}) async-start(f32[16,2,128]{2,1,0:T(2,128)} %get-tuple-element.30), calls=%async_computation | async-start | bytes 32768 | tf_op jit(solution)/shard_map/all_to_all | solution.py:493
  35.7 20.2 %copy-start.1 = (bf16[2,96,128]{2,1,0:T(8,128)(2,1)S(1)}, bf16[2,96,128]{2,1,0:T(8,128)(2,1)}, u32[]{:S(2)}) copy-start(bf16[2,96,128]{2,1,0:T(8,128)(2,1)} %param.25) | copy-start | bytes 147460
  35.7 20.2 %copy-start.2 = (f32[16,128]{1,0:T(8,128)S(1)}, f32[16,128]{1,0:T(8,128)}, u32[]{:S(2)}) copy-start(f32[16,128]{1,0:T(8,128)} %constant.37.clone.leaf_cos) | copy-start | bytes 24580
  35.8 20.2 %copy-start.3 = (f32[16,128]{1,0:T(8,128)S(1)}, f32[16,128]{1,0:T(8,128)}, u32[]{:S(2)}) copy-start(f32[16,128]{1,0:T(8,128)} %constant.38.clone.leaf_sin) | copy-start | bytes 24580
  35.8 20.2 %copy-start.4 = (s32[1,1,128]{2,1,0:T(1,128)S(1)}, s32[1,1,128]{2,1,0:T(1,128)}, u32[]{:S(2)}) copy-start(s32[1,1,128]{2,1,0:T(1,128)} %param.20) | copy-start | bytes 1540
  41.1 38.6 %copy-start = (f32[2,96,1,1,128]{4,3,2,1,0:T(1,128)S(1)}, f32[2,96,1,1,128]{4,3,2,1,0:T(1,128)}, u32[]{:S(2)}) copy-start(f32[2,96,1,1,128]{4,3,2,1,0:T(1,128)} %param.17) | copy-start | bytes 294916
  41.9 14.1 %all-to-all-start.1 = ((f32[32,2,128]{2,1,0:T(2,128)}), f32[32,2,128]{2,1,0:T(2,128)S(1)}, u32[]{:S(2)}, u32[]{:S(2)}) async-start(f32[32,2,128]{2,1,0:T(2,128)} %shard_map.178), calls=%async_computation.1 | async-start | bytes 65536 | tf_op jit(solution)/shard_map/all_to_all | solution.py:493
  57.4 4.7 %collective-permute-start.4 = (bf16[1,224,128]{2,1,0:T(8,128)(2,1)S(1)}, bf16[1,224,128]{2,1,0:T(8,128)(2,1)S(1)}, u32[]{:S(2)}, u32[]{:S(2)}) collective-permute-start(bf16[1,224,128]{2,1,0:T(8,128)(2,1)S(1)} %get-tuple-element.48), channel_id=1, source_target_pairs={{32,64},{96,128},{160,192},{224,256},{288,320},{352,384},{416,448}... | collective-permute-start | bytes 172040 | tf_op jit(solution)/shard_map/ppermute | solution.py:489
  58.1 5.6 %collective-permute-start.5 = (bf16[1,224,128]{2,1,0:T(8,128)(2,1)S(1)}, bf16[1,224,128]{2,1,0:T(8,128)(2,1)S(1)}, u32[]{:S(2)}, u32[]{:S(2)}) collective-permute-start(bf16[1,224,128]{2,1,0:T(8,128)(2,1)S(1)} %get-tuple-element.48), channel_id=1, source_target_pairs={{0,32},{64,96},{128,160},{192,224},{256,288},{320,352},{384,416},{... | collective-permute-start | bytes 172040 | tf_op jit(solution)/shard_map/ppermute | solution.py:489
  63.7 29.6 %collective-permute-start.6 = (bf16[3,224,128]{2,1,0:T(8,128)(2,1)S(1)}, bf16[3,224,128]{2,1,0:T(8,128)(2,1)S(1)}, u32[]{:S(2)}, u32[]{:S(2)}) collective-permute-start(bf16[3,224,128]{2,1,0:T(8,128)(2,1)S(1)} %constant_dynamic-update-slice_fusion.3.own), channel_id=1, source_target_pairs={{1,2},{3,4},{5,6},{7,8},{9,10},{11,12},{13,14},{15,16},{17,18},{19... | collective-permute-start | bytes 516104 | tf_op jit(solution)/shard_map/ppermute | solution.py:489
  68.5 24.8 %collective-permute-start.7 = (bf16[3,224,128]{2,1,0:T(8,128)(2,1)S(1)}, bf16[3,224,128]{2,1,0:T(8,128)(2,1)S(1)}, u32[]{:S(2)}, u32[]{:S(2)}) collective-permute-start(bf16[3,224,128]{2,1,0:T(8,128)(2,1)S(1)} %constant_dynamic-update-slice_fusion.3.own), channel_id=1, source_target_pairs={{0,1},{2,3},{4,5},{6,7},{8,9},{10,11},{12,13},{14,15},{16,17},{18,... | collective-permute-start | bytes 516104 | tf_op jit(solution)/shard_map/ppermute | solution.py:489
  70.4 16.6 %all-to-all-start.2 = ((f32[16,2,128]{2,1,0:T(2,128)}), f32[16,2,128]{2,1,0:T(2,128)S(1)}, u32[]{:S(2)}, u32[]{:S(2)}) async-start(f32[16,2,128]{2,1,0:T(2,128)} %get-tuple-element.47), calls=%async_computation.2 | async-start | bytes 32768 | tf_op jit(solution)/shard_map/all_to_all | solution.py:493
  87.8 14.2 %all-to-all-start.3 = ((f32[32,2,128]{2,1,0:T(2,128)}), f32[32,2,128]{2,1,0:T(2,128)S(1)}, u32[]{:S(2)}, u32[]{:S(2)}) async-start(f32[32,2,128]{2,1,0:T(2,128)} %shard_map.181), calls=%async_computation.3 | async-start | bytes 65536 | tf_op jit(solution)/shard_map/all_to_all | solution.py:493

commit v7 on v6

--- a/solution.py
+++ b/solution.py
@@ -12,8 +12,8 @@
 
 BX = ("bx_0", "bx_1")
 BY = ("by_0", "by_1", "by_2")
-FIRST = ("bx_0", "by_1", "by_2")
-SECOND = ("bx_1", "by_0")
+SHORT = ("bx_0", "by_1", "by_2")
+LONG = ("by_0", "bx_1")
 
 HIGHEST = lax.Precision.HIGHEST
 KAPPA = 1.5
@@ -197,17 +197,17 @@
         target[...] = source[...]
     high, depth = lax.div(row, near_z), lax.rem(row, near_z)
     across, lane = lax.div(col, run), lax.rem(col, run)
-    ordinal = lax.broadcasted_iota(jnp.int32, (run, 128), 0)
-    for z in range(near_z):
-        for x in range(near_x):
-            start = (across - x) * run - lane + top_y
-            apart_y = jnp.abs(ordinal + (start - top_y))
-            for group in range(groups):
-                shift = (group - high) * near_z + depth - z
-                keep = (apart_y >= 2) | (jnp.abs(shift) >= 2)
+    ordinal = lax.broadcasted_iota(jnp.int32, (near_z, 128), 0)
+    for group in range(groups):
+        start = (high - group) * near_z - depth
+        apart_x = jnp.abs(ordinal + start)
+        for other in range(run):
+            for x in range(near_x):
+                shift = (x - across) * run + lane - other
+                keep = (apart_x >= 2) | (jnp.abs(shift) >= 2)
                 for part in range(2):
-                    rows = transfer[shift + top_x, pl.ds(start, run), part, :]
-                    window[part, z * near_x + x, group * run : (group + 1) * run, :] = jnp.where(
+                    rows = transfer[pl.ds(start + top_x, near_z), shift + top_y, part, :]
+                    window[part, group * run + other, x * near_z : (x + 1) * near_z, :] = jnp.where(
                         keep, rows, 0.0
                     )
 
@@ -517,7 +517,7 @@
     high_count, near_z = lax.axis_size("bx_0"), lax.axis_size("bx_1")
     near_x = lax.axis_size("by_0")
     run = lax.axis_size(("by_1", "by_2"))
-    first_count, second_count = lax.axis_size(FIRST), lax.axis_size(SECOND)
+    short_count, long_count = lax.axis_size(SHORT), lax.axis_size(LONG)
     index = lax.axis_index(BX + BY).astype(jnp.int32).reshape(1)
 
     planes = jnp.asarray(directions(dirs)[:, :, None].astype(np.float32))
@@ -531,7 +531,7 @@
     receive = receive.reshape(rows, dirs)
 
     halo_shape = kept((1, rows + 2 * boxes, spheres), BF16)
-    column_shape = kept((first_count, 2, dirs))
+    column_shape = kept((long_count, 2, dirs))
     halo, column, cosines, sines, send = call(
         first_kernel,
         (
@@ -570,7 +570,7 @@
                 top_y=near_x * run - 1,
             ),
             (
-                kept((2, second_count, first_count, dirs)),
+                kept((2, short_count, long_count, dirs)),
                 kept((classes, pairs), jnp.int32),
                 kept((boxes, entries), jnp.int32),
             )
@@ -586,7 +586,7 @@
         )
 
     def apply(halo, column, window, prepared, tables=None):
-        columns = exchange(column, FIRST)
+        columns = exchange(column, LONG)
         ahead = swap(halo, BX, 0)
         behind = swap(halo, BX, 1)
         line = jnp.concatenate([behind, halo, ahead], axis=0)
@@ -594,11 +594,11 @@
         left = swap(line, BY, 1)
         partial = call(
             coarse_kernel,
-            kept((second_count, 2, dirs)),
+            kept((short_count, 2, dirs)),
             (resident(columns), resident(window)),
             1 << 24,
         )
-        partial = exchange(partial, SECOND)
+        partial = exchange(partial, SHORT)
         lines = resident(left), resident(line), resident(right)
         table = near_table.reshape(classes, rows, coefs)
         sums = (kept((rows, 2 * spheres)), kept((boxes, 2 * dirs)))
@@ -665,17 +665,17 @@
     once = resident(once)
     twice, everyone = call(
         last_kernel,
-        (kept((rows, spheres)), kept((first_count, 1, 128))),
+        (kept((rows, spheres)), kept((short_count, 1, 128))),
         (vector, once) + inward + far + (resident(sums),),
         flops=1 << 26,
     )
     everyone = call(
-        relay_kernel, kept((second_count, 1, 128)), (resident(exchange(everyone, FIRST)),), 1 << 20
+        relay_kernel, kept((long_count, 1, 128)), (resident(exchange(everyone, SHORT)),), 1 << 20
     )
     solved, residual = call(
         solve_kernel,
         (shape((rows, spheres)), shape((rows, spheres))),
-        (resident(exchange(everyone, SECOND)), vector, once, resident(twice)),
+        (resident(exchange(everyone, LONG)), vector, once, resident(twice)),
         flops=1 << 24,
     )
     return solved.reshape(incident.shape), residual.reshape(incident.shape)

time: 128 us -> 130 us (1.016)
  starting transfers between devices: 60.9 us -> 64.3 us
    all_to_all x4, starting transfers between devices: 33.9 us -> 37.5 us  [exchange(): return lax.all_to_all(x, axes, split_axis=0, concat_axis=0, tiled=True)]
  transfers between devices with their start and end apart: 12 -> 12, of which waited for: 6 -> 6; matrix products, arithmetic and copies ran while one was open for 0% -> 0% of each run, Pallas kernels for 12% -> 11%
where the time goes in v7:
time: 130 us
  starting transfers between devices  64.3 us (49%)
  blocking collectives  22.7 us (17%)
  waiting for transfers between devices  21.7 us (17%)
  Pallas kernels  20 us (15%)
    all_to_all x4, starting transfers between devices, exchange(): return lax.all_to_all(x, axes, split_axis=0, concat_axis=0, tiled=True)  37.5 us
    ppermute x8, starting transfers between devices, swap(): return lax.ppermute(x, axes, pairs + [(j, i) for i, j in pairs])  26.8 us
    all_to_all x2, blocking collectives, exchange(): return lax.all_to_all(x, axes, split_axis=0, concat_axis=0, tiled=True)  22.7 us
    pallas_call x11, Pallas kernels, call(): pl.pallas_call(kernel, out_shape=out_shape, interpret=INTERPRET, cost_est...  20 us
    all_to_all x4, waiting for transfers between devices, exchange(): return lax.all_to_all(x, axes, split_axis=0, concat_axis=0, tiled=True)  18.7 us
    ppermute x8, waiting for transfers between devices, swap(): return lax.ppermute(x, axes, pairs + [(j, i) for i, j in pairs])  3.03 us
  transfers between devices with their start and end apart: 12, of which 6 were waited for; matrix products, arithmetic and copies ran while one was open for 0% of the time, Pallas kernels for 11%

profile of v7, /device:TPU:1, one launch (start us, length us, event | category | flops | bytes accessed | tf_op | source)
XLA Modules:
  0.0 129.7 jit_solution(17465000219775745863)
XLA Ops:
  0.6 2.2 %shard_map.176 = (bf16[1,224,128]{2,1,0:T(8,128)(2,1)S(1)}, f32[32,2,128]{2,1,0:T(2,128)}, f32[128,128]{1,0:T(8,128)S(1)}, f32[128,128]{1,0:T(8,128)S(1)}, bf16[256,96]{1,0:T(8,128)(2,1)S(1)}) custom-call(f32[192,128]{1,0:T(8,128)} %bitcast.19, bf16[2,96,128]{2,1,0:T(8,128)(2,1)} %bitcast.29, f32[3,1,128]{2,1,0:T(1,128)} %bitcast.35, ...), custom_call_target="tpu_custom_call" | custom-call | flops 67108864 | bytes 1048576 | tf_op jit(solution)/shard_map/pallas_call | solution.py:36
  2.9 0.7 collective-permute-start
  3.5 8.2 %collective-permute-start.1 = (bf16[1,224,128]{2,1,0:T(8,128)(2,1)S(1)}, bf16[1,224,128]{2,1,0:T(8,128)(2,1)S(1)}, u32[]{:S(2)}, u32[]{:S(2)}) collective-permute-start(bf16[1,224,128]{2,1,0:T(8,128)(2,1)S(1)} %get-tuple-element.39), channel_id=1, source_target_pairs={{0,32},{64,96},{128,160},{192,224},{256,288},{320,352},{384,416},{... | collective-permute-start | bytes 172040 | tf_op jit(solution)/shard_map/ppermute | solution.py:489
  11.7 1.5 %collective-permute-done.1 = bf16[1,224,128]{2,1,0:T(8,128)(2,1)S(1)} collective-permute-done((bf16[1,224,128]{2,1,0:T(8,128)(2,1)S(1)}, bf16[1,224,128]{2,1,0:T(8,128)(2,1)S(1)}, u32[]{:S(2)}, u32[]{:S(2)}) %collective-permute-start.1) | collective-permute-done | bytes 57376 | tf_op jit(solution)/shard_map/ppermute | solution.py:489
  13.2 5.1 %collective-permute-start.3 = (bf16[3,224,128]{2,1,0:T(8,128)(2,1)S(1)}, bf16[3,224,128]{2,1,0:T(8,128)(2,1)S(1)}, u32[]{:S(2)}, u32[]{:S(2)}) collective-permute-start(bf16[3,224,128]{2,1,0:T(8,128)(2,1)S(1)} %constant_dynamic-update-slice_fusion.own), channel_id=1, source_target_pairs={{0,1},{2,3},{4,5},{6,7},{8,9},{10,11},{12,13},{14,15},{16,17},{18,... | collective-permute-start | bytes 516104 | tf_op jit(solution)/shard_map/ppermute | solution.py:489
  18.4 1.9 %collective-permute-start.2 = (bf16[3,224,128]{2,1,0:T(8,128)(2,1)S(1)}, bf16[3,224,128]{2,1,0:T(8,128)(2,1)S(1)}, u32[]{:S(2)}, u32[]{:S(2)}) collective-permute-start(bf16[3,224,128]{2,1,0:T(8,128)(2,1)S(1)} %constant_dynamic-update-slice_fusion.own), channel_id=1, source_target_pairs={{1,2},{3,4},{5,6},{7,8},{9,10},{11,12},{13,14},{15,16},{17,18},{19... | collective-permute-start | bytes 516104 | tf_op jit(solution)/shard_map/ppermute | solution.py:489
  20.3 14.1 %all-to-all-start = ((f32[32,2,128]{2,1,0:T(2,128)}), f32[32,2,128]{2,1,0:T(2,128)S(1)}, u32[]{:S(2)}, u32[]{:S(2)}) async-start(f32[32,2,128]{2,1,0:T(2,128)} %get-tuple-element.30), calls=%async_computation | async-start | bytes 65536 | tf_op jit(solution)/shard_map/all_to_all | solution.py:493
  34.4 2.0 %shard_map.177 = (f32[2,16,32,128]{3,2,1,0:T(8,128)S(1)}, s32[16,256]{1,0:T(8,128)S(1)}, s32[16,24]{1,0:T(8,128)S(1)}, s32[16,256]{1,0:T(8,128)S(1)}, s32[16,24]...) custom-call(s32[1]{0:T(128)} %bitcast.4.index, ...), custom_call_target="tpu_custom_call" | custom-call | flops 268435456 | bytes 1048576 | tf_op jit(solution)/shard_map/pallas_call | solution.py:36
  36.4 0.0 copy-start.2
  36.4 0.0 copy-start.3
  36.4 6.7 %all-to-all-done.columns = f32[32,2,128]{2,1,0:T(2,128)S(1)} async-done(((f32[32,2,128]{2,1,0:T(2,128)}), f32[32,2,128]{2,1,0:T(2,128)S(1)}, u32[]{:S(2)}, u32[]{:S(2)}) %all-to-all-start) | async-done | bytes 32800 | tf_op jit(solution)/shard_map/all_to_all | solution.py:493
  43.2 0.7 shard_map.178
  43.9 7.2 %all-to-all-start.1 = ((f32[16,2,128]{2,1,0:T(2,128)}), f32[16,2,128]{2,1,0:T(2,128)S(1)}, u32[]{:S(2)}, u32[]{:S(2)}) async-start(f32[16,2,128]{2,1,0:T(2,128)} %shard_map.178), calls=%async_computation.1 | async-start | bytes 32768 | tf_op jit(solution)/shard_map/all_to_all | solution.py:493
  51.1 7.1 %shard_map.179 = (f32[192,256]{1,0:T(8,128)S(1)}, f32[16,256]{1,0:T(8,128)S(1)}, bf16[1152,2048]{1,0:T(8,128)(2,1)}, bf16[384,144]{1,0:T(8,128)(2,1)S(1)}, f32[3...) custom-call(s32[16,256]{1,0:T(8,128)S(1)} %get-tuple-element.32.sources, s32[16,24]{1,0:T(8,128)S(1)} %get-tuple-element.33.far_sources, ...), custom_call_target="tpu_custom_call" | custom-call | flops 2147483648 | bytes 1048576 | tf_op jit(solution)/shard_map/pallas_call | solution.py:36
  58.3 0.2 all-to-all-done.1.partial
  58.5 1.4 %shard_map.180 = (f32[192,128]{1,0:T(8,128)S(1)}, bf16[1,224,128]{2,1,0:T(8,128)(2,1)S(1)}, f32[32,2,128]{2,1,0:T(2,128)}) custom-call(f32[16,2,128]{2,1,0:T(2,128)S(1)} %all-to-all-done.1.partial, f32[192,256]{1,0:T(8,128)S(1)} %get-tuple-element.40.near, f32[16,256]{1,0:T(8,128)S(1)} %get-tuple-element.41.leaf_in, ...), custom_call_target="tpu_custom_call" | custom-call | flops 67108864 | bytes 1048576 | tf_op jit(solution)/shard_map/pallas_call | solution.py:36
  60.0 0.7 collective-permute-start.4
  60.6 3.9 %collective-permute-start.5 = (bf16[1,224,128]{2,1,0:T(8,128)(2,1)S(1)}, bf16[1,224,128]{2,1,0:T(8,128)(2,1)S(1)}, u32[]{:S(2)}, u32[]{:S(2)}) collective-permute-start(bf16[1,224,128]{2,1,0:T(8,128)(2,1)S(1)} %get-tuple-element.48), channel_id=1, source_target_pairs={{0,32},{64,96},{128,160},{192,224},{256,288},{320,352},{384,416},{... | collective-permute-start | bytes 172040 | tf_op jit(solution)/shard_map/ppermute | solution.py:489
  64.6 1.5 %collective-permute-done.5 = bf16[1,224,128]{2,1,0:T(8,128)(2,1)S(1)} collective-permute-done((bf16[1,224,128]{2,1,0:T(8,128)(2,1)S(1)}, bf16[1,224,128]{2,1,0:T(8,128)(2,1)S(1)}, u32[]{:S(2)}, u32[]{:S(2)}) %collective-permute-start.5) | collective-permute-done | bytes 57376 | tf_op jit(solution)/shard_map/ppermute | solution.py:489
  66.1 3.5 %collective-permute-start.7 = (bf16[3,224,128]{2,1,0:T(8,128)(2,1)S(1)}, bf16[3,224,128]{2,1,0:T(8,128)(2,1)S(1)}, u32[]{:S(2)}, u32[]{:S(2)}) collective-permute-start(bf16[3,224,128]{2,1,0:T(8,128)(2,1)S(1)} %constant_dynamic-update-slice_fusion.3.own), channel_id=1, source_target_pairs={{0,1},{2,3},{4,5},{6,7},{8,9},{10,11},{12,13},{14,15},{16,17},{18,... | collective-permute-start | bytes 516104 | tf_op jit(solution)/shard_map/ppermute | solution.py:489
  69.6 2.9 %collective-permute-start.6 = (bf16[3,224,128]{2,1,0:T(8,128)(2,1)S(1)}, bf16[3,224,128]{2,1,0:T(8,128)(2,1)S(1)}, u32[]{:S(2)}, u32[]{:S(2)}) collective-permute-start(bf16[3,224,128]{2,1,0:T(8,128)(2,1)S(1)} %constant_dynamic-update-slice_fusion.3.own), channel_id=1, source_target_pairs={{1,2},{3,4},{5,6},{7,8},{9,10},{11,12},{13,14},{15,16},{17,18},{19... | collective-permute-start | bytes 516104 | tf_op jit(solution)/shard_map/ppermute | solution.py:489
  72.5 9.9 %all-to-all-start.2 = ((f32[32,2,128]{2,1,0:T(2,128)}), f32[32,2,128]{2,1,0:T(2,128)S(1)}, u32[]{:S(2)}, u32[]{:S(2)}) async-start(f32[32,2,128]{2,1,0:T(2,128)} %get-tuple-element.47), calls=%async_computation.2 | async-start | bytes 65536 | tf_op jit(solution)/shard_map/all_to_all | solution.py:493
  82.4 0.1 shard_map.183.sums
  82.6 8.6 %all-to-all-done.2.columns = f32[32,2,128]{2,1,0:T(2,128)S(1)} async-done(((f32[32,2,128]{2,1,0:T(2,128)}), f32[32,2,128]{2,1,0:T(2,128)S(1)}, u32[]{:S(2)}, u32[]{:S(2)}) %all-to-all-start.2) | async-done | bytes 32800 | tf_op jit(solution)/shard_map/all_to_all | solution.py:493
  91.2 0.7 shard_map.181
  91.9 6.3 %all-to-all-start.3 = ((f32[16,2,128]{2,1,0:T(2,128)}), f32[16,2,128]{2,1,0:T(2,128)S(1)}, u32[]{:S(2)}, u32[]{:S(2)}) async-start(f32[16,2,128]{2,1,0:T(2,128)} %shard_map.181), calls=%async_computation.3 | async-start | bytes 32768 | tf_op jit(solution)/shard_map/all_to_all | solution.py:493
  98.2 4.3 %shard_map.182 = (f32[192,256]{1,0:T(8,128)S(1)}, f32[16,256]{1,0:T(8,128)S(1)}) custom-call(bf16[3,224,128]{2,1,0:T(8,128)(2,1)S(1)} %collective-permute-done.6.before, bf16[3,224,128]{2,1,0:T(8,128)(2,1)S(1)} %constant_dynamic-update-slice_fusion.3.own, bf16[3,224,128]{2,1,0:T(8,128)(2,1)S(1)} %collective-permute-done.7.after, ...), custom_call_target="tpu_custom_call" | custom-call | flops 2147483648 | bytes 1048576 | tf_op jit(solution)/shard_map/pallas_call | solution.py:36
  102.5 3.0 %all-to-all-done.3.partial = f32[16,2,128]{2,1,0:T(2,128)S(1)} async-done(((f32[16,2,128]{2,1,0:T(2,128)}), f32[16,2,128]{2,1,0:T(2,128)S(1)}, u32[]{:S(2)}, u32[]{:S(2)}) %all-to-all-start.3) | async-done | bytes 16416 | tf_op jit(solution)/shard_map/all_to_all | solution.py:493
  105.5 0.5 shard_map.184
  106.1 11.0 %all_to_all.30.parts = f32[16,1,128]{2,1,0:T(1,128)S(1)} all-to-all(f32[16,1,128]{2,1,0:T(1,128)S(1)} %get-tuple-element.54), channel_id=1, replica_groups=mesh['bx_0'=2,'bx_1'=8,'by_0'=4,'by_1'=4,'by_2'=2] {'bx_0','by_1','by_2'}, dimensions={0} | all-to-all | bytes 16384 | tf_op jit(solution)/shard_map/all_to_all | solution.py:493
  117.2 11.6 %all_to_all.31.parts = f32[32,1,128]{2,1,0:T(1,128)S(1)} all-to-all(f32[32,1,128]{2,1,0:T(1,128)S(1)} %shard_map.185), channel_id=1, replica_groups=mesh['bx_0'=2,'bx_1'=8,'by_0'=4,'by_1'=4,'by_2'=2] {'by_0','bx_1'}, dimensions={0} | all-to-all | bytes 32768 | tf_op jit(solution)/shard_map/all_to_all | solution.py:493
  128.8 0.9 shard_map.186
  (21 shorter events, 0.1 us)
Async XLA Ops:
  2.9 8.8 %collective-permute-start = (bf16[1,224,128]{2,1,0:T(8,128)(2,1)S(1)}, bf16[1,224,128]{2,1,0:T(8,128)(2,1)S(1)}, u32[]{:S(2)}, u32[]{:S(2)}) collective-permute-start(bf16[1,224,128]{2,1,0:T(8,128)(2,1)S(1)} %get-tuple-element.39), channel_id=1, source_target_pairs={{32,64},{96,128},{160,192},{224,256},{288,320},{352,384},{416,448}... | collective-permute-start | bytes 172040 | tf_op jit(solution)/shard_map/ppermute | solution.py:489
  3.5 9.7 %collective-permute-start.1 = (bf16[1,224,128]{2,1,0:T(8,128)(2,1)S(1)}, bf16[1,224,128]{2,1,0:T(8,128)(2,1)S(1)}, u32[]{:S(2)}, u32[]{:S(2)}) collective-permute-start(bf16[1,224,128]{2,1,0:T(8,128)(2,1)S(1)} %get-tuple-element.39), channel_id=1, source_target_pairs={{0,32},{64,96},{128,160},{192,224},{256,288},{320,352},{384,416},{... | collective-permute-start | bytes 172040 | tf_op jit(solution)/shard_map/ppermute | solution.py:489
  13.2 37.9 %collective-permute-start.3 = (bf16[3,224,128]{2,1,0:T(8,128)(2,1)S(1)}, bf16[3,224,128]{2,1,0:T(8,128)(2,1)S(1)}, u32[]{:S(2)}, u32[]{:S(2)}) collective-permute-start(bf16[3,224,128]{2,1,0:T(8,128)(2,1)S(1)} %constant_dynamic-update-slice_fusion.own), channel_id=1, source_target_pairs={{0,1},{2,3},{4,5},{6,7},{8,9},{10,11},{12,13},{14,15},{16,17},{18,... | collective-permute-start | bytes 516104 | tf_op jit(solution)/shard_map/ppermute | solution.py:489
  18.4 32.8 %collective-permute-start.2 = (bf16[3,224,128]{2,1,0:T(8,128)(2,1)S(1)}, bf16[3,224,128]{2,1,0:T(8,128)(2,1)S(1)}, u32[]{:S(2)}, u32[]{:S(2)}) collective-permute-start(bf16[3,224,128]{2,1,0:T(8,128)(2,1)S(1)} %constant_dynamic-update-slice_fusion.own), channel_id=1, source_target_pairs={{1,2},{3,4},{5,6},{7,8},{9,10},{11,12},{13,14},{15,16},{17,18},{19... | collective-permute-start | bytes 516104 | tf_op jit(solution)/shard_map/ppermute | solution.py:489
  20.3 22.9 %all-to-all-start = ((f32[32,2,128]{2,1,0:T(2,128)}), f32[32,2,128]{2,1,0:T(2,128)S(1)}, u32[]{:S(2)}, u32[]{:S(2)}) async-start(f32[32,2,128]{2,1,0:T(2,128)} %get-tuple-element.30), calls=%async_computation | async-start | bytes 65536 | tf_op jit(solution)/shard_map/all_to_all | solution.py:493
  36.4 22.1 %copy-start.1 = (bf16[2,96,128]{2,1,0:T(8,128)(2,1)S(1)}, bf16[2,96,128]{2,1,0:T(8,128)(2,1)}, u32[]{:S(2)}) copy-start(bf16[2,96,128]{2,1,0:T(8,128)(2,1)} %param.25) | copy-start | bytes 147460
  36.4 22.1 %copy-start.2 = (f32[16,128]{1,0:T(8,128)S(1)}, f32[16,128]{1,0:T(8,128)}, u32[]{:S(2)}) copy-start(f32[16,128]{1,0:T(8,128)} %constant.38.clone.leaf_sin) | copy-start | bytes 24580
  36.4 22.1 %copy-start.3 = (f32[16,128]{1,0:T(8,128)S(1)}, f32[16,128]{1,0:T(8,128)}, u32[]{:S(2)}) copy-start(f32[16,128]{1,0:T(8,128)} %constant.37.clone.leaf_cos) | copy-start | bytes 24580
  36.4 22.1 %copy-start.4 = (s32[1,1,128]{2,1,0:T(1,128)S(1)}, s32[1,1,128]{2,1,0:T(1,128)}, u32[]{:S(2)}) copy-start(s32[1,1,128]{2,1,0:T(1,128)} %param.20) | copy-start | bytes 1540
  43.2 39.2 %copy-start = (f32[2,96,1,1,128]{4,3,2,1,0:T(1,128)S(1)}, f32[2,96,1,1,128]{4,3,2,1,0:T(1,128)}, u32[]{:S(2)}) copy-start(f32[2,96,1,1,128]{4,3,2,1,0:T(1,128)} %param.17) | copy-start | bytes 294916
  43.9 14.6 %all-to-all-start.1 = ((f32[16,2,128]{2,1,0:T(2,128)}), f32[16,2,128]{2,1,0:T(2,128)S(1)}, u32[]{:S(2)}, u32[]{:S(2)}) async-start(f32[16,2,128]{2,1,0:T(2,128)} %shard_map.178), calls=%async_computation.1 | async-start | bytes 32768 | tf_op jit(solution)/shard_map/all_to_all | solution.py:493
  60.0 4.6 %collective-permute-start.4 = (bf16[1,224,128]{2,1,0:T(8,128)(2,1)S(1)}, bf16[1,224,128]{2,1,0:T(8,128)(2,1)S(1)}, u32[]{:S(2)}, u32[]{:S(2)}) collective-permute-start(bf16[1,224,128]{2,1,0:T(8,128)(2,1)S(1)} %get-tuple-element.48), channel_id=1, source_target_pairs={{32,64},{96,128},{160,192},{224,256},{288,320},{352,384},{416,448}... | collective-permute-start | bytes 172040 | tf_op jit(solution)/shard_map/ppermute | solution.py:489
  60.6 5.5 %collective-permute-start.5 = (bf16[1,224,128]{2,1,0:T(8,128)(2,1)S(1)}, bf16[1,224,128]{2,1,0:T(8,128)(2,1)S(1)}, u32[]{:S(2)}, u32[]{:S(2)}) collective-permute-start(bf16[1,224,128]{2,1,0:T(8,128)(2,1)S(1)} %get-tuple-element.48), channel_id=1, source_target_pairs={{0,32},{64,96},{128,160},{192,224},{256,288},{320,352},{384,416},{... | collective-permute-start | bytes 172040 | tf_op jit(solution)/shard_map/ppermute | solution.py:489
  66.1 32.1 %collective-permute-start.7 = (bf16[3,224,128]{2,1,0:T(8,128)(2,1)S(1)}, bf16[3,224,128]{2,1,0:T(8,128)(2,1)S(1)}, u32[]{:S(2)}, u32[]{:S(2)}) collective-permute-start(bf16[3,224,128]{2,1,0:T(8,128)(2,1)S(1)} %constant_dynamic-update-slice_fusion.3.own), channel_id=1, source_target_pairs={{0,1},{2,3},{4,5},{6,7},{8,9},{10,11},{12,13},{14,15},{16,17},{18,... | collective-permute-start | bytes 516104 | tf_op jit(solution)/shard_map/ppermute | solution.py:489
  69.6 28.7 %collective-permute-start.6 = (bf16[3,224,128]{2,1,0:T(8,128)(2,1)S(1)}, bf16[3,224,128]{2,1,0:T(8,128)(2,1)S(1)}, u32[]{:S(2)}, u32[]{:S(2)}) collective-permute-start(bf16[3,224,128]{2,1,0:T(8,128)(2,1)S(1)} %constant_dynamic-update-slice_fusion.3.own), channel_id=1, source_target_pairs={{1,2},{3,4},{5,6},{7,8},{9,10},{11,12},{13,14},{15,16},{17,18},{19... | collective-permute-start | bytes 516104 | tf_op jit(solution)/shard_map/ppermute | solution.py:489
  72.5 18.7 %all-to-all-start.2 = ((f32[32,2,128]{2,1,0:T(2,128)}), f32[32,2,128]{2,1,0:T(2,128)S(1)}, u32[]{:S(2)}, u32[]{:S(2)}) async-start(f32[32,2,128]{2,1,0:T(2,128)} %get-tuple-element.47), calls=%async_computation.2 | async-start | bytes 65536 | tf_op jit(solution)/shard_map/all_to_all | solution.py:493
  91.9 13.6 %all-to-all-start.3 = ((f32[16,2,128]{2,1,0:T(2,128)}), f32[16,2,128]{2,1,0:T(2,128)S(1)}, u32[]{:S(2)}, u32[]{:S(2)}) async-start(f32[16,2,128]{2,1,0:T(2,128)} %shard_map.181), calls=%async_computation.3 | async-start | bytes 32768 | tf_op jit(solution)/shard_map/all_to_all | solution.py:493

commit v8 on v6

--- a/solution.py
+++ b/solution.py
@@ -187,16 +187,21 @@
     top_x,
     top_y,
 ):
+    *rest, held, sem = rest
     copied = len(rest) // 2 - 1
     window, near_out, far_out = rest[copied : copied + 3]
     row, col = lax.div(index[0], near_x * run), lax.rem(index[0], near_x * run)
     flips = lax.rem(row, 2), lax.rem(col, 2)
+    high, depth = lax.div(row, near_z), lax.rem(row, near_z)
+    across, lane = lax.div(col, run), lax.rem(col, run)
+    first_shift = depth - high * near_z - (near_z - 1)
+    fetch = pltpu.make_async_copy(transfer.at[pl.ds(first_shift + top_x, held.shape[0])], held, sem)
+    fetch.start()
     near_out[...] = mirrored(near_sources[...], spheres, *flips)
     far_out[...] = mirrored(far_sources[...], boxes, *flips)
     for source, target in zip(rest[:copied], rest[copied + 3 :]):
         target[...] = source[...]
-    high, depth = lax.div(row, near_z), lax.rem(row, near_z)
-    across, lane = lax.div(col, run), lax.rem(col, run)
+    fetch.wait()
     ordinal = lax.broadcasted_iota(jnp.int32, (run, 128), 0)
     for z in range(near_z):
         for x in range(near_x):
@@ -206,7 +211,7 @@
                 shift = (group - high) * near_z + depth - z
                 keep = (apart_y >= 2) | (jnp.abs(shift) >= 2)
                 for part in range(2):
-                    rows = transfer[shift + top_x, pl.ds(start, run), part, :]
+                    rows = held[group * near_z + near_z - 1 - z, pl.ds(start, run), part, :]
                     window[part, z * near_x + x, group * run : (group + 1) * run, :] = jnp.where(
                         keep, rows, 0.0
                     )
@@ -517,6 +522,7 @@
     high_count, near_z = lax.axis_size("bx_0"), lax.axis_size("bx_1")
     near_x = lax.axis_size("by_0")
     run = lax.axis_size(("by_1", "by_2"))
+    across_x = high_count * near_z
     first_count, second_count = lax.axis_size(FIRST), lax.axis_size(SECOND)
     index = lax.axis_index(BX + BY).astype(jnp.int32).reshape(1)
 
@@ -583,6 +589,12 @@
             )
             + copied,
             flops=1 << 28,
+            specs=[pl.BlockSpec(memory_space=pltpu.SMEM), pl.BlockSpec(memory_space=pl.ANY)]
+            + [whole] * (2 + len(copied)),
+            scratch_shapes=[
+                pltpu.VMEM((across_x, coarse_transfer.shape[2], 2, dirs), F32),
+                pltpu.SemaphoreType.DMA,
+            ],
         )
 
     def apply(halo, column, window, prepared, tables=None):
@@ -665,17 +677,17 @@
     once = resident(once)
     twice, everyone = call(
         last_kernel,
-        (kept((rows, spheres)), kept((first_count, 1, 128))),
+        (kept((rows, spheres)), kept((second_count, 1, 128))),
         (vector, once) + inward + far + (resident(sums),),
         flops=1 << 26,
     )
     everyone = call(
-        relay_kernel, kept((second_count, 1, 128)), (resident(exchange(everyone, FIRST)),), 1 << 20
+        relay_kernel, kept((first_count, 1, 128)), (resident(exchange(everyone, SECOND)),), 1 << 20
     )
     solved, residual = call(
         solve_kernel,
         (shape((rows, spheres)), shape((rows, spheres))),
-        (resident(exchange(everyone, SECOND)), vector, once, resident(twice)),
+        (resident(exchange(everyone, FIRST)), vector, once, resident(twice)),
         flops=1 << 24,
     )
     return solved.reshape(incident.shape), residual.reshape(incident.shape)

time: 128 us -> 129 us (level)
  blocking collectives: 23.7 us -> 25.1 us
    all_to_all x2, blocking collectives: 23.7 us -> 25.1 us  [exchange(): return lax.all_to_all(x, axes, split_axis=0, concat_axis=0, tiled=True)]
where the time goes in v8:
time: 129 us
  starting transfers between devices  60.9 us (47%)
  blocking collectives  25.1 us (19%)
  waiting for transfers between devices  21 us (16%)
  Pallas kernels  20.6 us (16%)
    all_to_all x4, starting transfers between devices, exchange(): return lax.all_to_all(x, axes, split_axis=0, concat_axis=0, tiled=True)  33.9 us
    ppermute x8, starting transfers between devices, swap(): return lax.ppermute(x, axes, pairs + [(j, i) for i, j in pairs])  27 us
    all_to_all x2, blocking collectives, exchange(): return lax.all_to_all(x, axes, split_axis=0, concat_axis=0, tiled=True)  25.1 us
    pallas_call x11, Pallas kernels, call(): pl.pallas_call(kernel, out_shape=out_shape, interpret=INTERPRET, cost_est...  20.6 us
    all_to_all x4, waiting for transfers between devices, exchange(): return lax.all_to_all(x, axes, split_axis=0, concat_axis=0, tiled=True)  17.9 us
    ppermute x8, waiting for transfers between devices, swap(): return lax.ppermute(x, axes, pairs + [(j, i) for i, j in pairs])  3.03 us
  transfers between devices with their start and end apart: 12, of which 6 were waited for; matrix products, arithmetic and copies ran while one was open for 0% of the time, Pallas kernels for 12%

profile of v8, /device:TPU:1, one launch (start us, length us, event | category | flops | bytes accessed | tf_op | source)
XLA Modules:
  0.0 128.6 jit_solution(18356501327233909065)
XLA Ops:
  0.6 2.2 %shard_map.176 = (bf16[1,224,128]{2,1,0:T(8,128)(2,1)S(1)}, f32[16,2,128]{2,1,0:T(2,128)}, f32[128,128]{1,0:T(8,128)S(1)}, f32[128,128]{1,0:T(8,128)S(1)}, bf16[256,96]{1,0:T(8,128)(2,1)S(1)}) custom-call(f32[192,128]{1,0:T(8,128)} %bitcast.19, bf16[2,96,128]{2,1,0:T(8,128)(2,1)} %bitcast.29, f32[3,1,128]{2,1,0:T(1,128)} %bitcast.35, ...), custom_call_target="tpu_custom_call" | custom-call | flops 67108864 | bytes 1048576 | tf_op jit(solution)/shard_map/pallas_call | solution.py:36
  2.8 0.7 collective-permute-start
  3.5 8.2 %collective-permute-start.1 = (bf16[1,224,128]{2,1,0:T(8,128)(2,1)S(1)}, bf16[1,224,128]{2,1,0:T(8,128)(2,1)S(1)}, u32[]{:S(2)}, u32[]{:S(2)}) collective-permute-start(bf16[1,224,128]{2,1,0:T(8,128)(2,1)S(1)} %get-tuple-element.39), channel_id=1, source_target_pairs={{0,32},{64,96},{128,160},{192,224},{256,288},{320,352},{384,416},{... | collective-permute-start | bytes 172040 | tf_op jit(solution)/shard_map/ppermute | solution.py:494
  11.7 1.5 %collective-permute-done.1 = bf16[1,224,128]{2,1,0:T(8,128)(2,1)S(1)} collective-permute-done((bf16[1,224,128]{2,1,0:T(8,128)(2,1)S(1)}, bf16[1,224,128]{2,1,0:T(8,128)(2,1)S(1)}, u32[]{:S(2)}, u32[]{:S(2)}) %collective-permute-start.1) | collective-permute-done | bytes 57376 | tf_op jit(solution)/shard_map/ppermute | solution.py:494
  13.2 4.9 %collective-permute-start.2 = (bf16[3,224,128]{2,1,0:T(8,128)(2,1)S(1)}, bf16[3,224,128]{2,1,0:T(8,128)(2,1)S(1)}, u32[]{:S(2)}, u32[]{:S(2)}) collective-permute-start(bf16[3,224,128]{2,1,0:T(8,128)(2,1)S(1)} %constant_dynamic-update-slice_fusion.own), channel_id=1, source_target_pairs={{1,2},{3,4},{5,6},{7,8},{9,10},{11,12},{13,14},{15,16},{17,18},{19... | collective-permute-start | bytes 516104 | tf_op jit(solution)/shard_map/ppermute | solution.py:494
  18.1 1.9 %collective-permute-start.3 = (bf16[3,224,128]{2,1,0:T(8,128)(2,1)S(1)}, bf16[3,224,128]{2,1,0:T(8,128)(2,1)S(1)}, u32[]{:S(2)}, u32[]{:S(2)}) collective-permute-start(bf16[3,224,128]{2,1,0:T(8,128)(2,1)S(1)} %constant_dynamic-update-slice_fusion.own), channel_id=1, source_target_pairs={{0,1},{2,3},{4,5},{6,7},{8,9},{10,11},{12,13},{14,15},{16,17},{18,... | collective-permute-start | bytes 516104 | tf_op jit(solution)/shard_map/ppermute | solution.py:494
  20.1 13.7 %all-to-all-start = ((f32[16,2,128]{2,1,0:T(2,128)}), f32[16,2,128]{2,1,0:T(2,128)S(1)}, u32[]{:S(2)}, u32[]{:S(2)}) async-start(f32[16,2,128]{2,1,0:T(2,128)} %get-tuple-element.30), calls=%async_computation | async-start | bytes 32768 | tf_op jit(solution)/shard_map/all_to_all | solution.py:498
  33.8 2.5 %shard_map.177 = (f32[2,32,16,128]{3,2,1,0:T(8,128)S(1)}, s32[16,256]{1,0:T(8,128)S(1)}, s32[16,24]{1,0:T(8,128)S(1)}, s32[16,256]{1,0:T(8,128)S(1)}, s32[16,24]...) custom-call(s32[1]{0:T(128)} %bitcast.4.index, ...), custom_call_target="tpu_custom_call" | custom-call | flops 268435456 | bytes 1048576 | tf_op jit(solution)/shard_map/pallas_call | solution.py:36
  36.3 0.0 copy-start.2
  36.3 0.0 copy-start.3
  36.4 4.7 %all-to-all-done.columns = f32[16,2,128]{2,1,0:T(2,128)S(1)} async-done(((f32[16,2,128]{2,1,0:T(2,128)}), f32[16,2,128]{2,1,0:T(2,128)S(1)}, u32[]{:S(2)}, u32[]{:S(2)}) %all-to-all-start) | async-done | bytes 16416 | tf_op jit(solution)/shard_map/all_to_all | solution.py:498
  41.1 0.7 shard_map.178
  41.9 5.4 %all-to-all-start.1 = ((f32[32,2,128]{2,1,0:T(2,128)}), f32[32,2,128]{2,1,0:T(2,128)S(1)}, u32[]{:S(2)}, u32[]{:S(2)}) async-start(f32[32,2,128]{2,1,0:T(2,128)} %shard_map.178), calls=%async_computation.1 | async-start | bytes 65536 | tf_op jit(solution)/shard_map/all_to_all | solution.py:498
  47.3 7.1 %shard_map.179 = (f32[192,256]{1,0:T(8,128)S(1)}, f32[16,256]{1,0:T(8,128)S(1)}, bf16[1152,2048]{1,0:T(8,128)(2,1)}, bf16[384,144]{1,0:T(8,128)(2,1)S(1)}, f32[3...) custom-call(s32[16,256]{1,0:T(8,128)S(1)} %get-tuple-element.32.sources, s32[16,24]{1,0:T(8,128)S(1)} %get-tuple-element.33.far_sources, ...), custom_call_target="tpu_custom_call" | custom-call | flops 2147483648 | bytes 1048576 | tf_op jit(solution)/shard_map/pallas_call | solution.py:36
  54.4 1.6 %all-to-all-done.1.partial = f32[32,2,128]{2,1,0:T(2,128)S(1)} async-done(((f32[32,2,128]{2,1,0:T(2,128)}), f32[32,2,128]{2,1,0:T(2,128)S(1)}, u32[]{:S(2)}, u32[]{:S(2)}) %all-to-all-start.1) | async-done | bytes 32800 | tf_op jit(solution)/shard_map/all_to_all | solution.py:498
  56.0 1.4 %shard_map.180 = (f32[192,128]{1,0:T(8,128)S(1)}, bf16[1,224,128]{2,1,0:T(8,128)(2,1)S(1)}, f32[16,2,128]{2,1,0:T(2,128)}) custom-call(f32[32,2,128]{2,1,0:T(2,128)S(1)} %all-to-all-done.1.partial, f32[192,256]{1,0:T(8,128)S(1)} %get-tuple-element.40.near, f32[16,256]{1,0:T(8,128)S(1)} %get-tuple-element.41.leaf_in, ...), custom_call_target="tpu_custom_call" | custom-call | flops 67108864 | bytes 1048576 | tf_op jit(solution)/shard_map/pallas_call | solution.py:36
  57.4 0.7 collective-permute-start.4
  58.1 4.0 %collective-permute-start.5 = (bf16[1,224,128]{2,1,0:T(8,128)(2,1)S(1)}, bf16[1,224,128]{2,1,0:T(8,128)(2,1)S(1)}, u32[]{:S(2)}, u32[]{:S(2)}) collective-permute-start(bf16[1,224,128]{2,1,0:T(8,128)(2,1)S(1)} %get-tuple-element.48), channel_id=1, source_target_pairs={{0,32},{64,96},{128,160},{192,224},{256,288},{320,352},{384,416},{... | collective-permute-start | bytes 172040 | tf_op jit(solution)/shard_map/ppermute | solution.py:494
  62.1 1.5 %collective-permute-done.5 = bf16[1,224,128]{2,1,0:T(8,128)(2,1)S(1)} collective-permute-done((bf16[1,224,128]{2,1,0:T(8,128)(2,1)S(1)}, bf16[1,224,128]{2,1,0:T(8,128)(2,1)S(1)}, u32[]{:S(2)}, u32[]{:S(2)}) %collective-permute-start.5) | collective-permute-done | bytes 57376 | tf_op jit(solution)/shard_map/ppermute | solution.py:494
  63.7 4.8 %collective-permute-start.6 = (bf16[3,224,128]{2,1,0:T(8,128)(2,1)S(1)}, bf16[3,224,128]{2,1,0:T(8,128)(2,1)S(1)}, u32[]{:S(2)}, u32[]{:S(2)}) collective-permute-start(bf16[3,224,128]{2,1,0:T(8,128)(2,1)S(1)} %constant_dynamic-update-slice_fusion.3.own), channel_id=1, source_target_pairs={{1,2},{3,4},{5,6},{7,8},{9,10},{11,12},{13,14},{15,16},{17,18},{19... | collective-permute-start | bytes 516104 | tf_op jit(solution)/shard_map/ppermute | solution.py:494
  68.5 1.9 %collective-permute-start.7 = (bf16[3,224,128]{2,1,0:T(8,128)(2,1)S(1)}, bf16[3,224,128]{2,1,0:T(8,128)(2,1)S(1)}, u32[]{:S(2)}, u32[]{:S(2)}) collective-permute-start(bf16[3,224,128]{2,1,0:T(8,128)(2,1)S(1)} %constant_dynamic-update-slice_fusion.3.own), channel_id=1, source_target_pairs={{0,1},{2,3},{4,5},{6,7},{8,9},{10,11},{12,13},{14,15},{16,17},{18,... | collective-permute-start | bytes 516104 | tf_op jit(solution)/shard_map/ppermute | solution.py:494
  70.4 9.3 %all-to-all-start.2 = ((f32[16,2,128]{2,1,0:T(2,128)}), f32[16,2,128]{2,1,0:T(2,128)S(1)}, u32[]{:S(2)}, u32[]{:S(2)}) async-start(f32[16,2,128]{2,1,0:T(2,128)} %get-tuple-element.47), calls=%async_computation.2 | async-start | bytes 32768 | tf_op jit(solution)/shard_map/all_to_all | solution.py:498
  79.7 0.1 shard_map.183.sums
  79.8 7.2 %all-to-all-done.2.columns = f32[16,2,128]{2,1,0:T(2,128)S(1)} async-done(((f32[16,2,128]{2,1,0:T(2,128)}), f32[16,2,128]{2,1,0:T(2,128)S(1)}, u32[]{:S(2)}, u32[]{:S(2)}) %all-to-all-start.2) | async-done | bytes 16416 | tf_op jit(solution)/shard_map/all_to_all | solution.py:498
  87.0 0.7 shard_map.181
  87.8 5.5 %all-to-all-start.3 = ((f32[32,2,128]{2,1,0:T(2,128)}), f32[32,2,128]{2,1,0:T(2,128)S(1)}, u32[]{:S(2)}, u32[]{:S(2)}) async-start(f32[32,2,128]{2,1,0:T(2,128)} %shard_map.181), calls=%async_computation.3 | async-start | bytes 65536 | tf_op jit(solution)/shard_map/all_to_all | solution.py:498
  93.3 4.3 %shard_map.182 = (f32[192,256]{1,0:T(8,128)S(1)}, f32[16,256]{1,0:T(8,128)S(1)}) custom-call(bf16[3,224,128]{2,1,0:T(8,128)(2,1)S(1)} %collective-permute-done.6.before, bf16[3,224,128]{2,1,0:T(8,128)(2,1)S(1)} %constant_dynamic-update-slice_fusion.3.own, bf16[3,224,128]{2,1,0:T(8,128)(2,1)S(1)} %collective-permute-done.7.after, ...), custom_call_target="tpu_custom_call" | custom-call | flops 2147483648 | bytes 1048576 | tf_op jit(solution)/shard_map/pallas_call | solution.py:36
  97.6 4.4 %all-to-all-done.3.partial = f32[32,2,128]{2,1,0:T(2,128)S(1)} async-done(((f32[32,2,128]{2,1,0:T(2,128)}), f32[32,2,128]{2,1,0:T(2,128)S(1)}, u32[]{:S(2)}, u32[]{:S(2)}) %all-to-all-start.3) | async-done | bytes 32800 | tf_op jit(solution)/shard_map/all_to_all | solution.py:498
  102.0 0.6 shard_map.184
  102.6 13.2 %all_to_all.30.parts = f32[32,1,128]{2,1,0:T(1,128)S(1)} all-to-all(f32[32,1,128]{2,1,0:T(1,128)S(1)} %get-tuple-element.54), channel_id=1, replica_groups=mesh['bx_0'=2,'bx_1'=8,'by_0'=4,'by_1'=4,'by_2'=2] {'bx_1','by_0'}, dimensions={0} | all-to-all | bytes 32768 | tf_op jit(solution)/shard_map/all_to_all | solution.py:498
  115.9 11.9 %all_to_all.31.parts = f32[16,1,128]{2,1,0:T(1,128)S(1)} all-to-all(f32[16,1,128]{2,1,0:T(1,128)S(1)} %shard_map.185), channel_id=1, replica_groups=mesh['bx_0'=2,'bx_1'=8,'by_0'=4,'by_1'=4,'by_2'=2] {'bx_0','by_1','by_2'}, dimensions={0} | all-to-all | bytes 16384 | tf_op jit(solution)/shard_map/all_to_all | solution.py:498
  127.7 0.8 shard_map.186
  (21 shorter events, 0.1 us)
Async XLA Ops:
  2.8 8.8 %collective-permute-start = (bf16[1,224,128]{2,1,0:T(8,128)(2,1)S(1)}, bf16[1,224,128]{2,1,0:T(8,128)(2,1)S(1)}, u32[]{:S(2)}, u32[]{:S(2)}) collective-permute-start(bf16[1,224,128]{2,1,0:T(8,128)(2,1)S(1)} %get-tuple-element.39), channel_id=1, source_target_pairs={{32,64},{96,128},{160,192},{224,256},{288,320},{352,384},{416,448}... | collective-permute-start | bytes 172040 | tf_op jit(solution)/shard_map/ppermute | solution.py:494
  3.5 9.7 %collective-permute-start.1 = (bf16[1,224,128]{2,1,0:T(8,128)(2,1)S(1)}, bf16[1,224,128]{2,1,0:T(8,128)(2,1)S(1)}, u32[]{:S(2)}, u32[]{:S(2)}) collective-permute-start(bf16[1,224,128]{2,1,0:T(8,128)(2,1)S(1)} %get-tuple-element.39), channel_id=1, source_target_pairs={{0,32},{64,96},{128,160},{192,224},{256,288},{320,352},{384,416},{... | collective-permute-start | bytes 172040 | tf_op jit(solution)/shard_map/ppermute | solution.py:494
  13.2 34.0 %collective-permute-start.2 = (bf16[3,224,128]{2,1,0:T(8,128)(2,1)S(1)}, bf16[3,224,128]{2,1,0:T(8,128)(2,1)S(1)}, u32[]{:S(2)}, u32[]{:S(2)}) collective-permute-start(bf16[3,224,128]{2,1,0:T(8,128)(2,1)S(1)} %constant_dynamic-update-slice_fusion.own), channel_id=1, source_target_pairs={{1,2},{3,4},{5,6},{7,8},{9,10},{11,12},{13,14},{15,16},{17,18},{19... | collective-permute-start | bytes 516104 | tf_op jit(solution)/shard_map/ppermute | solution.py:494
  18.1 29.1 %collective-permute-start.3 = (bf16[3,224,128]{2,1,0:T(8,128)(2,1)S(1)}, bf16[3,224,128]{2,1,0:T(8,128)(2,1)S(1)}, u32[]{:S(2)}, u32[]{:S(2)}) collective-permute-start(bf16[3,224,128]{2,1,0:T(8,128)(2,1)S(1)} %constant_dynamic-update-slice_fusion.own), channel_id=1, source_target_pairs={{0,1},{2,3},{4,5},{6,7},{8,9},{10,11},{12,13},{14,15},{16,17},{18,... | collective-permute-start | bytes 516104 | tf_op jit(solution)/shard_map/ppermute | solution.py:494
  20.1 21.0 %all-to-all-start = ((f32[16,2,128]{2,1,0:T(2,128)}), f32[16,2,128]{2,1,0:T(2,128)S(1)}, u32[]{:S(2)}, u32[]{:S(2)}) async-start(f32[16,2,128]{2,1,0:T(2,128)} %get-tuple-element.30), calls=%async_computation | async-start | bytes 32768 | tf_op jit(solution)/shard_map/all_to_all | solution.py:498
  36.3 19.6 %copy-start.1 = (bf16[2,96,128]{2,1,0:T(8,128)(2,1)S(1)}, bf16[2,96,128]{2,1,0:T(8,128)(2,1)}, u32[]{:S(2)}) copy-start(bf16[2,96,128]{2,1,0:T(8,128)(2,1)} %param.25) | copy-start | bytes 147460
  36.3 19.6 %copy-start.2 = (f32[16,128]{1,0:T(8,128)S(1)}, f32[16,128]{1,0:T(8,128)}, u32[]{:S(2)}) copy-start(f32[16,128]{1,0:T(8,128)} %constant.37.clone.leaf_cos) | copy-start | bytes 24580
  36.3 19.6 %copy-start.3 = (f32[16,128]{1,0:T(8,128)S(1)}, f32[16,128]{1,0:T(8,128)}, u32[]{:S(2)}) copy-start(f32[16,128]{1,0:T(8,128)} %constant.38.clone.leaf_sin) | copy-start | bytes 24580
  36.4 19.6 %copy-start.4 = (s32[1,1,128]{2,1,0:T(1,128)S(1)}, s32[1,1,128]{2,1,0:T(1,128)}, u32[]{:S(2)}) copy-start(s32[1,1,128]{2,1,0:T(1,128)} %param.20) | copy-start | bytes 1540
  41.1 38.6 %copy-start = (f32[2,96,1,1,128]{4,3,2,1,0:T(1,128)S(1)}, f32[2,96,1,1,128]{4,3,2,1,0:T(1,128)}, u32[]{:S(2)}) copy-start(f32[2,96,1,1,128]{4,3,2,1,0:T(1,128)} %param.17) | copy-start | bytes 294916
  41.9 14.1 %all-to-all-start.1 = ((f32[32,2,128]{2,1,0:T(2,128)}), f32[32,2,128]{2,1,0:T(2,128)S(1)}, u32[]{:S(2)}, u32[]{:S(2)}) async-start(f32[32,2,128]{2,1,0:T(2,128)} %shard_map.178), calls=%async_computation.1 | async-start | bytes 65536 | tf_op jit(solution)/shard_map/all_to_all | solution.py:498
  57.4 4.7 %collective-permute-start.4 = (bf16[1,224,128]{2,1,0:T(8,128)(2,1)S(1)}, bf16[1,224,128]{2,1,0:T(8,128)(2,1)S(1)}, u32[]{:S(2)}, u32[]{:S(2)}) collective-permute-start(bf16[1,224,128]{2,1,0:T(8,128)(2,1)S(1)} %get-tuple-element.48), channel_id=1, source_target_pairs={{32,64},{96,128},{160,192},{224,256},{288,320},{352,384},{416,448}... | collective-permute-start | bytes 172040 | tf_op jit(solution)/shard_map/ppermute | solution.py:494
  58.1 5.6 %collective-permute-start.5 = (bf16[1,224,128]{2,1,0:T(8,128)(2,1)S(1)}, bf16[1,224,128]{2,1,0:T(8,128)(2,1)S(1)}, u32[]{:S(2)}, u32[]{:S(2)}) collective-permute-start(bf16[1,224,128]{2,1,0:T(8,128)(2,1)S(1)} %get-tuple-element.48), channel_id=1, source_target_pairs={{0,32},{64,96},{128,160},{192,224},{256,288},{320,352},{384,416},{... | collective-permute-start | bytes 172040 | tf_op jit(solution)/shard_map/ppermute | solution.py:494
  63.7 29.6 %collective-permute-start.6 = (bf16[3,224,128]{2,1,0:T(8,128)(2,1)S(1)}, bf16[3,224,128]{2,1,0:T(8,128)(2,1)S(1)}, u32[]{:S(2)}, u32[]{:S(2)}) collective-permute-start(bf16[3,224,128]{2,1,0:T(8,128)(2,1)S(1)} %constant_dynamic-update-slice_fusion.3.own), channel_id=1, source_target_pairs={{1,2},{3,4},{5,6},{7,8},{9,10},{11,12},{13,14},{15,16},{17,18},{19... | collective-permute-start | bytes 516104 | tf_op jit(solution)/shard_map/ppermute | solution.py:494
  68.5 24.8 %collective-permute-start.7 = (bf16[3,224,128]{2,1,0:T(8,128)(2,1)S(1)}, bf16[3,224,128]{2,1,0:T(8,128)(2,1)S(1)}, u32[]{:S(2)}, u32[]{:S(2)}) collective-permute-start(bf16[3,224,128]{2,1,0:T(8,128)(2,1)S(1)} %constant_dynamic-update-slice_fusion.3.own), channel_id=1, source_target_pairs={{0,1},{2,3},{4,5},{6,7},{8,9},{10,11},{12,13},{14,15},{16,17},{18,... | collective-permute-start | bytes 516104 | tf_op jit(solution)/shard_map/ppermute | solution.py:494
  70.4 16.6 %all-to-all-start.2 = ((f32[16,2,128]{2,1,0:T(2,128)}), f32[16,2,128]{2,1,0:T(2,128)S(1)}, u32[]{:S(2)}, u32[]{:S(2)}) async-start(f32[16,2,128]{2,1,0:T(2,128)} %get-tuple-element.47), calls=%async_computation.2 | async-start | bytes 32768 | tf_op jit(solution)/shard_map/all_to_all | solution.py:498
  87.8 14.2 %all-to-all-start.3 = ((f32[32,2,128]{2,1,0:T(2,128)}), f32[32,2,128]{2,1,0:T(2,128)S(1)}, u32[]{:S(2)}, u32[]{:S(2)}) async-start(f32[32,2,128]{2,1,0:T(2,128)} %shard_map.181), calls=%async_computation.3 | async-start | bytes 65536 | tf_op jit(solution)/shard_map/all_to_all | solution.py:498

commit v9 on v7

--- a/solution.py
+++ b/solution.py
@@ -257,12 +257,25 @@
     near[...] = total
 
 
-def near_kernel(before, own, after, counts, table, select, chosen, near, leaf_in, columns):
-    @pl.when(pl.program_id(0) == 0)
-    def _():
-        near_start(before, own, after, select, chosen, near, leaf_in, columns)
-
-    near_step(columns, counts[...], table, near)
+def near_kernel(
+    before, own, after, counts, table_hbm, select, chosen, near, leaf_in, columns, block, table, sems
+):
+    groups, _, wide = block.shape
+    chunk = table.shape[0] // groups
+    loading = pltpu.make_async_copy(table_hbm, table, sems.at[groups])
+    loading.start()
+    fetching = []
+    for group in range(groups):
+        fetch = pltpu.make_async_copy(
+            counts.at[:, pl.ds(group * wide, wide)], block.at[group], sems.at[group]
+        )
+        fetch.start()
+        fetching.append(fetch)
+    near_start(before, own, after, select, chosen, near, leaf_in, columns)
+    loading.wait()
+    for group in range(groups):
+        fetching[group].wait()
+        near_step(columns, block[group], table.at[pl.ds(group * chunk, chunk)], near)
 
 
 def both_kernel(
@@ -544,7 +557,6 @@
         (vector, pattern, offsets.reshape(3, 1, spheres), planes, box, leaf_cos, leaf_sin),
         flops=1 << 26,
     )
-    chunk = classes // 2
     whole = pl.BlockSpec(memory_space=pltpu.VMEM)
 
     def windows():
@@ -602,9 +614,15 @@
         lines = resident(left), resident(line), resident(right)
         table = near_table.reshape(classes, rows, coefs)
         sums = (kept((rows, 2 * spheres)), kept((boxes, 2 * dirs)))
+        groups = classes // 4
+        any_spec = pl.BlockSpec(memory_space=pl.ANY)
+        scratch = [
+            pltpu.VMEM((rows, 9 * spheres), BF16),
+            pltpu.VMEM((groups, 9 * spheres, 4 * spheres), BF16),
+            pltpu.VMEM((classes, rows, coefs), BF16),
+            pltpu.SemaphoreType.DMA((groups + 1,)),
+        ]
         if tables is None:
-            groups = classes // 4
-            any_spec = pl.BlockSpec(memory_space=pl.ANY)
             near, leaf_in, *tables = call(
                 both_kernel,
                 sums
@@ -618,12 +636,7 @@
                 flops=1 << 31,
                 specs=[whole] * 10 + [any_spec],
                 out_specs=(whole, whole, any_spec, whole, whole, whole),
-                scratch_shapes=[
-                    pltpu.VMEM((rows, 9 * spheres), BF16),
-                    pltpu.VMEM((groups, 9 * spheres, 4 * spheres), BF16),
-                    pltpu.VMEM((classes, rows, coefs), BF16),
-                    pltpu.SemaphoreType.DMA((groups + 1,)),
-                ],
+                scratch_shapes=scratch,
             )
         else:
             counts, select, chosen, _ = tables
@@ -632,18 +645,9 @@
                 sums,
                 lines + (counts, table, resident(select), resident(chosen)),
                 flops=1 << 31,
-                grid=(classes // chunk,),
-                in_specs=[
-                    whole,
-                    whole,
-                    whole,
-                    pl.BlockSpec((9 * spheres, chunk * spheres), lambda k: (0, k)),
-                    pl.BlockSpec((chunk, rows, coefs), lambda k: (k, 0, 0)),
-                    whole,
-                    whole,
-                ],
+                specs=[whole] * 3 + [any_spec] * 2 + [whole] * 2,
                 out_specs=(whole, whole),
-                scratch_shapes=[pltpu.VMEM((rows, 9 * spheres), BF16)],
+                scratch_shapes=scratch,
             )
         return (resident(partial), resident(near), resident(leaf_in)), tables
 

time: 130 us -> 131 us (level)
  transfers between devices with their start and end apart: 12 -> 12, of which waited for: 6 -> 6; matrix products, arithmetic and copies ran while one was open for 0% -> 0% of each run, Pallas kernels for 11% -> 12%
where the time goes in v9:
time: 131 us; the launch traced here: 130 us
  starting transfers between devices  64.3 us (49%)
  blocking collectives  22.8 us (17%)
  waiting for transfers between devices  21.6 us (16%)
  Pallas kernels  20.1 us (15%)
    all_to_all x4, starting transfers between devices, exchange(): return lax.all_to_all(x, axes, split_axis=0, concat_axis=0, tiled=True)  37.5 us
    ppermute x8, starting transfers between devices, swap(): return lax.ppermute(x, axes, pairs + [(j, i) for i, j in pairs])  26.8 us
    all_to_all x2, blocking collectives, exchange(): return lax.all_to_all(x, axes, split_axis=0, concat_axis=0, tiled=True)  22.8 us
    pallas_call x11, Pallas kernels, call(): pl.pallas_call(kernel, out_shape=out_shape, interpret=INTERPRET, cost_est...  20.1 us
    all_to_all x4, waiting for transfers between devices, exchange(): return lax.all_to_all(x, axes, split_axis=0, concat_axis=0, tiled=True)  18.5 us
    ppermute x8, waiting for transfers between devices, swap(): return lax.ppermute(x, axes, pairs + [(j, i) for i, j in pairs])  3.03 us
  transfers between devices with their start and end apart: 12, of which 6 were waited for; matrix products, arithmetic and copies ran while one was open for 0% of the time, Pallas kernels for 12%

profile of v9, /device:TPU:1, one launch (start us, length us, event | category | flops | bytes accessed | tf_op | source)
XLA Modules:
  0.0 129.8 jit_solution(9286698145263736949)
XLA Ops:
  0.6 2.2 %shard_map.176 = (bf16[1,224,128]{2,1,0:T(8,128)(2,1)S(1)}, f32[32,2,128]{2,1,0:T(2,128)}, f32[128,128]{1,0:T(8,128)S(1)}, f32[128,128]{1,0:T(8,128)S(1)}, bf16[256,96]{1,0:T(8,128)(2,1)S(1)}) custom-call(f32[192,128]{1,0:T(8,128)} %bitcast.19, bf16[2,96,128]{2,1,0:T(8,128)(2,1)} %bitcast.29, f32[3,1,128]{2,1,0:T(1,128)} %bitcast.35, ...), custom_call_target="tpu_custom_call" | custom-call | flops 67108864 | bytes 1048576 | tf_op jit(solution)/shard_map/pallas_call | solution.py:36
  2.9 0.7 collective-permute-start
  3.5 8.2 %collective-permute-start.1 = (bf16[1,224,128]{2,1,0:T(8,128)(2,1)S(1)}, bf16[1,224,128]{2,1,0:T(8,128)(2,1)S(1)}, u32[]{:S(2)}, u32[]{:S(2)}) collective-permute-start(bf16[1,224,128]{2,1,0:T(8,128)(2,1)S(1)} %get-tuple-element.39), channel_id=1, source_target_pairs={{0,32},{64,96},{128,160},{192,224},{256,288},{320,352},{384,416},{... | collective-permute-start | bytes 172040 | tf_op jit(solution)/shard_map/ppermute | solution.py:502
  11.7 1.5 %collective-permute-done.1 = bf16[1,224,128]{2,1,0:T(8,128)(2,1)S(1)} collective-permute-done((bf16[1,224,128]{2,1,0:T(8,128)(2,1)S(1)}, bf16[1,224,128]{2,1,0:T(8,128)(2,1)S(1)}, u32[]{:S(2)}, u32[]{:S(2)}) %collective-permute-start.1) | collective-permute-done | bytes 57376 | tf_op jit(solution)/shard_map/ppermute | solution.py:502
  13.2 5.1 %collective-permute-start.3 = (bf16[3,224,128]{2,1,0:T(8,128)(2,1)S(1)}, bf16[3,224,128]{2,1,0:T(8,128)(2,1)S(1)}, u32[]{:S(2)}, u32[]{:S(2)}) collective-permute-start(bf16[3,224,128]{2,1,0:T(8,128)(2,1)S(1)} %constant_dynamic-update-slice_fusion.own), channel_id=1, source_target_pairs={{0,1},{2,3},{4,5},{6,7},{8,9},{10,11},{12,13},{14,15},{16,17},{18,... | collective-permute-start | bytes 516104 | tf_op jit(solution)/shard_map/ppermute | solution.py:502
  18.4 1.9 %collective-permute-start.2 = (bf16[3,224,128]{2,1,0:T(8,128)(2,1)S(1)}, bf16[3,224,128]{2,1,0:T(8,128)(2,1)S(1)}, u32[]{:S(2)}, u32[]{:S(2)}) collective-permute-start(bf16[3,224,128]{2,1,0:T(8,128)(2,1)S(1)} %constant_dynamic-update-slice_fusion.own), channel_id=1, source_target_pairs={{1,2},{3,4},{5,6},{7,8},{9,10},{11,12},{13,14},{15,16},{17,18},{19... | collective-permute-start | bytes 516104 | tf_op jit(solution)/shard_map/ppermute | solution.py:502
  20.3 14.1 %all-to-all-start = ((f32[32,2,128]{2,1,0:T(2,128)}), f32[32,2,128]{2,1,0:T(2,128)S(1)}, u32[]{:S(2)}, u32[]{:S(2)}) async-start(f32[32,2,128]{2,1,0:T(2,128)} %get-tuple-element.30), calls=%async_computation | async-start | bytes 65536 | tf_op jit(solution)/shard_map/all_to_all | solution.py:506
  34.4 2.0 %shard_map.177 = (f32[2,16,32,128]{3,2,1,0:T(8,128)S(1)}, s32[16,256]{1,0:T(8,128)S(1)}, s32[16,24]{1,0:T(8,128)S(1)}, s32[16,256]{1,0:T(8,128)S(1)}, s32[16,24]...) custom-call(s32[1]{0:T(128)} %bitcast.4.index, ...), custom_call_target="tpu_custom_call" | custom-call | flops 268435456 | bytes 1048576 | tf_op jit(solution)/shard_map/pallas_call | solution.py:36
  36.4 0.0 copy-start.2
  36.4 0.0 copy-start.3
  36.4 6.7 %all-to-all-done.columns = f32[32,2,128]{2,1,0:T(2,128)S(1)} async-done(((f32[32,2,128]{2,1,0:T(2,128)}), f32[32,2,128]{2,1,0:T(2,128)S(1)}, u32[]{:S(2)}, u32[]{:S(2)}) %all-to-all-start) | async-done | bytes 32800 | tf_op jit(solution)/shard_map/all_to_all | solution.py:506
  43.2 0.7 shard_map.178
  43.9 7.2 %all-to-all-start.1 = ((f32[16,2,128]{2,1,0:T(2,128)}), f32[16,2,128]{2,1,0:T(2,128)S(1)}, u32[]{:S(2)}, u32[]{:S(2)}) async-start(f32[16,2,128]{2,1,0:T(2,128)} %shard_map.178), calls=%async_computation.1 | async-start | bytes 32768 | tf_op jit(solution)/shard_map/all_to_all | solution.py:506
  51.1 7.1 %shard_map.179 = (f32[192,256]{1,0:T(8,128)S(1)}, f32[16,256]{1,0:T(8,128)S(1)}, bf16[1152,2048]{1,0:T(8,128)(2,1)}, bf16[384,144]{1,0:T(8,128)(2,1)S(1)}, f32[3...) custom-call(s32[16,256]{1,0:T(8,128)S(1)} %get-tuple-element.32.sources, s32[16,24]{1,0:T(8,128)S(1)} %get-tuple-element.33.far_sources, ...), custom_call_target="tpu_custom_call" | custom-call | flops 2147483648 | bytes 1048576 | tf_op jit(solution)/shard_map/pallas_call | solution.py:36
  58.3 0.2 all-to-all-done.1.partial
  58.5 1.4 %shard_map.180 = (f32[192,128]{1,0:T(8,128)S(1)}, bf16[1,224,128]{2,1,0:T(8,128)(2,1)S(1)}, f32[32,2,128]{2,1,0:T(2,128)}) custom-call(f32[16,2,128]{2,1,0:T(2,128)S(1)} %all-to-all-done.1.partial, f32[192,256]{1,0:T(8,128)S(1)} %get-tuple-element.40.near, f32[16,256]{1,0:T(8,128)S(1)} %get-tuple-element.41.leaf_in, ...), custom_call_target="tpu_custom_call" | custom-call | flops 67108864 | bytes 1048576 | tf_op jit(solution)/shard_map/pallas_call | solution.py:36
  60.0 0.7 collective-permute-start.4
  60.6 3.9 %collective-permute-start.5 = (bf16[1,224,128]{2,1,0:T(8,128)(2,1)S(1)}, bf16[1,224,128]{2,1,0:T(8,128)(2,1)S(1)}, u32[]{:S(2)}, u32[]{:S(2)}) collective-permute-start(bf16[1,224,128]{2,1,0:T(8,128)(2,1)S(1)} %get-tuple-element.48), channel_id=1, source_target_pairs={{0,32},{64,96},{128,160},{192,224},{256,288},{320,352},{384,416},{... | collective-permute-start | bytes 172040 | tf_op jit(solution)/shard_map/ppermute | solution.py:502
  64.6 1.5 %collective-permute-done.5 = bf16[1,224,128]{2,1,0:T(8,128)(2,1)S(1)} collective-permute-done((bf16[1,224,128]{2,1,0:T(8,128)(2,1)S(1)}, bf16[1,224,128]{2,1,0:T(8,128)(2,1)S(1)}, u32[]{:S(2)}, u32[]{:S(2)}) %collective-permute-start.5) | collective-permute-done | bytes 57376 | tf_op jit(solution)/shard_map/ppermute | solution.py:502
  66.1 3.5 %collective-permute-start.7 = (bf16[3,224,128]{2,1,0:T(8,128)(2,1)S(1)}, bf16[3,224,128]{2,1,0:T(8,128)(2,1)S(1)}, u32[]{:S(2)}, u32[]{:S(2)}) collective-permute-start(bf16[3,224,128]{2,1,0:T(8,128)(2,1)S(1)} %constant_dynamic-update-slice_fusion.3.own), channel_id=1, source_target_pairs={{0,1},{2,3},{4,5},{6,7},{8,9},{10,11},{12,13},{14,15},{16,17},{18,... | collective-permute-start | bytes 516104 | tf_op jit(solution)/shard_map/ppermute | solution.py:502
  69.6 2.9 %collective-permute-start.6 = (bf16[3,224,128]{2,1,0:T(8,128)(2,1)S(1)}, bf16[3,224,128]{2,1,0:T(8,128)(2,1)S(1)}, u32[]{:S(2)}, u32[]{:S(2)}) collective-permute-start(bf16[3,224,128]{2,1,0:T(8,128)(2,1)S(1)} %constant_dynamic-update-slice_fusion.3.own), channel_id=1, source_target_pairs={{1,2},{3,4},{5,6},{7,8},{9,10},{11,12},{13,14},{15,16},{17,18},{19... | collective-permute-start | bytes 516104 | tf_op jit(solution)/shard_map/ppermute | solution.py:502
  72.5 9.9 %all-to-all-start.2 = ((f32[32,2,128]{2,1,0:T(2,128)}), f32[32,2,128]{2,1,0:T(2,128)S(1)}, u32[]{:S(2)}, u32[]{:S(2)}) async-start(f32[32,2,128]{2,1,0:T(2,128)} %get-tuple-element.47), calls=%async_computation.2 | async-start | bytes 65536 | tf_op jit(solution)/shard_map/all_to_all | solution.py:506
  82.4 0.1 shard_map.183.sums
  82.6 8.6 %all-to-all-done.2.columns = f32[32,2,128]{2,1,0:T(2,128)S(1)} async-done(((f32[32,2,128]{2,1,0:T(2,128)}), f32[32,2,128]{2,1,0:T(2,128)S(1)}, u32[]{:S(2)}, u32[]{:S(2)}) %all-to-all-start.2) | async-done | bytes 32800 | tf_op jit(solution)/shard_map/all_to_all | solution.py:506
  91.2 0.7 shard_map.181
  91.9 6.3 %all-to-all-start.3 = ((f32[16,2,128]{2,1,0:T(2,128)}), f32[16,2,128]{2,1,0:T(2,128)S(1)}, u32[]{:S(2)}, u32[]{:S(2)}) async-start(f32[16,2,128]{2,1,0:T(2,128)} %shard_map.181), calls=%async_computation.3 | async-start | bytes 32768 | tf_op jit(solution)/shard_map/all_to_all | solution.py:506
  98.2 4.4 %shard_map.182 = (f32[192,256]{1,0:T(8,128)S(1)}, f32[16,256]{1,0:T(8,128)S(1)}) custom-call(bf16[3,224,128]{2,1,0:T(8,128)(2,1)S(1)} %collective-permute-done.6.before, bf16[3,224,128]{2,1,0:T(8,128)(2,1)S(1)} %constant_dynamic-update-slice_fusion.3.own, bf16[3,224,128]{2,1,0:T(8,128)(2,1)S(1)} %collective-permute-done.7.after, ...), custom_call_target="tpu_custom_call" | custom-call | flops 2147483648 | bytes 1048576 | tf_op jit(solution)/shard_map/pallas_call | solution.py:36
  102.7 2.9 %all-to-all-done.3.partial = f32[16,2,128]{2,1,0:T(2,128)S(1)} async-done(((f32[16,2,128]{2,1,0:T(2,128)}), f32[16,2,128]{2,1,0:T(2,128)S(1)}, u32[]{:S(2)}, u32[]{:S(2)}) %all-to-all-start.3) | async-done | bytes 16416 | tf_op jit(solution)/shard_map/all_to_all | solution.py:506
  105.5 0.5 shard_map.184
  106.1 11.2 %all_to_all.30.parts = f32[16,1,128]{2,1,0:T(1,128)S(1)} all-to-all(f32[16,1,128]{2,1,0:T(1,128)S(1)} %get-tuple-element.54), channel_id=1, replica_groups=mesh['bx_0'=2,'bx_1'=8,'by_0'=4,'by_1'=4,'by_2'=2] {'bx_0','by_1','by_2'}, dimensions={0} | all-to-all | bytes 16384 | tf_op jit(solution)/shard_map/all_to_all | solution.py:506
  117.3 11.6 %all_to_all.31.parts = f32[32,1,128]{2,1,0:T(1,128)S(1)} all-to-all(f32[32,1,128]{2,1,0:T(1,128)S(1)} %shard_map.185), channel_id=1, replica_groups=mesh['bx_0'=2,'bx_1'=8,'by_0'=4,'by_1'=4,'by_2'=2] {'by_0','bx_1'}, dimensions={0} | all-to-all | bytes 32768 | tf_op jit(solution)/shard_map/all_to_all | solution.py:506
  128.9 0.9 shard_map.186
  (21 shorter events, 0.1 us)
Async XLA Ops:
  2.9 8.8 %collective-permute-start = (bf16[1,224,128]{2,1,0:T(8,128)(2,1)S(1)}, bf16[1,224,128]{2,1,0:T(8,128)(2,1)S(1)}, u32[]{:S(2)}, u32[]{:S(2)}) collective-permute-start(bf16[1,224,128]{2,1,0:T(8,128)(2,1)S(1)} %get-tuple-element.39), channel_id=1, source_target_pairs={{32,64},{96,128},{160,192},{224,256},{288,320},{352,384},{416,448}... | collective-permute-start | bytes 172040 | tf_op jit(solution)/shard_map/ppermute | solution.py:502
  3.5 9.7 %collective-permute-start.1 = (bf16[1,224,128]{2,1,0:T(8,128)(2,1)S(1)}, bf16[1,224,128]{2,1,0:T(8,128)(2,1)S(1)}, u32[]{:S(2)}, u32[]{:S(2)}) collective-permute-start(bf16[1,224,128]{2,1,0:T(8,128)(2,1)S(1)} %get-tuple-element.39), channel_id=1, source_target_pairs={{0,32},{64,96},{128,160},{192,224},{256,288},{320,352},{384,416},{... | collective-permute-start | bytes 172040 | tf_op jit(solution)/shard_map/ppermute | solution.py:502
  13.2 37.9 %collective-permute-start.3 = (bf16[3,224,128]{2,1,0:T(8,128)(2,1)S(1)}, bf16[3,224,128]{2,1,0:T(8,128)(2,1)S(1)}, u32[]{:S(2)}, u32[]{:S(2)}) collective-permute-start(bf16[3,224,128]{2,1,0:T(8,128)(2,1)S(1)} %constant_dynamic-update-slice_fusion.own), channel_id=1, source_target_pairs={{0,1},{2,3},{4,5},{6,7},{8,9},{10,11},{12,13},{14,15},{16,17},{18,... | collective-permute-start | bytes 516104 | tf_op jit(solution)/shard_map/ppermute | solution.py:502
  18.4 32.8 %collective-permute-start.2 = (bf16[3,224,128]{2,1,0:T(8,128)(2,1)S(1)}, bf16[3,224,128]{2,1,0:T(8,128)(2,1)S(1)}, u32[]{:S(2)}, u32[]{:S(2)}) collective-permute-start(bf16[3,224,128]{2,1,0:T(8,128)(2,1)S(1)} %constant_dynamic-update-slice_fusion.own), channel_id=1, source_target_pairs={{1,2},{3,4},{5,6},{7,8},{9,10},{11,12},{13,14},{15,16},{17,18},{19... | collective-permute-start | bytes 516104 | tf_op jit(solution)/shard_map/ppermute | solution.py:502
  20.3 22.9 %all-to-all-start = ((f32[32,2,128]{2,1,0:T(2,128)}), f32[32,2,128]{2,1,0:T(2,128)S(1)}, u32[]{:S(2)}, u32[]{:S(2)}) async-start(f32[32,2,128]{2,1,0:T(2,128)} %get-tuple-element.30), calls=%async_computation | async-start | bytes 65536 | tf_op jit(solution)/shard_map/all_to_all | solution.py:506
  36.4 22.1 %copy-start.1 = (bf16[2,96,128]{2,1,0:T(8,128)(2,1)S(1)}, bf16[2,96,128]{2,1,0:T(8,128)(2,1)}, u32[]{:S(2)}) copy-start(bf16[2,96,128]{2,1,0:T(8,128)(2,1)} %param.25) | copy-start | bytes 147460
  36.4 22.1 %copy-start.2 = (f32[16,128]{1,0:T(8,128)S(1)}, f32[16,128]{1,0:T(8,128)}, u32[]{:S(2)}) copy-start(f32[16,128]{1,0:T(8,128)} %constant.38.clone.leaf_sin) | copy-start | bytes 24580
  36.4 22.1 %copy-start.3 = (f32[16,128]{1,0:T(8,128)S(1)}, f32[16,128]{1,0:T(8,128)}, u32[]{:S(2)}) copy-start(f32[16,128]{1,0:T(8,128)} %constant.37.clone.leaf_cos) | copy-start | bytes 24580
  36.4 22.1 %copy-start.4 = (s32[1,1,128]{2,1,0:T(1,128)S(1)}, s32[1,1,128]{2,1,0:T(1,128)}, u32[]{:S(2)}) copy-start(s32[1,1,128]{2,1,0:T(1,128)} %param.20) | copy-start | bytes 1540
  43.2 39.2 %copy-start = (f32[2,96,1,1,128]{4,3,2,1,0:T(1,128)S(1)}, f32[2,96,1,1,128]{4,3,2,1,0:T(1,128)}, u32[]{:S(2)}) copy-start(f32[2,96,1,1,128]{4,3,2,1,0:T(1,128)} %param.17) | copy-start | bytes 294916
  43.9 14.6 %all-to-all-start.1 = ((f32[16,2,128]{2,1,0:T(2,128)}), f32[16,2,128]{2,1,0:T(2,128)S(1)}, u32[]{:S(2)}, u32[]{:S(2)}) async-start(f32[16,2,128]{2,1,0:T(2,128)} %shard_map.178), calls=%async_computation.1 | async-start | bytes 32768 | tf_op jit(solution)/shard_map/all_to_all | solution.py:506
  60.0 4.6 %collective-permute-start.4 = (bf16[1,224,128]{2,1,0:T(8,128)(2,1)S(1)}, bf16[1,224,128]{2,1,0:T(8,128)(2,1)S(1)}, u32[]{:S(2)}, u32[]{:S(2)}) collective-permute-start(bf16[1,224,128]{2,1,0:T(8,128)(2,1)S(1)} %get-tuple-element.48), channel_id=1, source_target_pairs={{32,64},{96,128},{160,192},{224,256},{288,320},{352,384},{416,448}... | collective-permute-start | bytes 172040 | tf_op jit(solution)/shard_map/ppermute | solution.py:502
  60.6 5.5 %collective-permute-start.5 = (bf16[1,224,128]{2,1,0:T(8,128)(2,1)S(1)}, bf16[1,224,128]{2,1,0:T(8,128)(2,1)S(1)}, u32[]{:S(2)}, u32[]{:S(2)}) collective-permute-start(bf16[1,224,128]{2,1,0:T(8,128)(2,1)S(1)} %get-tuple-element.48), channel_id=1, source_target_pairs={{0,32},{64,96},{128,160},{192,224},{256,288},{320,352},{384,416},{... | collective-permute-start | bytes 172040 | tf_op jit(solution)/shard_map/ppermute | solution.py:502
  66.1 32.1 %collective-permute-start.7 = (bf16[3,224,128]{2,1,0:T(8,128)(2,1)S(1)}, bf16[3,224,128]{2,1,0:T(8,128)(2,1)S(1)}, u32[]{:S(2)}, u32[]{:S(2)}) collective-permute-start(bf16[3,224,128]{2,1,0:T(8,128)(2,1)S(1)} %constant_dynamic-update-slice_fusion.3.own), channel_id=1, source_target_pairs={{0,1},{2,3},{4,5},{6,7},{8,9},{10,11},{12,13},{14,15},{16,17},{18,... | collective-permute-start | bytes 516104 | tf_op jit(solution)/shard_map/ppermute | solution.py:502
  69.6 28.7 %collective-permute-start.6 = (bf16[3,224,128]{2,1,0:T(8,128)(2,1)S(1)}, bf16[3,224,128]{2,1,0:T(8,128)(2,1)S(1)}, u32[]{:S(2)}, u32[]{:S(2)}) collective-permute-start(bf16[3,224,128]{2,1,0:T(8,128)(2,1)S(1)} %constant_dynamic-update-slice_fusion.3.own), channel_id=1, source_target_pairs={{1,2},{3,4},{5,6},{7,8},{9,10},{11,12},{13,14},{15,16},{17,18},{19... | collective-permute-start | bytes 516104 | tf_op jit(solution)/shard_map/ppermute | solution.py:502
  72.5 18.7 %all-to-all-start.2 = ((f32[32,2,128]{2,1,0:T(2,128)}), f32[32,2,128]{2,1,0:T(2,128)S(1)}, u32[]{:S(2)}, u32[]{:S(2)}) async-start(f32[32,2,128]{2,1,0:T(2,128)} %get-tuple-element.47), calls=%async_computation.2 | async-start | bytes 65536 | tf_op jit(solution)/shard_map/all_to_all | solution.py:506
  91.9 13.6 %all-to-all-start.3 = ((f32[16,2,128]{2,1,0:T(2,128)}), f32[16,2,128]{2,1,0:T(2,128)S(1)}, u32[]{:S(2)}, u32[]{:S(2)}) async-start(f32[16,2,128]{2,1,0:T(2,128)} %shard_map.181), calls=%async_computation.3 | async-start | bytes 32768 | tf_op jit(solution)/shard_map/all_to_all | solution.py:506
